TPU v7x, 64 devices: a 2x2x8 block of a 4x4x8 slice. The times are simulated.
64 devices in a mesh: dp: 4 (over x, y), cp: 16 (over z, core).
Axes of the slice: x: 2, y: 2, z: 8, core: 2. Of those that a mesh axis runs over, the one named last changes fastest.
The devices are a block of a 4x4x8 slice.
Arguments:
- x_in: bfloat16 [24, 2048, 2304], P('dp', 'cp'), parts along dimension 0
- ln_w: bfloat16 [2, 4, 2304], replicated
- qk_w: bfloat16 [2, 2, 256], replicated
- w_q: bfloat16 [2, 2304, 2048], replicated
- w_k: bfloat16 [2, 2304, 1024], replicated
- w_v: bfloat16 [2, 2304, 1024], replicated
- w_o: bfloat16 [2, 2048, 2304], replicated
- w_gate: bfloat16 [2, 2304, 9216], replicated
- w_up: bfloat16 [2, 2304, 9216], replicated
- w_down: bfloat16 [2, 9216, 2304], replicated
Outputs:
- output: bfloat16 [24, 2048, 2304], P('dp', 'cp'), parts along dimension 0
There are 4 independent parts. A program takes and returns all parts, laid end to end along the dimension named above; an argument that names none is the same for every part.
All inputs are finite; a program needn't handle non-finite values.
Results may differ from a plain program's by a relative error of at most 0.02.
Values are sent between devices in bfloat16 or wider.
A program may use at most 768 MiB of HBM per device.

v0:
```python
import jax
import jax.numpy as jnp
from jax import lax
from jax.sharding import PartitionSpec as P

WINDOW = 1024
NORM_EPS = 1e-6
LOCAL_BASE = 10000.0
GLOBAL_BASE = 1000000.0
GLOBAL_SCALE = 8.0


def rms_scale(values_in, gain):
    vals_f32 = values_in.astype(jnp.float32)
    inv_rms = lax.rsqrt(jnp.mean(vals_f32 * vals_f32, axis=-1, keepdims=True) + NORM_EPS)
    return vals_f32 * inv_rms * (1.0 + gain.astype(jnp.float32))


def rope_apply(head_vals, positions, rope_base, pos_scale):
    head_dim = head_vals.shape[-1]
    half_dim = head_dim // 2
    inv_freq = rope_base ** (-2.0 * jnp.arange(half_dim, dtype=jnp.float32) / head_dim)
    ang_all = (positions.astype(jnp.float32) / pos_scale)[:, None] * inv_freq[None, :]
    cos_ang = jnp.cos(ang_all)[:, None, :]
    sin_ang = jnp.sin(ang_all)[:, None, :]
    first_half = head_vals[..., :half_dim]
    second_half = head_vals[..., half_dim:]
    return jnp.concatenate([first_half * cos_ang - second_half * sin_ang, second_half * cos_ang + first_half * sin_ang], axis=-1)


def attend(q_ready, k_all, v_all, q_pos, k_pos, window):
    score_scale = q_ready.shape[-1] ** -0.5
    scores = jnp.einsum("btgrd,bugd->bgrtu", q_ready, k_all, preferred_element_type=jnp.float32) * score_scale
    pos_diff = q_pos[:, None] - k_pos[None, :]
    keep_mask = (pos_diff >= 0) & (k_pos >= 0)[None, :]
    if window is not None:
        keep_mask = keep_mask & (pos_diff < window)
    attn_probs = jax.nn.softmax(jnp.where(keep_mask, scores, -1e30), axis=-1).astype(jnp.bfloat16)
    return jnp.einsum("bgrtu,bugd->btgrd", attn_probs, v_all, preferred_element_type=jnp.float32).astype(jnp.bfloat16)


def run_layer(x_loc, q_pos, weights, layer_idx, rope_base, pos_scale, collect_kv, window):
    ln_w, qk_w, w_q, w_k, w_v, w_o, w_gate, w_up, w_down = weights
    n_batch, tok_len = x_loc.shape[:2]
    head_dim = qk_w.shape[-1]
    kv_heads = w_k.shape[-1] // head_dim
    n_heads = w_q.shape[-1] // head_dim
    a_loc = rms_scale(x_loc, ln_w[layer_idx, 0]).astype(jnp.bfloat16)
    q_raw = jnp.einsum("btd,df->btf", a_loc, w_q[layer_idx], preferred_element_type=jnp.float32).astype(jnp.bfloat16)
    k_raw = jnp.einsum("btd,df->btf", a_loc, w_k[layer_idx], preferred_element_type=jnp.float32).astype(jnp.bfloat16)
    v_raw = jnp.einsum("btd,df->btf", a_loc, w_v[layer_idx], preferred_element_type=jnp.float32).astype(jnp.bfloat16)
    q_ready = rope_apply(rms_scale(q_raw.reshape(n_batch, tok_len, n_heads, head_dim), qk_w[layer_idx, 0]), q_pos, rope_base, pos_scale).astype(jnp.bfloat16)
    q_ready = q_ready.reshape(n_batch, tok_len, kv_heads, n_heads // kv_heads, head_dim)
    k_ready = rope_apply(rms_scale(k_raw.reshape(n_batch, tok_len, kv_heads, head_dim), qk_w[layer_idx, 1]), q_pos, rope_base, pos_scale).astype(jnp.bfloat16)
    v_loc = v_raw.reshape(n_batch, tok_len, kv_heads, head_dim)
    k_all, v_all, k_pos = collect_kv(k_ready, v_loc)
    attn_o = attend(q_ready, k_all, v_all, q_pos, k_pos, window).reshape(n_batch, tok_len, n_heads * head_dim)
    attn_out = jnp.einsum("btf,fd->btd", attn_o, w_o[layer_idx], preferred_element_type=jnp.float32).astype(jnp.bfloat16)
    x_mid = (x_loc.astype(jnp.float32) + rms_scale(attn_out, ln_w[layer_idx, 1])).astype(jnp.bfloat16)
    ffn_in = rms_scale(x_mid, ln_w[layer_idx, 2]).astype(jnp.bfloat16)
    gate_val = jnp.einsum("btd,df->btf", ffn_in, w_gate[layer_idx], preferred_element_type=jnp.float32)
    up_val = jnp.einsum("btd,df->btf", ffn_in, w_up[layer_idx], preferred_element_type=jnp.float32)
    act_val = (jax.nn.gelu(gate_val, approximate=True) * up_val).astype(jnp.bfloat16)
    mlp_out = jnp.einsum("btf,fd->btd", act_val, w_down[layer_idx], preferred_element_type=jnp.float32).astype(jnp.bfloat16)
    return (x_mid.astype(jnp.float32) + rms_scale(mlp_out, ln_w[layer_idx, 3])).astype(jnp.bfloat16)


def solution(mesh):
    group_size = mesh.shape["cp"]

    def device_fn(x_loc, ln_w, qk_w, w_q, w_k, w_v, w_o, w_gate, w_up, w_down):
        weights = (ln_w, qk_w, w_q, w_k, w_v, w_o, w_gate, w_up, w_down)
        tok_len = x_loc.shape[1]
        dev_idx = lax.axis_index("cp")
        q_pos = dev_idx * tok_len + jnp.arange(tok_len)

        def earlier_tokens(k_ready, v_loc):
            need_len = WINDOW - 1
            n_hops = min(group_size - 1, -(-need_len // tok_len))
            k_parts = []
            v_parts = []
            pos_parts = []
            for hop_dist in range(n_hops, 0, -1):
                take_len = min(tok_len, need_len - (hop_dist - 1) * tok_len)
                perm_pairs = [(src_dev, src_dev + hop_dist) for src_dev in range(group_size - hop_dist)]
                k_parts.append(lax.ppermute(k_ready[:, tok_len - take_len:], "cp", perm_pairs))
                v_parts.append(lax.ppermute(v_loc[:, tok_len - take_len:], "cp", perm_pairs))
                pos_parts.append((dev_idx - hop_dist) * tok_len + (tok_len - take_len) + jnp.arange(take_len))
            k_parts.append(k_ready)
            v_parts.append(v_loc)
            pos_parts.append(q_pos)
            return jnp.concatenate(k_parts, axis=1), jnp.concatenate(v_parts, axis=1), jnp.concatenate(pos_parts)

        def whole_sequence(k_ready, v_loc):
            k_all = lax.all_gather(k_ready, "cp", axis=1, tiled=True)
            v_all = lax.all_gather(v_loc, "cp", axis=1, tiled=True)
            return k_all, v_all, jnp.arange(group_size * tok_len)

        x_mid = run_layer(x_loc, q_pos, weights, 0, LOCAL_BASE, 1.0, earlier_tokens, WINDOW)
        return run_layer(x_mid, q_pos, weights, 1, GLOBAL_BASE, GLOBAL_SCALE, whole_sequence, None)

    act_part = P("dp", "cp", None)
    return jax.shard_map(device_fn, mesh=mesh, in_specs=(act_part,) + (P(),) * 9, out_specs=act_part, check_vma=False)
```

profile of v0, /device:TPU:21, one launch (start us, length us, event | category | flops | bytes accessed | tf_op | source)
XLA Modules:
  0.0 1730.1 jit_solution(2940989103702973087)
XLA Ops:
  30.4 12.2 collective-permute-start.9
  57.7 7.4 fusion.176
  75.8 10.1 fusion.147
  89.0 123.3 %collective-permute-done.8 = bf16[6,127,4,256]{3,2,1,0:T(4,128)(2,1)} collective-permute-done((bf16[6,127,4,256]{3,2,1,0:T(4,128)(2,1)}, bf16[6,127,4,256]{3,2,1,0:T(4,128)(2,1)}, u32[]{:S(2)}, u32[]{:S(2)}) %collective-permute-start.8) | collective-permute-done | bytes 1560608 | tf_op jit(solution)/shard_map/ppermute | solution.py:86
  212.3 8.9 collective-permute-start
  235.1 23.7 %collective-permute-done = bf16[6,127,4,256]{3,2,1,0:T(4,128)(2,1)} collective-permute-done((bf16[6,127,4,256]{3,2,1,0:T(4,128)(2,1)}, bf16[6,127,4,256]{3,2,1,0:T(4,128)(2,1)}, u32[]{:S(2)}, u32[]{:S(2)}) %collective-permute-start) | collective-permute-done | bytes 1560608 | tf_op jit(solution)/shard_map/ppermute | solution.py:87
  258.8 294.8 %collective-permute-start.13 = (bf16[6,128,4,256]{3,1,2,0:T(8,128)(2,1)}, bf16[6,128,4,256]{3,1,2,0:T(8,128)(2,1)}, u32[]{:S(2)}, u32[]{:S(2)}) collective-permute-start(bf16[6,128,4,256]{3,1,2,0:T(8,128)(2,1)} %pad_maximum_fusion), channel_id=1, source_target_pairs={{0,3},{1,4},{2,5},{3,6},{4,7},{5,8},{6,9},{7,10},{8,11},{9,12},{10... | collective-permute-start | bytes 4718600 | tf_op jit(solution)/shard_map/ppermute | solution.py:86
  558.5 8.0 collective-permute-start.1
  588.3 29.6 %collective-permute-done.14 = bf16[6,128,4,256]{3,1,2,0:T(8,128)(2,1)} collective-permute-done((bf16[6,128,4,256]{3,1,2,0:T(8,128)(2,1)}, bf16[6,128,4,256]{3,1,2,0:T(8,128)(2,1)}, u32[]{:S(2)}, u32[]{:S(2)}) %collective-permute-start.14) | collective-permute-done | bytes 1572896 | tf_op jit(solution)/shard_map/ppermute | solution.py:86
  617.9 27.3 %collective-permute-start.4 = (bf16[6,128,4,256]{1,3,2,0:T(8,128)(2,1)}, bf16[6,128,4,256]{1,3,2,0:T(8,128)(2,1)}, u32[]{:S(2)}, u32[]{:S(2)}) collective-permute-start(bf16[6,128,4,256]{1,3,2,0:T(8,128)(2,1)} %copy.81), channel_id=1, source_target_pairs={{0,4},{1,5},{2,6},{3,7},{4,8},{5,9},{6,10},{7,11},{8,12},{9,13},{1... | collective-permute-start | bytes 4718600 | tf_op jit(solution)/shard_map/ppermute | solution.py:87
  651.6 109.4 %collective-permute-start.5 = (bf16[6,128,4,256]{1,3,2,0:T(8,128)(2,1)}, bf16[6,128,4,256]{1,3,2,0:T(8,128)(2,1)}, u32[]{:S(2)}, u32[]{:S(2)}) collective-permute-start(bf16[6,128,4,256]{1,3,2,0:T(8,128)(2,1)} %copy.81), channel_id=1, source_target_pairs={{0,3},{1,4},{2,5},{3,6},{4,7},{5,8},{6,9},{7,10},{8,11},{9,12},{10... | collective-permute-start | bytes 4718600 | tf_op jit(solution)/shard_map/ppermute | solution.py:87
  761.0 85.9 %concatenate.42 = bf16[6,1151,4,256]{3,1,2,0:T(8,128)(2,1)} concatenate(bf16[6,127,4,256]{3,1,2,0:T(8,128)(2,1)} %copy.93, bf16[6,128,4,256]{3,1,2,0:T(8,128)(2,1)} %collective-permute-done.9, bf16[6,128,4,256]{3,1,2,0:T(8,128)(2,1)} %collective-permute-done.10, bf16[6,128,4,256]{3,1,2,0:T(8,128)(2,1)} %collective-permute-done.11, ...), dimensions={1} | concatenate | bytes 28286976 | tf_op jit(solution)/shard_map/concatenate | solution.py:92
  849.3 8.1 collective-permute-start.7
  857.5 19.9 %fusion.243 = (f32[6,4,2,128]{3,2,1,0:T(2,128)}, f32[6,4,2,128,1151]{3,4,2,1,0:T(8,128)}) fusion(pred[128,1151]{0,1:T(8,128)(4,1)} %fusion.208, bf16[6,128,4,2,128]{4,1,3,2,0:T(8,128)(2,1)} %bitcast.236, bf16[6,128,4,2,128]{4,1,3,2,0:T(8,128)(2,1)} %bitcast.237, bf16[6,1151,4,256]{3,1,2,0:T(8,128)(2,1)} %concatenate.42), kind=kOutput, calls=%fused_computation.250 | convolution fusion | flops 3655312384 | bytes 45748096 | tf_op jit(solution)/shard_map/sub | solution.py:38
  882.1 17.2 collective-permute-done.7
  899.2 22.4 %concatenate.39 = bf16[6,1151,4,256]{1,3,2,0:T(8,128)(2,1)} concatenate(bf16[6,127,4,256]{1,3,2,0:T(8,128)(2,1)} %copy.88, bf16[6,128,4,256]{1,3,2,0:T(8,128)(2,1)} %collective-permute-done.1, bf16[6,128,4,256]{1,3,2,0:T(8,128)(2,1)} %collective-permute-done.2, bf16[6,128,4,256]{1,3,2,0:T(8,128)(2,1)} %collective-permute-done.3, bf16[6,128,4,256]{1,3,2,0:T(8,128)(2,1)} %collective-permute-done.4, ...), dimensions={1} | concatenate | bytes 28286976 | tf_op jit(solution)/shard_map/concatenate | solution.py:92
  921.7 17.1 fusion.164
  938.7 12.1 fusion.82
  953.0 39.5 %fusion.12 = f32[6,128,9216]{2,1,0:T(8,128)} fusion(bf16[2,2304,9216]{2,1,0:T(8,128)(2,1)} %param.17, bf16[6,128,2304]{2,1,0:T(8,128)(2,1)S(1)} %get-tuple-element.18, f32[2304]{0:T(1024)S(1)} %copy-done.18, f32[6,128]{1,0:T(8,128)S(1)} %add_rsqrt_fusion.9), kind=kOutput, calls=%fused_computation.15 | convolution fusion | flops 32621985792 | bytes 74330112 | tf_op jit(solution)/shard_map/btd,df->btf/dot_general | solution.py:61
  992.5 43.6 %fusion.29.clone.3.clone.5 = bf16[6,128,9216]{2,1,0:T(8,128)(2,1)} fusion(f32[6,128,9216]{2,1,0:T(8,128)} %fusion.12, bf16[2,2304,9216]{2,1,0:T(8,128)(2,1)} %param.18, bf16[6,128,2304]{2,1,0:T(8,128)(2,1)S(1)} %get-tuple-element.18, f32[2304]{0:T(1024)S(1)} %copy-done.18, f32[6,128]{1,0:T(8,128)S(1)} %add_rsqrt_fusion.9), kind=kOutput, calls=%fused_computation.34.clone.clone.clone.clone.clone.clone.clone.2 | convolution fusion | flops 32692764672 | bytes 88485888 | tf_op jit(solution)/shard_map/btd,df->btf/dot_general | solution.py:62
  1036.1 38.5 %fusion.84 = (f32[6,128]{1,0:T(8,128)S(1)}, bf16[6,128,2304]{2,1,0:T(8,128)(2,1)S(1)}) fusion(bf16[2,9216,2304]{2,1,0:T(8,128)(2,1)} %param.19, bf16[6,128,9216]{2,1,0:T(8,128)(2,1)} %fusion.29.clone.3.clone.5), kind=kOutput, calls=%fused_computation.104 | convolution fusion | flops 32621985792 | bytes 60165120 | tf_op jit(solution)/shard_map/btf,fd->btd/dot_general | solution.py:64
  1098.2 7.8 fusion.191
  1109.6 10.1 fusion.144
  1139.5 278.8 %all-gather.5.cloned.1.call-done = bf16[6,2048,4,256]{3,1,2,0:T(8,128)(2,1)} async-done(((bf16[6,128,4,256]{3,1,2,0:T(8,128)(2,1)}), bf16[6,2048,4,256]{3,1,2,0:T(8,128)(2,1)}) %all-gather.5.cloned.1.call-update) | async-done | bytes 25165840 | tf_op jit(solution)/shard_map/all_gather | solution.py:95
  1418.4 25.8 %fusion.39 = f32[6,4,2048,128,2]{3,2,4,1,0:T(8,128)} fusion(bf16[6,2048,4,256]{3,1,2,0:T(8,128)(2,1)} %all-gather.5.cloned.1.call-done, bf16[6,128,4,2,128]{4,1,3,2,0:T(8,128)(2,1)} %bitcast.234, bf16[6,128,4,2,128]{4,1,3,2,0:T(8,128)(2,1)} %bitcast.235), kind=kOutput, calls=%fused_computation.47 | convolution fusion | flops 6448742400 | bytes 78643200 | tf_op jit(solution)/shard_map/btgrd,bugd->bgrtu/dot_general | solution.py:33
  1444.2 54.0 %fusion.252 = (f32[6,4,2,128]{3,2,1,0:T(2,128)}, f32[6,4,2,128,2048]{3,4,2,1,0:T(8,128)}) fusion(f32[6,4,2048,128,2]{3,2,4,1,0:T(8,128)} %fusion.39, pred[128,2048]{0,1:T(8,128)(4,1)} %subtract_compare_fusion), kind=kOutput, calls=%fused_computation.251 | output fusion | flops 75499520 | bytes 100950016 | tf_op jit(solution)/shard_map/sub | solution.py:38
  1498.1 58.3 %all-gather.3.cloned.1.call-done = bf16[6,2048,4,256]{1,3,2,0:T(8,128)(2,1)} async-done(((bf16[6,128,4,256]{1,3,2,0:T(8,128)(2,1)}), bf16[6,2048,4,256]{1,3,2,0:T(8,128)(2,1)}) %all-gather.3.cloned.1.call-update) | async-done | bytes 25165840 | tf_op jit(solution)/shard_map/all_gather | solution.py:96
  1556.4 26.8 %fusion.167 = bf16[6,4,256,2,128]{4,2,3,1,0:T(8,128)(2,1)} fusion(f32[6,4,2,128,2048]{3,4,2,1,0:T(8,128)} %get-tuple-element.42, f32[6,4,2,128]{3,2,1,0:T(2,128)} %get-tuple-element.41, bf16[6,2048,4,256]{1,3,2,0:T(8,128)(2,1)} %all-gather.3.cloned.1.call-done), kind=kOutput, calls=%fused_computation.171 | convolution fusion | flops 6469189632 | bytes 78667776 | tf_op jit(solution)/shard_map/bgrtu,bugd->btgrd/dot_general | solution.py:39
  1583.2 12.3 fusion.86
  1597.7 39.4 %fusion.6 = f32[6,128,9216]{2,1,0:T(8,128)} fusion(bf16[2,2304,9216]{2,1,0:T(8,128)(2,1)} %param.17, bf16[6,128,2304]{2,1,0:T(8,128)(2,1)S(1)} %get-tuple-element.14, f32[2304]{0:T(1024)S(1)} %copy-done.15, f32[6,128]{1,0:T(8,128)S(1)} %add_rsqrt_fusion.5), kind=kOutput, calls=%fused_computation.9 | convolution fusion | flops 32621985792 | bytes 74330112 | tf_op jit(solution)/shard_map/btd,df->btf/dot_general | solution.py:61
  1637.1 43.8 %fusion.38.clone.3.clone.5 = bf16[6,128,9216]{2,1,0:T(8,128)(2,1)} fusion(f32[6,128,9216]{2,1,0:T(8,128)} %fusion.6, bf16[2,2304,9216]{2,1,0:T(8,128)(2,1)} %param.18, bf16[6,128,2304]{2,1,0:T(8,128)(2,1)S(1)} %get-tuple-element.14, f32[2304]{0:T(1024)S(1)} %copy-done.15, f32[6,128]{1,0:T(8,128)S(1)} %add_rsqrt_fusion.5), kind=kOutput, calls=%fused_computation.43.clone.clone.clone.clone.clone.clone.clone.2 | convolution fusion | flops 32692764672 | bytes 88485888 | tf_op jit(solution)/shard_map/btd,df->btf/dot_general | solution.py:62
  1680.9 38.3 %fusion.88 = (f32[6,128]{1,0:T(8,128)S(1)}, bf16[6,128,2304]{2,1,0:T(8,128)(2,1)S(1)}) fusion(bf16[2,9216,2304]{2,1,0:T(8,128)(2,1)} %param.19, bf16[6,128,9216]{2,1,0:T(8,128)(2,1)} %fusion.38.clone.3.clone.5), kind=kOutput, calls=%fused_computation.108 | convolution fusion | flops 32621985792 | bytes 60165120 | tf_op jit(solution)/shard_map/btf,fd->btd/dot_general | solution.py:64
  (155 shorter events, 161.1 us)
Async XLA Ops:
  6.5 1411.8 %all-gather.5.cloned.1.call-start = ((), (), s32[]{:S(2)}) async-start(), calls=%async_computation.1 | async-start | bytes 26738688 | tf_op jit(solution)/shard_map/all_gather | solution.py:95
  8.9 11.5 copy-start.19
  13.0 7.4 copy-start.25
  28.5 29.1 %copy-start.2 = (bf16[6,128,2304]{2,1,0:T(8,128)(2,1)S(1)}, bf16[6,128,2304]{2,1,0:T(8,128)(2,1)}, u32[]{:S(2)}) copy-start(bf16[6,128,2304]{2,1,0:T(8,128)(2,1)} %param.10) | copy-start | bytes 10616836
  28.5 29.1 %copy-start.20 = (f32[2304]{0:T(1024)S(1)}, f32[2304]{0:T(1024)}, u32[]{:S(2)}) copy-start(f32[2304]{0:T(1024)} %copy-done.19) | copy-start | bytes 27652
  28.5 29.1 %copy-start.26 = (f32[6,128]{1,0:T(8,128)S(1)}, f32[6,128]{1,0:T(8,128)}, u32[]{:S(2)}) copy-start(f32[6,128]{1,0:T(8,128)} %copy-done.25) | copy-start | bytes 9220
  30.4 523.3 %collective-permute-start.9 = (bf16[6,128,4,256]{3,1,2,0:T(8,128)(2,1)}, bf16[6,128,4,256]{3,1,2,0:T(8,128)(2,1)}, u32[]{:S(2)}, u32[]{:S(2)}) collective-permute-start(bf16[6,128,4,256]{3,1,2,0:T(8,128)(2,1)} %pad_maximum_fusion), channel_id=1, source_target_pairs={{0,7},{1,8},{2,9},{3,10},{4,11},{5,12},{6,13},{7,14},{8,15},{16,23... | collective-permute-start | bytes 4718600 | tf_op jit(solution)/shard_map/ppermute | solution.py:86
  42.5 513.6 %collective-permute-start.10 = (bf16[6,128,4,256]{3,1,2,0:T(8,128)(2,1)}, bf16[6,128,4,256]{3,1,2,0:T(8,128)(2,1)}, u32[]{:S(2)}, u32[]{:S(2)}) collective-permute-start(bf16[6,128,4,256]{3,1,2,0:T(8,128)(2,1)} %pad_maximum_fusion), channel_id=1, source_target_pairs={{0,6},{1,7},{2,8},{3,9},{4,10},{5,11},{6,12},{7,13},{8,14},{9,15},... | collective-permute-start | bytes 4718600 | tf_op jit(solution)/shard_map/ppermute | solution.py:86
  46.7 511.8 %collective-permute-start.11 = (bf16[6,128,4,256]{3,1,2,0:T(8,128)(2,1)}, bf16[6,128,4,256]{3,1,2,0:T(8,128)(2,1)}, u32[]{:S(2)}, u32[]{:S(2)}) collective-permute-start(bf16[6,128,4,256]{3,1,2,0:T(8,128)(2,1)} %pad_maximum_fusion), channel_id=1, source_target_pairs={{0,5},{1,6},{2,7},{3,8},{4,9},{5,10},{6,11},{7,12},{8,13},{9,14},{... | collective-permute-start | bytes 4718600 | tf_op jit(solution)/shard_map/ppermute | solution.py:86
  49.1 517.4 %collective-permute-start.12 = (bf16[6,128,4,256]{3,1,2,0:T(8,128)(2,1)}, bf16[6,128,4,256]{3,1,2,0:T(8,128)(2,1)}, u32[]{:S(2)}, u32[]{:S(2)}) collective-permute-start(bf16[6,128,4,256]{3,1,2,0:T(8,128)(2,1)} %pad_maximum_fusion), channel_id=1, source_target_pairs={{0,4},{1,5},{2,6},{3,7},{4,8},{5,9},{6,10},{7,11},{8,12},{9,13},{1... | collective-permute-start | bytes 4718600 | tf_op jit(solution)/shard_map/ppermute | solution.py:86
  55.0 157.3 %collective-permute-start.8 = (bf16[6,127,4,256]{3,2,1,0:T(4,128)(2,1)}, bf16[6,127,4,256]{3,2,1,0:T(4,128)(2,1)}, u32[]{:S(2)}, u32[]{:S(2)}) collective-permute-start(bf16[6,127,4,256]{3,2,1,0:T(4,128)(2,1)} %copy.92), channel_id=1, source_target_pairs={{0,8},{1,9},{2,10},{3,11},{4,12},{5,13},{6,14},{7,15},{16,24},{17,... | collective-permute-start | bytes 4681736 | tf_op jit(solution)/shard_map/ppermute | solution.py:86
  89.0 132.2 %copy-start = (f32[96,8,8,256]{3,2,1,0:T(8,128)}, f32[96,8,8,256]{3,2,1,0:T(8,128)S(1)}, u32[]{:S(2)}) copy-start(f32[96,8,8,256]{3,2,1,0:T(8,128)S(1)} %copy.120) | copy-start | bytes 18874372
  212.3 46.5 %collective-permute-start = (bf16[6,127,4,256]{3,2,1,0:T(4,128)(2,1)}, bf16[6,127,4,256]{3,2,1,0:T(4,128)(2,1)}, u32[]{:S(2)}, u32[]{:S(2)}) collective-permute-start(bf16[6,127,4,256]{3,2,1,0:T(4,128)(2,1)} %slice.144), channel_id=1, source_target_pairs={{0,8},{1,9},{2,10},{3,11},{4,12},{5,13},{6,14},{7,15},{16,24},{17,... | collective-permute-start | bytes 4681736 | tf_op jit(solution)/shard_map/ppermute | solution.py:87
  235.1 611.8 %copy-start.21 = (s32[128]{0:T(128)}, s32[128]{0:T(128)S(1)}, u32[]{:S(2)}) copy-start(s32[128]{0:T(128)S(1)} %iota_add_fusion.8) | copy-start | bytes 1540
  258.8 325.4 %collective-permute-start.13 = (bf16[6,128,4,256]{3,1,2,0:T(8,128)(2,1)}, bf16[6,128,4,256]{3,1,2,0:T(8,128)(2,1)}, u32[]{:S(2)}, u32[]{:S(2)}) collective-permute-start(bf16[6,128,4,256]{3,1,2,0:T(8,128)(2,1)} %pad_maximum_fusion), channel_id=1, source_target_pairs={{0,3},{1,4},{2,5},{3,6},{4,7},{5,8},{6,9},{7,10},{8,11},{9,12},{10... | collective-permute-start | bytes 4718600 | tf_op jit(solution)/shard_map/ppermute | solution.py:86
  553.7 64.2 %collective-permute-start.14 = (bf16[6,128,4,256]{3,1,2,0:T(8,128)(2,1)}, bf16[6,128,4,256]{3,1,2,0:T(8,128)(2,1)}, u32[]{:S(2)}, u32[]{:S(2)}) collective-permute-start(bf16[6,128,4,256]{3,1,2,0:T(8,128)(2,1)} %pad_maximum_fusion), channel_id=1, source_target_pairs={{0,2},{1,3},{2,4},{3,5},{4,6},{5,7},{6,8},{7,9},{8,10},{9,11},{10,... | collective-permute-start | bytes 4718600 | tf_op jit(solution)/shard_map/ppermute | solution.py:86
  556.1 95.5 %collective-permute-start.15 = (bf16[6,128,4,256]{3,1,2,0:T(8,128)(2,1)}, bf16[6,128,4,256]{3,1,2,0:T(8,128)(2,1)}, u32[]{:S(2)}, u32[]{:S(2)}) collective-permute-start(bf16[6,128,4,256]{3,1,2,0:T(8,128)(2,1)} %pad_maximum_fusion), channel_id=1, source_target_pairs={{0,1},{1,2},{2,3},{3,4},{4,5},{5,6},{6,7},{7,8},{8,9},{9,10},{10,1... | collective-permute-start | bytes 4718600 | tf_op jit(solution)/shard_map/ppermute | solution.py:86
  558.5 288.4 %collective-permute-start.1 = (bf16[6,128,4,256]{1,3,2,0:T(8,128)(2,1)}, bf16[6,128,4,256]{1,3,2,0:T(8,128)(2,1)}, u32[]{:S(2)}, u32[]{:S(2)}) collective-permute-start(bf16[6,128,4,256]{1,3,2,0:T(8,128)(2,1)} %copy.81), channel_id=1, source_target_pairs={{0,7},{1,8},{2,9},{3,10},{4,11},{5,12},{6,13},{7,14},{8,15},{16,23... | collective-permute-start | bytes 4718600 | tf_op jit(solution)/shard_map/ppermute | solution.py:87
  566.5 282.9 %collective-permute-start.2 = (bf16[6,128,4,256]{1,3,2,0:T(8,128)(2,1)}, bf16[6,128,4,256]{1,3,2,0:T(8,128)(2,1)}, u32[]{:S(2)}, u32[]{:S(2)}) collective-permute-start(bf16[6,128,4,256]{1,3,2,0:T(8,128)(2,1)} %copy.81), channel_id=1, source_target_pairs={{0,6},{1,7},{2,8},{3,9},{4,10},{5,11},{6,12},{7,13},{8,14},{9,15},... | collective-permute-start | bytes 4718600 | tf_op jit(solution)/shard_map/ppermute | solution.py:87
  584.2 293.2 %collective-permute-start.3 = (bf16[6,128,4,256]{1,3,2,0:T(8,128)(2,1)}, bf16[6,128,4,256]{1,3,2,0:T(8,128)(2,1)}, u32[]{:S(2)}, u32[]{:S(2)}) collective-permute-start(bf16[6,128,4,256]{1,3,2,0:T(8,128)(2,1)} %copy.81), channel_id=1, source_target_pairs={{0,5},{1,6},{2,7},{3,8},{4,9},{5,10},{6,11},{7,12},{8,13},{9,14},{... | collective-permute-start | bytes 4718600 | tf_op jit(solution)/shard_map/ppermute | solution.py:87
  617.9 259.5 %collective-permute-start.4 = (bf16[6,128,4,256]{1,3,2,0:T(8,128)(2,1)}, bf16[6,128,4,256]{1,3,2,0:T(8,128)(2,1)}, u32[]{:S(2)}, u32[]{:S(2)}) collective-permute-start(bf16[6,128,4,256]{1,3,2,0:T(8,128)(2,1)} %copy.81), channel_id=1, source_target_pairs={{0,4},{1,5},{2,6},{3,7},{4,8},{5,9},{6,10},{7,11},{8,12},{9,13},{1... | collective-permute-start | bytes 4718600 | tf_op jit(solution)/shard_map/ppermute | solution.py:87
  651.6 225.8 %collective-permute-start.5 = (bf16[6,128,4,256]{1,3,2,0:T(8,128)(2,1)}, bf16[6,128,4,256]{1,3,2,0:T(8,128)(2,1)}, u32[]{:S(2)}, u32[]{:S(2)}) collective-permute-start(bf16[6,128,4,256]{1,3,2,0:T(8,128)(2,1)} %copy.81), channel_id=1, source_target_pairs={{0,3},{1,4},{2,5},{3,6},{4,7},{5,8},{6,9},{7,10},{8,11},{9,12},{10... | collective-permute-start | bytes 4718600 | tf_op jit(solution)/shard_map/ppermute | solution.py:87
  846.9 35.2 %collective-permute-start.6 = (bf16[6,128,4,256]{1,3,2,0:T(8,128)(2,1)}, bf16[6,128,4,256]{1,3,2,0:T(8,128)(2,1)}, u32[]{:S(2)}, u32[]{:S(2)}) collective-permute-start(bf16[6,128,4,256]{1,3,2,0:T(8,128)(2,1)} %copy.81), channel_id=1, source_target_pairs={{0,2},{1,3},{2,4},{3,5},{4,6},{5,7},{6,8},{7,9},{8,10},{9,11},{10,... | collective-permute-start | bytes 4718600 | tf_op jit(solution)/shard_map/ppermute | solution.py:87
  849.3 49.9 %collective-permute-start.7 = (bf16[6,128,4,256]{1,3,2,0:T(8,128)(2,1)}, bf16[6,128,4,256]{1,3,2,0:T(8,128)(2,1)}, u32[]{:S(2)}, u32[]{:S(2)}) collective-permute-start(bf16[6,128,4,256]{1,3,2,0:T(8,128)(2,1)} %copy.81), channel_id=1, source_target_pairs={{0,1},{1,2},{2,3},{3,4},{4,5},{5,6},{6,7},{7,8},{8,9},{9,10},{10,1... | collective-permute-start | bytes 4718600 | tf_op jit(solution)/shard_map/ppermute | solution.py:87
  938.7 12.2 copy-start.13
  1036.1 38.6 %copy-start.12 = (f32[2304]{0:T(1024)S(1)}, f32[2304]{0:T(1024)}, u32[]{:S(2)}) copy-start(f32[2304]{0:T(1024)} %get-tuple-element.8) | copy-start | bytes 27652
  1083.9 9.9 copy-start.24
  1098.1 10.6 copy-start.22
  1098.1 458.3 %all-gather.3.cloned.1.call-start = ((), (), s32[]{:S(2)}) async-start(), calls=%async_computation | async-start | bytes 26738688 | tf_op jit(solution)/shard_map/all_gather | solution.py:96
  1122.8 9.2 copy-start.23
  1583.2 12.4 copy-start.11
  1680.9 38.3 %copy-start.14 = (f32[2304]{0:T(1024)S(1)}, f32[2304]{0:T(1024)}, u32[]{:S(2)}) copy-start(f32[2304]{0:T(1024)} %get-tuple-element.5) | copy-start | bytes 27652
  (15 other events, 41.3 us)
Sparse Core Ops, SparseCore 0:
  1098.2 320.0 all-gather.4
  1419.9 136.4 all-gather.2
where the time goes:
time: 1740 us; the launch traced here: 1730 us
  waiting for transfers between devices  545 us (31%)
  starting transfers between devices  494 us (28%)
  matrix products  405 us (23%)
  local copies, waits for them, and re-layouts  164 us (9%)
  other arithmetic  107 us (6%)
    ppermute x8, starting transfers between devices, earlier_tokens(): lax.ppermute(k_ready[:, tok_len - take_len:], 'cp', perm_pairs)  324 us
    all_gather x1, waiting for transfers between devices, whole_sequence(): k_all = lax.all_gather(k_ready, 'cp', axis=1, tiled=True)  279 us
    ppermute x8, starting transfers between devices, earlier_tokens(): lax.ppermute(v_loc[:, tok_len - take_len:], 'cp', perm_pairs)  171 us
    ppermute x8, waiting for transfers between devices, earlier_tokens(): lax.ppermute(k_ready[:, tok_len - take_len:], 'cp', perm_pairs)  162 us
    dot_general x2, matrix products, run_layer(): jnp.einsum('btd,df->btf', ffn_in, w_up[layer_idx], preferred_element_type...  87.4 us
    concatenate x1, local copies, waits for them, and re-layouts, earlier_tokens(): jnp.concatenate(k_parts, axis=1)  85.9 us
    dot_general x2, matrix products, run_layer(): jnp.einsum('btd,df->btf', ffn_in, w_gate[layer_idx], preferred_element_ty...  78.9 us
    dot_general x2, matrix products, run_layer(): jnp.einsum('btf,fd->btd', act_val, w_down[layer_idx], preferred_element_t...  76.8 us
  transfers between devices with their start and end apart: 18, of which 9 were waited for; matrix products, arithmetic and copies ran while one was open for 16% of the time, Pallas kernels for 0%

commit v1 on v0

v1 whole, which is shorter than its diff:
```python
import functools

import jax
import jax.numpy as jnp
from jax import lax
from jax.experimental import pallas as pl
from jax.experimental.pallas import tpu as pltpu
from jax.sharding import PartitionSpec as P

WINDOW = 1024
NORM_EPS = 1e-6
LOCAL_BASE = 10000.0
GLOBAL_BASE = 1000000.0
GLOBAL_SCALE = 8.0
NEG = -1e30

ROW_CHIP = (0, 3, 4, 1, 5, 6)
SPECIAL = (2, 7)
VMEM_LIMIT = 64 * 1024 * 1024 - 128 * 1024


def pick(idx, table):
    out = jnp.int32(table[-1])
    for i in range(len(table) - 2, -1, -1):
        out = jnp.where(idx == i, jnp.int32(table[i]), out)
    return out


def placement():
    me = lax.axis_index("cp")
    chip, core = me // 2, me % 2
    roles = [0] * 8
    rows = [0] * 8
    for b, c in enumerate(ROW_CHIP):
        rows[c] = b
    for i, c in enumerate(SPECIAL):
        roles[c] = 1
        rows[c] = 3 * i
    return me, chip, core, pick(chip, roles), pick(chip, rows)


def slot_place(s, core, special, row):
    k = s % 2
    blk = jnp.where(special == 1, 2 * k + (k + core) % 2, 4 + 2 * s + (s + core) % 2)
    b = jnp.where(special == 1, row + s // 2, row)
    return b, blk


def home_of(b, blk):
    core = ((blk + 1) // 2) % 2
    half = blk // 2
    chip = jnp.where(blk < 4, SPECIAL[b // 3], ROW_CHIP[b])
    slot = jnp.where(blk < 4, (b % 3) * 2 + half, half - 2)
    return chip * 2 + core, slot


def group_barrier(n_dev):
    me = lax.axis_index("cp")
    barrier = pltpu.get_barrier_semaphore()
    for d in range(1, n_dev):
        dev = lax.rem(me + d, n_dev)
        pl.semaphore_signal(barrier, inc=1, device_id={"cp": dev}, device_id_type=pl.DeviceIdType.MESH)
    pl.semaphore_wait(barrier, n_dev - 1)


def remote(src, dst, send, recv, dev):
    return pltpu.make_async_remote_copy(
        src_ref=src, dst_ref=dst, send_sem=send, recv_sem=recv, device_id={"cp": dev},
        device_id_type=pl.DeviceIdType.MESH,
    )


def exchange_kernel(to_home, n_dev, x_ref, o_ref, buf, send, recv, sem):
    me, _, core, special, row = placement()
    n = x_ref.shape[0]
    homes = [home_of(b, me) for b in range(n)]
    places = [slot_place(s, core, special, row) for s in range(n)]
    places = [(blk, b) for b, blk in places]
    dest, origin = (homes, places) if to_home else (places, homes)
    for i, (dev, dst) in enumerate(dest):

        @pl.when(dev == me)
        def _():
            pltpu.make_async_copy(x_ref.at[i], buf.at[i], sem.at[i]).start()

    group_barrier(n_dev)
    for i, (dev, dst) in enumerate(dest):

        @pl.when(dev != me)
        def _():
            remote(x_ref.at[i], o_ref.at[dst], send.at[i], recv.at[dst], dev).start()

    for i, (dev, dst) in enumerate(dest):

        @pl.when(dev == me)
        def _():
            pltpu.make_async_copy(x_ref.at[i], buf.at[i], sem.at[i]).wait()
            pltpu.make_async_copy(buf.at[i], o_ref.at[dst], sem.at[i]).start()
            pltpu.make_async_copy(buf.at[i], o_ref.at[dst], sem.at[i]).wait()

    for i, (dev, _) in enumerate(origin):

        @pl.when(dev != me)
        def _():
            remote(x_ref.at[i], o_ref.at[i], send.at[i], recv.at[i], dev).wait_recv()

    for i, (dev, dst) in enumerate(dest):

        @pl.when(dev != me)
        def _():
            remote(x_ref.at[i], o_ref.at[dst], send.at[i], recv.at[dst], dev).wait_send()


def exchange(to_home, n_dev, x, cid):
    n = x.shape[0]
    dma = pltpu.SemaphoreType.DMA
    return pl.pallas_call(
        functools.partial(exchange_kernel, to_home, n_dev),
        out_shape=jax.ShapeDtypeStruct(x.shape, x.dtype),
        in_specs=[pl.BlockSpec(memory_space=pl.ANY)],
        out_specs=pl.BlockSpec(memory_space=pl.ANY),
        scratch_shapes=[pltpu.VMEM(x.shape, x.dtype), dma((n,)), dma((n,)), dma((n,))],
        compiler_params=pltpu.CompilerParams(collective_id=cid, has_side_effects=True),
    )(x)


def norm_rows(vals, gain):
    inv = lax.rsqrt(jnp.mean(vals * vals, axis=-1, keepdims=True) + NORM_EPS)
    return vals * inv * (1.0 + gain)


def qkv_kernel(layer, nq, nk, slots, x_ref, ln_ref, qk_ref, cos_ref, sin_ref, wq_ref, wk_ref, wv_ref, q_ref, k_ref, v_ref, a_ref):
    i = pl.program_id(0)
    rows = x_ref.shape[0] // slots
    hd = wq_ref.shape[-1]
    half = hd // 2

    @pl.when(i == 0)
    def _():
        gain = ln_ref[layer, 0:1, :].astype(jnp.float32)
        for s in range(slots):
            r = pl.ds(s * rows, rows)
            a_ref[r, :] = norm_rows(x_ref[r, :].astype(jnp.float32), gain).astype(jnp.bfloat16)

    def product(s, w_ref):
        return jnp.dot(a_ref[pl.ds(s * rows, rows), :], w_ref[0], preferred_element_type=jnp.float32).astype(jnp.bfloat16)

    def turned(s, w_ref, which):
        vals = norm_rows(product(s, w_ref).astype(jnp.float32), qk_ref[layer, which : which + 1, :].astype(jnp.float32))
        first, second = vals[:, :half], vals[:, half:]
        r = pl.ds(s * rows, rows)
        cos, sin = cos_ref[r, :], sin_ref[r, :]
        return jnp.concatenate([first * cos - second * sin, second * cos + first * sin], axis=-1).astype(jnp.bfloat16)

    @pl.when(i < nq)
    def _():
        for s in range(slots):
            q_ref[s, 0] = turned(s, wq_ref, 0) * jnp.bfloat16(hd**-0.5)

    @pl.when((i >= nq) & (i < nq + nk))
    def _():
        for s in range(slots):
            k_ref[s] = turned(s, wk_ref, 1)

    @pl.when(i >= nq + nk)
    def _():
        for s in range(slots):
            v_ref[s] = product(s, wv_ref)


def qkv(layer, x, ln_w, qk_w, cos, sin, w_q, w_k, w_v):
    slots, rows, dim = x.shape
    hd = qk_w.shape[-1]
    nq, nk = w_q.shape[-1] // hd, w_k.shape[-1] // hd
    x2 = x.reshape(slots * rows, dim)
    whole = lambda a: pl.BlockSpec(a.shape, lambda i: (0,) * a.ndim)
    at = lambda lo, n: (lambda i: jnp.clip(i - lo, 0, n - 1))
    iq, ik, iv = at(0, nq), at(nq, nk), at(nq + nk, nk)
    wspec = lambda f: pl.BlockSpec((1, dim, hd), lambda i: (layer, 0, f(i)))
    return pl.pallas_call(
        functools.partial(qkv_kernel, layer, nq, nk, slots),
        grid=(nq + 2 * nk,),
        in_specs=[whole(x2), whole(ln_w), whole(qk_w), whole(cos), whole(sin), wspec(iq), wspec(ik), wspec(iv)],
        out_specs=[
            pl.BlockSpec((slots, 1, rows, hd), lambda i: (0, iq(i), 0, 0)),
            pl.BlockSpec((slots, rows, hd), lambda i: (0, 0, ik(i))),
            pl.BlockSpec((slots, rows, hd), lambda i: (0, 0, iv(i))),
        ],
        out_shape=[
            jax.ShapeDtypeStruct((slots, nq, rows, hd), jnp.bfloat16),
            jax.ShapeDtypeStruct((slots, rows, nk * hd), jnp.bfloat16),
            jax.ShapeDtypeStruct((slots, rows, nk * hd), jnp.bfloat16),
        ],
        scratch_shapes=[pltpu.VMEM(x2.shape, jnp.bfloat16)],
        compiler_params=pltpu.CompilerParams(dimension_semantics=("arbitrary",), vmem_limit_bytes=VMEM_LIMIT),
    )(x2, ln_w, qk_w, cos, sin, w_q, w_k, w_v)


def attn_kernel(window_blocks, q_ref, k_ref, v_ref, o_ref, kbuf, vbuf, qbuf, obuf, acc, mx, sm, bias,
                qsem, ksem, vsem, ksend, vsend, fsend, krecv, vrecv, osem):
    me, chip, core, special, row = placement()
    mate = chip * 2 + (1 - core)
    slots, nq, rows, hd = q_ref.shape
    nk = k_ref.shape[-1] // hd
    rep = nq // nk
    tile = 2 * rows
    barrier = pltpu.get_barrier_semaphore()

    def tell(dev):
        pl.semaphore_signal(barrier, inc=1, device_id={"cp": dev}, device_id_type=pl.DeviceIdType.MESH)

    def buf_index(s, c):
        b, blk = slot_place(s, c, special, row)
        return jnp.where(special == 1, (s // 2) * 4 + blk, blk)

    serve_chip = [jnp.where(row == 0, ROW_CHIP[r], ROW_CHIP[r + 3]) for r in range(3)]
    my_special = jnp.where(row < 3, SPECIAL[0], SPECIAL[1]) * 2 + core

    for s in range(slots):
        idx = buf_index(s, core)
        pltpu.make_async_copy(k_ref.at[s], kbuf.at[idx], ksem.at[s]).start()
        pltpu.make_async_copy(v_ref.at[s], vbuf.at[idx], vsem.at[s]).start()
        pltpu.make_async_copy(q_ref.at[s], qbuf.at[s], qsem.at[s]).start()

    tell(mate)

    @pl.when(special == 1)
    def _():
        for r in range(3):
            tell(serve_chip[r] * 2 + core)
        pl.semaphore_wait(barrier, 4)

    @pl.when(special == 0)
    def _():
        tell(my_special)
        pl.semaphore_wait(barrier, 2)

    @pl.when(special == 1)
    def _():
        for k in range(2):
            for r in range(3):
                s = 2 * r + k
                blk = 2 * k + (k + core) % 2
                dev = serve_chip[r] * 2 + core
                remote(k_ref.at[s], kbuf.at[blk], ksend.at[1, s], krecv.at[blk], dev).start()
                remote(v_ref.at[s], vbuf.at[blk], vsend.at[1, s], vrecv.at[blk], dev).start()

    for s in range(slots):
        idx = buf_index(s, core)
        remote(k_ref.at[s], kbuf.at[idx], ksend.at[0, s], krecv.at[idx], mate).start()
        remote(v_ref.at[s], vbuf.at[idx], vsend.at[0, s], vrecv.at[idx], mate).start()

    qi = lax.broadcasted_iota(jnp.int32, (rows, tile), 0)
    ki = lax.broadcasted_iota(jnp.int32, (rows, tile), 1)
    bias[0] = jnp.zeros((rows, tile), jnp.float32)
    bias[1] = jnp.where(ki <= qi, 0.0, NEG)
    bias[2] = jnp.where(ki <= qi + rows, 0.0, NEG)
    bias[3] = jnp.where(ki > qi, 0.0, NEG)
    bias[4] = jnp.where(ki > qi + rows, 0.0, NEG)

    def one_tile(s, t, base, blk):
        last = blk // 2
        edge = jnp.where(t == last, 1 + blk % 2, 0)
        if window_blocks is not None:
            old = (blk - window_blocks) // 2
            edge = jnp.where((blk >= window_blocks) & (t == old), 3 + (blk - window_blocks) % 2, edge)
        off = bias[edge]
        off2 = jnp.concatenate([off] * rep, axis=0)
        kt = kbuf.at[pl.ds(base + 2 * t, 2)]
        vt = vbuf.at[pl.ds(base + 2 * t, 2)]
        for g in range(nk):
            u = s * nk + g
            q2 = qbuf[s, g * rep : (g + 1) * rep].reshape(rep * rows, hd)
            kk = kt[:, :, g * hd : (g + 1) * hd].reshape(tile, hd)
            vv = vt[:, :, g * hd : (g + 1) * hd].reshape(tile, hd)
            sc = lax.dot_general(q2, kk, (((1,), (1,)), ((), ())), preferred_element_type=jnp.float32) + off2
            m_old = mx[u][:, :1]
            m_new = jnp.maximum(m_old, jnp.max(sc, axis=-1, keepdims=True))
            p = jnp.exp(sc - m_new)
            alpha = jnp.exp(m_old - m_new)
            sm[u] = jnp.broadcast_to(alpha * sm[u][:, :1] + jnp.sum(p, axis=-1, keepdims=True), sm.shape[1:])
            mx[u] = jnp.broadcast_to(m_new, mx.shape[1:])
            acc[u] = alpha * acc[u] + jnp.dot(p.astype(jnp.bfloat16), vv, preferred_element_type=jnp.float32)

    def start_tile(blk):
        if window_blocks is None:
            return jnp.int32(0)
        return jnp.maximum(blk - window_blocks, 0) // 2

    mx[...] = jnp.full(mx.shape, NEG, jnp.float32)
    sm[...] = jnp.zeros(sm.shape, jnp.float32)
    acc[...] = jnp.zeros(acc.shape, jnp.float32)

    for s in range(slots):
        pltpu.make_async_copy(k_ref.at[s], kbuf.at[buf_index(s, core)], ksem.at[s]).wait()
        pltpu.make_async_copy(v_ref.at[s], vbuf.at[buf_index(s, core)], vsem.at[s]).wait()
        pltpu.make_async_copy(q_ref.at[s], qbuf.at[s], qsem.at[s]).wait()
    for s in range(slots):
        idx = buf_index(s, 1 - core)
        remote(k_ref.at[s], kbuf.at[idx], ksend.at[0, s], krecv.at[idx], mate).wait()
        remote(v_ref.at[s], vbuf.at[idx], vsend.at[0, s], vrecv.at[idx], mate).wait()

    @pl.loop(0, slots)
    def _(s):
        b, blk = slot_place(s, core, special, row)
        base = jnp.where(special == 1, (s // 2) * 4, 0)
        first = jnp.where(special == 1, 0, jnp.maximum(start_tile(blk), 2))

        @pl.loop(first, blk // 2 + 1)
        def _(t):
            one_tile(s, t, base, blk)

    @pl.when(special == 0)
    def _():
        mine = [2 * k + (k + core) % 2 for k in range(2)]
        theirs = [2 * k + (k + 1 - core) % 2 for k in range(2)]
        for k in range(2):
            blk = mine[k]
            remote(k_ref.at[k], kbuf.at[blk], fsend.at[0, k], krecv.at[blk], mate).wait_recv()
            remote(kbuf.at[blk], kbuf.at[blk], fsend.at[0, k], krecv.at[blk], mate).start()
            remote(v_ref.at[k], vbuf.at[blk], fsend.at[1, k], vrecv.at[blk], mate).wait_recv()
            remote(vbuf.at[blk], vbuf.at[blk], fsend.at[1, k], vrecv.at[blk], mate).start()
        for k in range(2):
            blk = theirs[k]
            remote(kbuf.at[blk], kbuf.at[blk], fsend.at[0, k], krecv.at[blk], mate).wait()
            remote(vbuf.at[blk], vbuf.at[blk], fsend.at[1, k], vrecv.at[blk], mate).wait()

        @pl.loop(0, slots)
        def _(s):
            _, blk = slot_place(s, core, special, row)

            @pl.loop(start_tile(blk), 2)
            def _(t):
                one_tile(s, t, 0, blk)

    @pl.when(special == 1)
    def _():
        for s in range(slots):
            remote(k_ref.at[s], kbuf.at[0], ksend.at[1, s], krecv.at[0], mate).wait_send()
            remote(v_ref.at[s], vbuf.at[0], vsend.at[1, s], vrecv.at[0], mate).wait_send()

    @pl.loop(0, slots)
    def _(s):
        for g in range(nk):
            u = s * nk + g
            out = (acc[u] / sm[u][:, :1]).astype(jnp.bfloat16)
            for h in range(rep):
                lo = (g * rep + h) * hd
                obuf[s, :, lo : lo + hd] = out[h * rows : (h + 1) * rows]

    copy = pltpu.make_async_copy(obuf, o_ref, osem)
    copy.start()
    copy.wait()


def attention(window, q, k, v, cid):
    slots, nq, rows, hd = q.shape
    nk = k.shape[-1] // hd
    blocks = 16
    units = slots * nk
    dma = pltpu.SemaphoreType.DMA
    any_spec = pl.BlockSpec(memory_space=pl.ANY)
    body = functools.partial(attn_kernel, None if window is None else window // rows)
    return pl.pallas_call(
        body,
        out_shape=jax.ShapeDtypeStruct((slots, rows, nq * hd), jnp.bfloat16),
        in_specs=[any_spec] * 3,
        out_specs=any_spec,
        scratch_shapes=[
            pltpu.VMEM((blocks, rows, nk * hd), jnp.bfloat16),
            pltpu.VMEM((blocks, rows, nk * hd), jnp.bfloat16),
            pltpu.VMEM(q.shape, jnp.bfloat16),
            pltpu.VMEM((slots, rows, nq * hd), jnp.bfloat16),
            pltpu.VMEM((units, nq // nk * rows, hd), jnp.float32),
            pltpu.VMEM((units, nq // nk * rows, 128), jnp.float32),
            pltpu.VMEM((units, nq // nk * rows, 128), jnp.float32),
            pltpu.VMEM((5, rows, 2 * rows), jnp.float32),
            dma((slots,)), dma((slots,)), dma((slots,)),
            dma((2, slots)), dma((2, slots)), dma((2, 2)),
            dma((blocks,)), dma((blocks,)), dma,
        ],
        compiler_params=pltpu.CompilerParams(collective_id=cid, has_side_effects=True, vmem_limit_bytes=VMEM_LIMIT),
    )(q, k, v)


def rope_tables(pos, hd):
    half = hd // 2
    out = []
    for base, scale in ((LOCAL_BASE, 1.0), (GLOBAL_BASE, GLOBAL_SCALE)):
        freq = base ** (-2.0 * jnp.arange(half, dtype=jnp.float32) / hd)
        ang = (pos.astype(jnp.float32) / scale)[:, None] * freq[None, :]
        out += [jnp.cos(ang), jnp.sin(ang)]
    return out


def solution(mesh):
    n_dev = mesh.shape["cp"]

    def device_fn(x_loc, ln_w, qk_w, w_q, w_k, w_v, w_o, w_gate, w_up, w_down):
        slots, rows, dim = x_loc.shape
        hd = qk_w.shape[-1]
        _, _, core, special, row = placement()
        blk = jnp.stack([slot_place(s, core, special, row)[1] for s in range(slots)])
        pos = (blk[:, None] * rows + jnp.arange(rows)[None, :]).reshape(-1)
        tables = rope_tables(pos, hd)

        def layer(x, l, window):
            q, k, v = qkv(l, x, ln_w, qk_w, tables[2 * l], tables[2 * l + 1], w_q, w_k, w_v)
            o = attention(window, q, k, v, 1 + l).reshape(slots * rows, -1)
            x2 = x.reshape(slots * rows, dim)
            f32 = jnp.float32
            gain = ln_w[l].astype(f32)
            att = jnp.dot(o, w_o[l], preferred_element_type=f32).astype(jnp.bfloat16)
            y = (x2.astype(f32) + norm_rows(att.astype(f32), gain[1])).astype(jnp.bfloat16)
            c = norm_rows(y.astype(f32), gain[2]).astype(jnp.bfloat16)
            gate = jnp.dot(c, w_gate[l], preferred_element_type=f32)
            up = jnp.dot(c, w_up[l], preferred_element_type=f32)
            act = (jax.nn.gelu(gate, approximate=True) * up).astype(jnp.bfloat16)
            m = jnp.dot(act, w_down[l], preferred_element_type=f32).astype(jnp.bfloat16)
            out = (y.astype(f32) + norm_rows(m.astype(f32), gain[3])).astype(jnp.bfloat16)
            return out.reshape(slots, rows, dim)

        x = exchange(True, n_dev, x_loc, 0)
        x = layer(x, 0, WINDOW)
        x = layer(x, 1, None)
        return exchange(False, n_dev, x, 3)

    act_part = P("dp", "cp", None)
    return jax.shard_map(device_fn, mesh=mesh, in_specs=(act_part,) + (P(),) * 9, out_specs=act_part, check_vma=False)
```

time: 1740 us -> 734 us (0.42)
  the two profiles are of different devices: /device:TPU:21 before, /device:TPU:63 now
where the time goes in v1:
time: 734 us; the launch traced here: 725 us
  Pallas kernels  435 us (59%)
  matrix products  268 us (37%)
  other arithmetic  17.4 us (2%)
    pallas_call x2, Pallas kernels, exchange(): pl.pallas_call(functools.partial(exchange_kernel, to_home, n_dev), out_sh...  192 us
    pallas_call x2, Pallas kernels, attention(): pl.pallas_call(body, out_shape=jax.ShapeDtypeStruct((slots, rows, nq * hd...  190 us
    dot_general x2, matrix products, layer(): up = jnp.dot(c, w_up[l], preferred_element_type=f32)  87.9 us
    dot_general x2, matrix products, layer(): gate = jnp.dot(c, w_gate[l], preferred_element_type=f32)  78.8 us
    dot_general x2, matrix products, layer(): m = jnp.dot(act, w_down[l], preferred_element_type=f32).astype(jnp.bfloat16)  76.6 us
    pallas_call x2, Pallas kernels, qkv(): pl.pallas_call(functools.partial(qkv_kernel, layer, nq, nk, slots), grid=...  53.8 us
    dot_general x2, matrix products, layer(): att = jnp.dot(o, w_o[l], preferred_element_type=f32).astype(jnp.bfloat16)  24.2 us

profile of v1, /device:TPU:63, one launch (start us, length us, event | category | flops | bytes accessed | tf_op | source)
XLA Modules:
  0.0 725.1 jit_solution(8614533587491645828)
XLA Ops:
  0.0 0.1 stack.27
  0.1 0.1 convert_bitcast_fusion
  0.2 2.5 multiply_sine_fusion.1
  2.7 0.0 copy-done.7
  2.7 98.3 %shard_map.100 = bf16[6,128,2304]{2,1,0:T(8,128)(2,1)} custom-call(bf16[6,128,2304]{2,1,0:T(8,128)(2,1)} %x_ref.1), custom_call_target="tpu_custom_call" | custom-call | tf_op jit(solution)/shard_map/pallas_call | solution.py:117
  100.9 26.8 %shard_map.101 = (bf16[6,8,128,256]{3,2,1,0:T(8,128)(2,1)}, bf16[6,128,1024]{2,1,0:T(8,128)(2,1)}, bf16[6,128,1024]{2,1,0:T(8,128)(2,1)}) custom-call(bf16[768,2304]{1,0:T(8,128)(2,1)} %bitcast.90, bf16[2,4,2304]{2,1,0:T(4,128)(2,1)} %ln_ref.3, bf16[2,2,256]{2,1,0:T(2,128)(2,1)} %qk_ref.3, f32[768,128]{1,0:T(8,128)} %get-tuple-element.32.cos_ref, ...), custom_call_target="tpu_custom_call" | custom-call | tf_op jit(solution)/shard_map/pallas_call | solution.py:180
  127.8 86.5 %shard_map.102 = bf16[6,128,2048]{2,1,0:T(8,128)(2,1)} custom-call(bf16[6,8,128,256]{3,2,1,0:T(8,128)(2,1)} %get-tuple-element.11.q_ref, bf16[6,128,1024]{2,1,0:T(8,128)(2,1)} %get-tuple-element.12.k_ref, bf16[6,128,1024]{2,1,0:T(8,128)(2,1)} %get-tuple-element.13.v_ref), custom_call_target="tpu_custom_call" | custom-call | tf_op jit(solution)/shard_map/pallas_call | solution.py:364
  214.3 0.0 copy-start.2
  214.3 0.0 copy-start
  214.3 12.1 %fusion.58 = (f32[768]{0:T(1024)S(1)}, bf16[768,2304]{1,0:T(8,128)(2,1)S(1)}) fusion(bf16[768,2048]{1,0:T(8,128)(2,1)} %bitcast.92, bf16[2,2048,2304]{2,1,0:T(8,128)(2,1)} %param.16), kind=kOutput, calls=%fused_computation.66 | convolution fusion | flops 7254834176 | bytes 16124928 | tf_op jit(solution)/shard_map/dot_general | solution.py:413
  226.4 0.0 copy-done.2
  226.4 0.8 fusion.100
  227.2 0.0 copy-done
  227.2 2.2 fusion.70
  229.4 39.4 %fusion.10 = f32[768,9216]{1,0:T(8,128)} fusion(bf16[2,2304,9216]{2,1,0:T(8,128)(2,1)} %param.17, bf16[768,2304]{1,0:T(8,128)(2,1)S(1)} %get-tuple-element.26, f32[2304]{0:T(1024)S(1)} %get-tuple-element.42, f32[768]{0:T(1024)S(1)} %add_rsqrt_fusion.4), kind=kOutput, calls=%fused_computation.10 | convolution fusion | flops 32621985792 | bytes 74330112 | tf_op jit(solution)/shard_map/dot_general | solution.py:416
  268.8 44.0 %fusion.26.clone.3.clone.5 = bf16[768,9216]{1,0:T(8,128)(2,1)} fusion(f32[768,9216]{1,0:T(8,128)} %fusion.10, bf16[2,2304,9216]{2,1,0:T(8,128)(2,1)} %param.18, bf16[768,2304]{1,0:T(8,128)(2,1)S(1)} %get-tuple-element.26, f32[2304]{0:T(1024)S(1)} %get-tuple-element.42, f32[768]{0:T(1024)S(1)} %add_rsqrt_fusion.4), kind=kOutput, calls=%fused_computation.28.clone.clone.clone.clone.clone.clone.clone.2 | convolution fusion | flops 32692764672 | bytes 88485888 | tf_op jit(solution)/shard_map/dot_general | solution.py:417
  312.8 38.3 %fusion.62 = (f32[768]{0:T(1024)S(1)}, bf16[768,2304]{1,0:T(8,128)(2,1)S(1)}) fusion(bf16[2,9216,2304]{2,1,0:T(8,128)(2,1)} %param.19, bf16[768,9216]{1,0:T(8,128)(2,1)} %fusion.26.clone.3.clone.5), kind=kOutput, calls=%fused_computation.70 | convolution fusion | flops 32621985792 | bytes 60165120 | tf_op jit(solution)/shard_map/dot_general | solution.py:419
  351.2 3.5 fusion.73.x_ref
  354.7 0.1 broadcast_multiply_fusion
  354.8 2.5 multiply_sine_fusion
  357.3 26.9 %shard_map.103 = (bf16[6,8,128,256]{3,2,1,0:T(8,128)(2,1)}, bf16[6,128,1024]{2,1,0:T(8,128)(2,1)}, bf16[6,128,1024]{2,1,0:T(8,128)(2,1)}) custom-call(bf16[768,2304]{1,0:T(8,128)(2,1)} %fusion.73.x_ref, bf16[2,4,2304]{2,1,0:T(4,128)(2,1)} %ln_ref.3, bf16[2,2,256]{2,1,0:T(2,128)(2,1)} %qk_ref.3, f32[768,128]{1,0:T(8,128)} %get-tuple-element.30.cos_ref, ...), custom_call_target="tpu_custom_call" | custom-call | tf_op jit(solution)/shard_map/pallas_call | solution.py:180
  384.3 103.2 %shard_map.104 = bf16[6,128,2048]{2,1,0:T(8,128)(2,1)} custom-call(bf16[6,8,128,256]{3,2,1,0:T(8,128)(2,1)} %get-tuple-element.14.q_ref, bf16[6,128,1024]{2,1,0:T(8,128)(2,1)} %get-tuple-element.15.k_ref, bf16[6,128,1024]{2,1,0:T(8,128)(2,1)} %get-tuple-element.16.v_ref), custom_call_target="tpu_custom_call" | custom-call | tf_op jit(solution)/shard_map/pallas_call | solution.py:364
  487.5 0.0 copy-start.1
  487.5 12.1 %fusion.64 = (f32[768]{0:T(1024)S(1)}, bf16[768,2304]{1,0:T(8,128)(2,1)S(1)}) fusion(bf16[768,2048]{1,0:T(8,128)(2,1)} %bitcast.93, bf16[2,2048,2304]{2,1,0:T(8,128)(2,1)} %param.16), kind=kOutput, calls=%fused_computation.72 | convolution fusion | flops 7254834176 | bytes 16124928 | tf_op jit(solution)/shard_map/dot_general | solution.py:413
  499.7 2.2 fusion.74
  501.9 0.0 copy-done.6
  501.9 39.4 %fusion.4 = f32[768,9216]{1,0:T(8,128)} fusion(bf16[2,2304,9216]{2,1,0:T(8,128)(2,1)} %param.17, bf16[768,2304]{1,0:T(8,128)(2,1)S(1)} %get-tuple-element.24, f32[2304]{0:T(1024)S(1)} %copy-done.6, f32[768]{0:T(1024)S(1)} %add_rsqrt_fusion.1), kind=kOutput, calls=%fused_computation.4 | convolution fusion | flops 32621985792 | bytes 74330112 | tf_op jit(solution)/shard_map/dot_general | solution.py:416
  541.3 43.9 %fusion.35.clone.3.clone.5 = bf16[768,9216]{1,0:T(8,128)(2,1)} fusion(f32[768,9216]{1,0:T(8,128)} %fusion.4, bf16[2,2304,9216]{2,1,0:T(8,128)(2,1)} %param.18, bf16[768,2304]{1,0:T(8,128)(2,1)S(1)} %get-tuple-element.24, f32[2304]{0:T(1024)S(1)} %copy-done.6, f32[768]{0:T(1024)S(1)} %add_rsqrt_fusion.1), kind=kOutput, calls=%fused_computation.37.clone.clone.clone.clone.clone.clone.clone.2 | convolution fusion | flops 32692764672 | bytes 88485888 | tf_op jit(solution)/shard_map/dot_general | solution.py:417
  585.2 38.3 %fusion.68 = (f32[768]{0:T(1024)S(1)}, bf16[768,2304]{1,0:T(8,128)(2,1)S(1)}) fusion(bf16[2,9216,2304]{2,1,0:T(8,128)(2,1)} %param.19, bf16[768,9216]{1,0:T(8,128)(2,1)} %fusion.35.clone.3.clone.5), kind=kOutput, calls=%fused_computation.76 | convolution fusion | flops 32621985792 | bytes 60165120 | tf_op jit(solution)/shard_map/dot_general | solution.py:419
  623.5 3.5 fusion.77
  627.1 93.6 %shard_map.105 = bf16[6,128,2304]{2,1,0:T(8,128)(2,1)} custom-call(bf16[6,128,2304]{2,1,0:T(8,128)(2,1)} %bitcast.91), custom_call_target="tpu_custom_call" | custom-call | tf_op jit(solution)/shard_map/pallas_call | solution.py:117
  720.7 4.0 copy.12
  (21 shorter events, 0.1 us)
Async XLA Ops:
  0.1 2.6 copy-start.7
  214.3 12.2 %copy-start.2 = (bf16[2,4,2304]{2,1,0:T(4,128)(2,1)S(1)}, bf16[2,4,2304]{2,1,0:T(4,128)(2,1)}, u32[]{:S(2)}) copy-start(bf16[2,4,2304]{2,1,0:T(4,128)(2,1)} %ln_ref.3) | copy-start | bytes 110596
  214.3 12.9 %copy-start = (bf16[6,128,2304]{2,1,0:T(8,128)(2,1)S(1)}, bf16[6,128,2304]{2,1,0:T(8,128)(2,1)}, u32[]{:S(2)}) copy-start(bf16[6,128,2304]{2,1,0:T(8,128)(2,1)} %shard_map.100) | copy-start | bytes 10616836
  312.8 38.3 %copy-start.5 = (f32[2304]{0:T(1024)S(1)}, f32[2304]{0:T(1024)}, u32[]{:S(2)}) copy-start(f32[2304]{0:T(1024)} %get-tuple-element.43) | copy-start | bytes 27652
  351.2 3.6 copy-start.8
  487.5 12.2 %copy-start.1 = (bf16[768,2304]{1,0:T(8,128)(2,1)S(1)}, bf16[768,2304]{1,0:T(8,128)(2,1)}, u32[]{:S(2)}) copy-start(bf16[768,2304]{1,0:T(8,128)(2,1)} %fusion.73.x_ref) | copy-start | bytes 10616836
  487.5 12.2 %copy-start.3 = (f32[2304]{0:T(1024)S(1)}, f32[2304]{0:T(1024)}, u32[]{:S(2)}) copy-start(f32[2304]{0:T(1024)} %get-tuple-element.19) | copy-start | bytes 27652
  499.7 2.3 copy-start.6
  585.2 38.3 %copy-start.4 = (f32[2304]{0:T(1024)S(1)}, f32[2304]{0:T(1024)}, u32[]{:S(2)}) copy-start(f32[2304]{0:T(1024)} %get-tuple-element.17) | copy-start | bytes 27652

commit v2 on v1

--- a/solution.py
+++ b/solution.py
@@ -129,7 +129,7 @@
     return vals * inv * (1.0 + gain)
 
 
-def qkv_kernel(layer, nq, nk, slots, x_ref, ln_ref, qk_ref, cos_ref, sin_ref, wq_ref, wk_ref, wv_ref, q_ref, k_ref, v_ref, a_ref):
+def qkv_kernel(layer, nq, nk, slots, x_ref, ln_ref, qk_ref, cos_ref, sin_ref, wq_ref, wk_ref, wv_ref, q_ref, k_ref, v_ref, a_ref, raw_ref):
     i = pl.program_id(0)
     rows = x_ref.shape[0] // slots
     hd = wq_ref.shape[-1]
@@ -142,30 +142,34 @@
             r = pl.ds(s * rows, rows)
             a_ref[r, :] = norm_rows(x_ref[r, :].astype(jnp.float32), gain).astype(jnp.bfloat16)
 
-    def product(s, w_ref):
-        return jnp.dot(a_ref[pl.ds(s * rows, rows), :], w_ref[0], preferred_element_type=jnp.float32).astype(jnp.bfloat16)
-
-    def turned(s, w_ref, which):
-        vals = norm_rows(product(s, w_ref).astype(jnp.float32), qk_ref[layer, which : which + 1, :].astype(jnp.float32))
+    def product(w_ref):
+        raw_ref[...] = jnp.dot(a_ref[...], w_ref[0], preferred_element_type=jnp.float32)
+
+    def turned(s, which):
+        r = pl.ds(s * rows, rows)
+        raw = raw_ref[r, :].astype(jnp.bfloat16).astype(jnp.float32)
+        vals = norm_rows(raw, qk_ref[layer, which : which + 1, :].astype(jnp.float32))
         first, second = vals[:, :half], vals[:, half:]
-        r = pl.ds(s * rows, rows)
         cos, sin = cos_ref[r, :], sin_ref[r, :]
         return jnp.concatenate([first * cos - second * sin, second * cos + first * sin], axis=-1).astype(jnp.bfloat16)
 
     @pl.when(i < nq)
     def _():
-        for s in range(slots):
-            q_ref[s, 0] = turned(s, wq_ref, 0) * jnp.bfloat16(hd**-0.5)
+        product(wq_ref)
+        for s in range(slots):
+            q_ref[s, 0] = turned(s, 0) * jnp.bfloat16(hd**-0.5)
 
     @pl.when((i >= nq) & (i < nq + nk))
     def _():
-        for s in range(slots):
-            k_ref[s] = turned(s, wk_ref, 1)
+        product(wk_ref)
+        for s in range(slots):
+            k_ref[s] = turned(s, 1)
 
     @pl.when(i >= nq + nk)
     def _():
-        for s in range(slots):
-            v_ref[s] = product(s, wv_ref)
+        product(wv_ref)
+        for s in range(slots):
+            v_ref[s] = raw_ref[pl.ds(s * rows, rows), :].astype(jnp.bfloat16)
 
 
 def qkv(layer, x, ln_w, qk_w, cos, sin, w_q, w_k, w_v):
@@ -191,19 +195,20 @@
             jax.ShapeDtypeStruct((slots, rows, nk * hd), jnp.bfloat16),
             jax.ShapeDtypeStruct((slots, rows, nk * hd), jnp.bfloat16),
         ],
-        scratch_shapes=[pltpu.VMEM(x2.shape, jnp.bfloat16)],
+        scratch_shapes=[pltpu.VMEM(x2.shape, jnp.bfloat16), pltpu.VMEM((slots * rows, hd), jnp.float32)],
         compiler_params=pltpu.CompilerParams(dimension_semantics=("arbitrary",), vmem_limit_bytes=VMEM_LIMIT),
     )(x2, ln_w, qk_w, cos, sin, w_q, w_k, w_v)
 
 
-def attn_kernel(window_blocks, q_ref, k_ref, v_ref, o_ref, kbuf, vbuf, qbuf, obuf, acc, mx, sm, bias,
+def attn_kernel(window_blocks, q_ref, k_ref, v_ref, o_ref, kbuf, vbuf, qbuf, obuf, acc, mx, sm, sbuf, wacc, wm, wl, bias,
                 qsem, ksem, vsem, ksend, vsend, fsend, krecv, vrecv, osem):
     me, chip, core, special, row = placement()
     mate = chip * 2 + (1 - core)
     slots, nq, rows, hd = q_ref.shape
     nk = k_ref.shape[-1] // hd
     rep = nq // nk
-    tile = 2 * rows
+    per = 4
+    tile = per * rows
     barrier = pltpu.get_barrier_semaphore()
 
     def tell(dev):
@@ -253,43 +258,53 @@
     qi = lax.broadcasted_iota(jnp.int32, (rows, tile), 0)
     ki = lax.broadcasted_iota(jnp.int32, (rows, tile), 1)
     bias[0] = jnp.zeros((rows, tile), jnp.float32)
-    bias[1] = jnp.where(ki <= qi, 0.0, NEG)
-    bias[2] = jnp.where(ki <= qi + rows, 0.0, NEG)
-    bias[3] = jnp.where(ki > qi, 0.0, NEG)
-    bias[4] = jnp.where(ki > qi + rows, 0.0, NEG)
-
-    def one_tile(s, t, base, blk):
-        last = blk // 2
-        edge = jnp.where(t == last, 1 + blk % 2, 0)
+    for j in range(per):
+        bias[1 + j] = jnp.where(ki <= qi + j * rows, 0.0, NEG)
         if window_blocks is not None:
-            old = (blk - window_blocks) // 2
-            edge = jnp.where((blk >= window_blocks) & (t == old), 3 + (blk - window_blocks) % 2, edge)
-        off = bias[edge]
-        off2 = jnp.concatenate([off] * rep, axis=0)
-        kt = kbuf.at[pl.ds(base + 2 * t, 2)]
-        vt = vbuf.at[pl.ds(base + 2 * t, 2)]
-        for g in range(nk):
-            u = s * nk + g
-            q2 = qbuf[s, g * rep : (g + 1) * rep].reshape(rep * rows, hd)
-            kk = kt[:, :, g * hd : (g + 1) * hd].reshape(tile, hd)
-            vv = vt[:, :, g * hd : (g + 1) * hd].reshape(tile, hd)
-            sc = lax.dot_general(q2, kk, (((1,), (1,)), ((), ())), preferred_element_type=jnp.float32) + off2
-            m_old = mx[u][:, :1]
-            m_new = jnp.maximum(m_old, jnp.max(sc, axis=-1, keepdims=True))
-            p = jnp.exp(sc - m_new)
-            alpha = jnp.exp(m_old - m_new)
-            sm[u] = jnp.broadcast_to(alpha * sm[u][:, :1] + jnp.sum(p, axis=-1, keepdims=True), sm.shape[1:])
-            mx[u] = jnp.broadcast_to(m_new, mx.shape[1:])
-            acc[u] = alpha * acc[u] + jnp.dot(p.astype(jnp.bfloat16), vv, preferred_element_type=jnp.float32)
+            bias[1 + per + j] = jnp.where(ki > qi + j * rows, 0.0, NEG)
 
     def start_tile(blk):
         if window_blocks is None:
             return jnp.int32(0)
-        return jnp.maximum(blk - window_blocks, 0) // 2
-
-    mx[...] = jnp.full(mx.shape, NEG, jnp.float32)
-    sm[...] = jnp.zeros(sm.shape, jnp.float32)
-    acc[...] = jnp.zeros(acc.shape, jnp.float32)
+        return jnp.maximum(blk - window_blocks, 0) // per
+
+    def scores(s, t, base, blk):
+        edge = jnp.where(t == blk // per, 1 + blk % per, 0)
+        if window_blocks is not None:
+            old = blk - window_blocks
+            edge = jnp.where((old >= 0) & (t == old // per), 1 + per + old % per, edge)
+        off = bias[edge][None]
+        kt = kbuf.at[pl.ds(base + per * t, per)]
+        out = []
+        for g in range(nk):
+            q2 = qbuf[s, g * rep : (g + 1) * rep].reshape(rep * rows, hd)
+            kk = kt[:, :, g * hd : (g + 1) * hd].reshape(tile, hd)
+            sc = lax.dot_general(q2, kk, (((1,), (1,)), ((), ())), preferred_element_type=jnp.float32)
+            out.append((sc.reshape(rep, rows, tile) + off).reshape(rep * rows, tile))
+        return out
+
+    lanes = 128
+
+    def columns(val, op):
+        parts = [val[:, j * lanes : (j + 1) * lanes] for j in range(tile // lanes)]
+        return functools.reduce(op, parts)
+
+    def spread(val):
+        return jnp.concatenate([val] * (tile // lanes), axis=1)
+
+    def row_max(val):
+        return jnp.broadcast_to(jnp.max(val, axis=-1, keepdims=True), val.shape)
+
+    def values(t, base, g):
+        return vbuf.at[pl.ds(base + per * t, per)][:, :, g * hd : (g + 1) * hd].reshape(tile, hd)
+
+    def finish(s, total, weight):
+        for g in range(nk):
+            out = (total[g] / jnp.sum(weight[g], axis=-1, keepdims=True)).astype(jnp.bfloat16)
+            for h in range(rep):
+                lo = (g * rep + h) * hd
+                obuf[s, :, lo : lo + hd] = out[h * rows : (h + 1) * rows]
+        pltpu.make_async_copy(obuf.at[s], o_ref.at[s], osem.at[s]).start()
 
     for s in range(slots):
         pltpu.make_async_copy(k_ref.at[s], kbuf.at[buf_index(s, core)], ksem.at[s]).wait()
@@ -302,13 +317,43 @@
 
     @pl.loop(0, slots)
     def _(s):
-        b, blk = slot_place(s, core, special, row)
-        base = jnp.where(special == 1, (s // 2) * 4, 0)
-        first = jnp.where(special == 1, 0, jnp.maximum(start_tile(blk), 2))
-
-        @pl.loop(first, blk // 2 + 1)
+        _, blk = slot_place(s, core, special, row)
+        base = jnp.where(special == 1, (s // 2) * per, 0)
+        first = jnp.where(special == 1, 0, jnp.maximum(start_tile(blk), 1))
+        last = blk // per + 1
+        for g in range(nk):
+            wm[g] = jnp.full(wm.shape[1:], NEG, jnp.float32)
+            wl[g] = jnp.zeros(wl.shape[1:], jnp.float32)
+            wacc[g] = jnp.zeros(wacc.shape[1:], jnp.float32)
+
+        @pl.loop(first, last)
         def _(t):
-            one_tile(s, t, base, blk)
+            for g, sc in enumerate(scores(s, t, base, blk)):
+                sbuf[g, t] = sc
+                wm[g] = jnp.maximum(wm[g], columns(sc, jnp.maximum))
+
+        for g in range(nk):
+            wm[g] = row_max(wm[g])
+
+        @pl.loop(first, last)
+        def _(t):
+            for g in range(nk):
+                p = jnp.exp(sbuf[g, t] - spread(wm[g]))
+                wl[g] += columns(p, jnp.add)
+                wacc[g] += jnp.dot(p.astype(jnp.bfloat16), values(t, base, g), preferred_element_type=jnp.float32)
+
+        more = (special == 0) & (start_tile(blk) == 0)
+
+        @pl.when(more)
+        def _():
+            for g in range(nk):
+                mx[s, g] = wm[g]
+                sm[s, g] = wl[g]
+                acc[s, g] = wacc[g]
+
+        @pl.when(jnp.logical_not(more))
+        def _():
+            finish(s, [wacc[g] for g in range(nk)], [wl[g] for g in range(nk)])
 
     @pl.when(special == 0)
     def _():
@@ -329,9 +374,18 @@
         def _(s):
             _, blk = slot_place(s, core, special, row)
 
-            @pl.loop(start_tile(blk), 2)
-            def _(t):
-                one_tile(s, t, 0, blk)
+            @pl.when(start_tile(blk) == 0)
+            def _():
+                total, weight = [], []
+                for g, sc in enumerate(scores(s, 0, 0, blk)):
+                    old = mx[s, g]
+                    new = row_max(jnp.maximum(old, columns(sc, jnp.maximum)))
+                    p = jnp.exp(sc - spread(new))
+                    alpha = jnp.exp(old - new)
+                    weight.append(alpha * sm[s, g] + columns(p, jnp.add))
+                    part = jnp.dot(p.astype(jnp.bfloat16), values(0, 0, g), preferred_element_type=jnp.float32)
+                    total.append(jnp.concatenate([alpha] * (hd // lanes), axis=1) * acc[s, g] + part)
+                finish(s, total, weight)
 
     @pl.when(special == 1)
     def _():
@@ -339,25 +393,15 @@
             remote(k_ref.at[s], kbuf.at[0], ksend.at[1, s], krecv.at[0], mate).wait_send()
             remote(v_ref.at[s], vbuf.at[0], vsend.at[1, s], vrecv.at[0], mate).wait_send()
 
-    @pl.loop(0, slots)
-    def _(s):
-        for g in range(nk):
-            u = s * nk + g
-            out = (acc[u] / sm[u][:, :1]).astype(jnp.bfloat16)
-            for h in range(rep):
-                lo = (g * rep + h) * hd
-                obuf[s, :, lo : lo + hd] = out[h * rows : (h + 1) * rows]
-
-    copy = pltpu.make_async_copy(obuf, o_ref, osem)
-    copy.start()
-    copy.wait()
+    for s in range(slots):
+        pltpu.make_async_copy(obuf.at[s], o_ref.at[s], osem.at[s]).wait()
 
 
 def attention(window, q, k, v, cid):
     slots, nq, rows, hd = q.shape
     nk = k.shape[-1] // hd
     blocks = 16
-    units = slots * nk
+    wide = nq // nk * rows
     dma = pltpu.SemaphoreType.DMA
     any_spec = pl.BlockSpec(memory_space=pl.ANY)
     body = functools.partial(attn_kernel, None if window is None else window // rows)
@@ -371,16 +415,108 @@
             pltpu.VMEM((blocks, rows, nk * hd), jnp.bfloat16),
             pltpu.VMEM(q.shape, jnp.bfloat16),
             pltpu.VMEM((slots, rows, nq * hd), jnp.bfloat16),
-            pltpu.VMEM((units, nq // nk * rows, hd), jnp.float32),
-            pltpu.VMEM((units, nq // nk * rows, 128), jnp.float32),
-            pltpu.VMEM((units, nq // nk * rows, 128), jnp.float32),
-            pltpu.VMEM((5, rows, 2 * rows), jnp.float32),
+            pltpu.VMEM((slots, nk, wide, hd), jnp.float32),
+            pltpu.VMEM((slots, nk, wide, 128), jnp.float32),
+            pltpu.VMEM((slots, nk, wide, 128), jnp.float32),
+            pltpu.VMEM((nk, blocks // 4, wide, 4 * rows), jnp.float32),
+            pltpu.VMEM((nk, wide, hd), jnp.float32),
+            pltpu.VMEM((nk, wide, 128), jnp.float32),
+            pltpu.VMEM((nk, wide, 128), jnp.float32),
+            pltpu.VMEM((9, rows, 4 * rows), jnp.float32),
             dma((slots,)), dma((slots,)), dma((slots,)),
             dma((2, slots)), dma((2, slots)), dma((2, 2)),
-            dma((blocks,)), dma((blocks,)), dma,
+            dma((blocks,)), dma((blocks,)), dma((slots,)),
         ],
         compiler_params=pltpu.CompilerParams(collective_id=cid, has_side_effects=True, vmem_limit_bytes=VMEM_LIMIT),
     )(q, k, v)
+
+
+def post_kernel(layer, n_o, n_f, slots, o_ref, x_ref, ln_ref, wo_ref, wg_ref, wu_ref, wd_ref, out_ref, att, y_ref, c_ref, acc, act):
+    i = pl.program_id(0)
+    rows = x_ref.shape[0] // slots
+    tn = wo_ref.shape[-1]
+    f32 = jnp.float32
+
+    @pl.when(i < n_o)
+    def _():
+        part = jnp.dot(o_ref[...], wo_ref[0], preferred_element_type=f32).astype(jnp.bfloat16)
+        att[:, pl.ds(pl.multiple_of(i * tn, tn), tn)] = part
+
+    @pl.when(i == n_o - 1)
+    def _():
+        for s in range(slots):
+            r = pl.ds(s * rows, rows)
+            y = x_ref[r, :].astype(f32) + norm_rows(att[r, :].astype(f32), ln_ref[layer, 1:2, :].astype(f32))
+            y = y.astype(jnp.bfloat16)
+            y_ref[r, :] = y
+            c_ref[r, :] = norm_rows(y.astype(f32), ln_ref[layer, 2:3, :].astype(f32)).astype(jnp.bfloat16)
+
+    def up(slot):
+        gate = jnp.dot(c_ref[...], wg_ref[0], preferred_element_type=f32)
+        val = jnp.dot(c_ref[...], wu_ref[0], preferred_element_type=f32)
+        act[slot] = (jax.nn.gelu(gate, approximate=True) * val).astype(jnp.bfloat16)
+
+    def down(slot):
+        return jnp.dot(act[slot], wd_ref[0], preferred_element_type=f32)
+
+    j = i - n_o
+
+    @pl.when(j == 0)
+    def _():
+        up(0)
+
+    @pl.when(j == 1)
+    def _():
+        acc[...] = down(0)
+        up(1)
+
+    for parity in range(2):
+
+        @pl.when((j > 1) & (j < n_f) & (j % 2 == parity))
+        def _():
+            acc[...] += down(1 - parity)
+            up(parity)
+
+    @pl.when(j == n_f)
+    def _():
+        acc[...] += down((n_f - 1) % 2)
+        for s in range(slots):
+            r = pl.ds(s * rows, rows)
+            m = acc[r, :].astype(jnp.bfloat16).astype(f32)
+            out = y_ref[r, :].astype(f32) + norm_rows(m, ln_ref[layer, 3:4, :].astype(f32))
+            out_ref[r, :] = out.astype(jnp.bfloat16)
+
+
+def post(layer, o, x, ln_w, w_o, w_gate, w_up, w_down):
+    slots, rows, dim = x.shape
+    inner, ff = w_o.shape[1], w_gate.shape[-1]
+    total = slots * rows
+    tn, tf = min(256, dim), min(512, ff)
+    n_o, n_f = dim // tn, ff // tf
+    o2, x2 = o.reshape(total, inner), x.reshape(total, dim)
+    one = lambda a: pl.BlockSpec(a.shape, lambda i: (0,) * a.ndim, pipeline_mode=pl.Buffered(1))
+    at_f = lambda i: jnp.clip(i - n_o, 0, n_f - 1)
+    return pl.pallas_call(
+        functools.partial(post_kernel, layer, n_o, n_f, slots),
+        grid=(n_o + n_f + 1,),
+        in_specs=[
+            one(o2), one(x2), one(ln_w),
+            pl.BlockSpec((1, inner, tn), lambda i: (layer, 0, jnp.minimum(i, n_o - 1))),
+            pl.BlockSpec((1, dim, tf), lambda i: (layer, 0, at_f(i))),
+            pl.BlockSpec((1, dim, tf), lambda i: (layer, 0, at_f(i))),
+            pl.BlockSpec((1, tf, dim), lambda i: (layer, at_f(i - 1), 0)),
+        ],
+        out_specs=pl.BlockSpec((total, dim), lambda i: (0, 0), pipeline_mode=pl.Buffered(1)),
+        out_shape=jax.ShapeDtypeStruct((total, dim), jnp.bfloat16),
+        scratch_shapes=[
+            pltpu.VMEM((total, dim), jnp.bfloat16),
+            pltpu.VMEM((total, dim), jnp.bfloat16),
+            pltpu.VMEM((total, dim), jnp.bfloat16),
+            pltpu.VMEM((total, dim), jnp.float32),
+            pltpu.VMEM((2, total, tf), jnp.bfloat16),
+        ],
+        compiler_params=pltpu.CompilerParams(dimension_semantics=("arbitrary",), vmem_limit_bytes=VMEM_LIMIT),
+    )(o2, x2, ln_w, w_o, w_gate, w_up, w_down).reshape(slots, rows, dim)
 
 
 def rope_tables(pos, hd):
@@ -406,19 +542,8 @@
 
         def layer(x, l, window):
             q, k, v = qkv(l, x, ln_w, qk_w, tables[2 * l], tables[2 * l + 1], w_q, w_k, w_v)
-            o = attention(window, q, k, v, 1 + l).reshape(slots * rows, -1)
-            x2 = x.reshape(slots * rows, dim)
-            f32 = jnp.float32
-            gain = ln_w[l].astype(f32)
-            att = jnp.dot(o, w_o[l], preferred_element_type=f32).astype(jnp.bfloat16)
-            y = (x2.astype(f32) + norm_rows(att.astype(f32), gain[1])).astype(jnp.bfloat16)
-            c = norm_rows(y.astype(f32), gain[2]).astype(jnp.bfloat16)
-            gate = jnp.dot(c, w_gate[l], preferred_element_type=f32)
-            up = jnp.dot(c, w_up[l], preferred_element_type=f32)
-            act = (jax.nn.gelu(gate, approximate=True) * up).astype(jnp.bfloat16)
-            m = jnp.dot(act, w_down[l], preferred_element_type=f32).astype(jnp.bfloat16)
-            out = (y.astype(f32) + norm_rows(m.astype(f32), gain[3])).astype(jnp.bfloat16)
-            return out.reshape(slots, rows, dim)
+            o = attention(window, q, k, v, 1 + l)
+            return post(l, o, x, ln_w, w_o, w_gate, w_up, w_down)
 
         x = exchange(True, n_dev, x_loc, 0)
         x = layer(x, 0, WINDOW)

time: 734 us -> 628 us (0.86)
  the two profiles are of different devices: /device:TPU:63 before, /device:TPU:21 now
where the time goes in v2:
time: 628 us; the launch traced here: 620 us
  Pallas kernels  611 us (97%)
    pallas_call x2, Pallas kernels, post(): pl.pallas_call(functools.partial(post_kernel, layer, n_o, n_f, slots), gr...  251 us
    pallas_call x2, Pallas kernels, exchange(): pl.pallas_call(functools.partial(exchange_kernel, to_home, n_dev), out_sh...  199 us
    pallas_call x2, Pallas kernels, attention(): pl.pallas_call(body, out_shape=jax.ShapeDtypeStruct((slots, rows, nq * hd...  106 us
    pallas_call x2, Pallas kernels, qkv(): pl.pallas_call(functools.partial(qkv_kernel, layer, nq, nk, slots), grid=...  53.7 us

profile of v2, /device:TPU:21, one launch (start us, length us, event | category | flops | bytes accessed | tf_op | source)
XLA Modules:
  0.0 620.3 jit_solution(11169407123832797959)
XLA Ops:
  0.0 0.1 stack.27
  0.1 0.1 convert_bitcast_fusion
  0.2 2.5 multiply_sine_fusion.1
  2.7 84.8 %shard_map.100 = bf16[6,128,2304]{2,1,0:T(8,128)(2,1)} custom-call(bf16[6,128,2304]{2,1,0:T(8,128)(2,1)} %x_ref.1), custom_call_target="tpu_custom_call" | custom-call | tf_op jit(solution)/shard_map/pallas_call | solution.py:117
  87.5 26.8 %shard_map.101 = (bf16[6,8,128,256]{3,2,1,0:T(8,128)(2,1)}, bf16[6,128,1024]{2,1,0:T(8,128)(2,1)}, bf16[6,128,1024]{2,1,0:T(8,128)(2,1)}) custom-call(bf16[768,2304]{1,0:T(8,128)(2,1)} %bitcast.14, bf16[2,4,2304]{2,1,0:T(4,128)(2,1)} %ln_ref.7, bf16[2,2,256]{2,1,0:T(2,128)(2,1)} %qk_ref.3, f32[768,128]{1,0:T(8,128)} %get-tuple-element.20.cos_ref, ...), custom_call_target="tpu_custom_call" | custom-call | tf_op jit(solution)/shard_map/pallas_call | solution.py:184
  114.4 46.4 %shard_map.102 = bf16[6,128,2048]{2,1,0:T(8,128)(2,1)} custom-call(bf16[6,8,128,256]{3,2,1,0:T(8,128)(2,1)} %get-tuple-element.11.q_ref, bf16[6,128,1024]{2,1,0:T(8,128)(2,1)} %get-tuple-element.12.k_ref, bf16[6,128,1024]{2,1,0:T(8,128)(2,1)} %get-tuple-element.13.v_ref), custom_call_target="tpu_custom_call" | custom-call | tf_op jit(solution)/shard_map/pallas_call | solution.py:408
  160.7 125.9 %shard_map.103.x_ref = bf16[768,2304]{1,0:T(8,128)(2,1)} custom-call(bf16[768,2048]{1,0:T(8,128)(2,1)} %bitcast.17, bf16[768,2304]{1,0:T(8,128)(2,1)} %bitcast.15, bf16[2,4,2304]{2,1,0:T(4,128)(2,1)} %ln_ref.7, bf16[2,2048,2304]{2,1,0:T(8,128)(2,1)} %wo_ref.3, bf16[2,2304,9216]{2,1,0:T(8,128)(2,1)} %wg_ref.3, bf16[2,2304,9216]{2,1,0:T(8,128)(2,1)} %wu_ref.3, ...), custom_call_target="tpu_custom_call" | custom-call | tf_op jit(solution)/shard_map/pallas_call | solution.py:499
  286.6 0.1 broadcast_multiply_fusion
  286.7 2.5 multiply_sine_fusion
  289.2 26.9 %shard_map.104 = (bf16[6,8,128,256]{3,2,1,0:T(8,128)(2,1)}, bf16[6,128,1024]{2,1,0:T(8,128)(2,1)}, bf16[6,128,1024]{2,1,0:T(8,128)(2,1)}) custom-call(bf16[768,2304]{1,0:T(8,128)(2,1)} %shard_map.103.x_ref, bf16[2,4,2304]{2,1,0:T(4,128)(2,1)} %ln_ref.7, bf16[2,2,256]{2,1,0:T(2,128)(2,1)} %qk_ref.3, f32[768,128]{1,0:T(8,128)} %get-tuple-element.18.cos_ref, ...), custom_call_target="tpu_custom_call" | custom-call | tf_op jit(solution)/shard_map/pallas_call | solution.py:184
  316.1 59.8 %shard_map.105 = bf16[6,128,2048]{2,1,0:T(8,128)(2,1)} custom-call(bf16[6,8,128,256]{3,2,1,0:T(8,128)(2,1)} %get-tuple-element.14.q_ref, bf16[6,128,1024]{2,1,0:T(8,128)(2,1)} %get-tuple-element.15.k_ref, bf16[6,128,1024]{2,1,0:T(8,128)(2,1)} %get-tuple-element.16.v_ref), custom_call_target="tpu_custom_call" | custom-call | tf_op jit(solution)/shard_map/pallas_call | solution.py:408
  375.9 125.6 %shard_map.106 = bf16[768,2304]{1,0:T(8,128)(2,1)} custom-call(bf16[768,2048]{1,0:T(8,128)(2,1)} %bitcast.18, bf16[768,2304]{1,0:T(8,128)(2,1)} %shard_map.103.x_ref, bf16[2,4,2304]{2,1,0:T(4,128)(2,1)} %ln_ref.7, bf16[2,2048,2304]{2,1,0:T(8,128)(2,1)} %wo_ref.3, bf16[2,2304,9216]{2,1,0:T(8,128)(2,1)} %wg_ref.3, bf16[2,2304,9216]{2,1,0:T(8,128)(2,1)} %wu_ref.3, ...), custom_call_target="tpu_custom_call" | custom-call | tf_op jit(solution)/shard_map/pallas_call | solution.py:499
  501.5 114.4 %shard_map.107 = bf16[6,128,2304]{2,1,0:T(8,128)(2,1)} custom-call(bf16[6,128,2304]{2,1,0:T(8,128)(2,1)} %bitcast.16), custom_call_target="tpu_custom_call" | custom-call | tf_op jit(solution)/shard_map/pallas_call | solution.py:117
  615.9 4.0 copy.12
  (3 shorter events, 0.0 us)

commit v3 on v0

v3 whole, which is shorter than its diff:
```python
import functools

import jax
import jax.numpy as jnp
from jax import lax
from jax.experimental import pallas as pl
from jax.experimental.pallas import tpu as pltpu
from jax.sharding import PartitionSpec as P

WINDOW = 1024
NORM_EPS = 1e-6
LOCAL_BASE = 10000.0
GLOBAL_BASE = 1000000.0
GLOBAL_SCALE = 8.0
NEG = -1e30

ROW_CHIP = (0, 3, 4, 1, 5, 6)
SPECIAL = (2, 7)
VMEM_LIMIT = 64 * 1024 * 1024 - 128 * 1024
MESH = pl.DeviceIdType.MESH
BF16, F32 = jnp.bfloat16, jnp.float32
ANY = pl.BlockSpec(memory_space=pl.ANY)
WHOLE = pl.BlockSpec(memory_space=pltpu.VMEM)
DMA = pltpu.SemaphoreType.DMA


def pick(idx, table):
    out = jnp.int32(table[-1])
    for i in range(len(table) - 2, -1, -1):
        out = jnp.where(idx == i, jnp.int32(table[i]), out)
    return out


def placement():
    me = lax.axis_index("cp")
    chip, core = me // 2, me % 2
    roles = [0] * 8
    rows = [0] * 8
    for b, c in enumerate(ROW_CHIP):
        rows[c] = b
    for i, c in enumerate(SPECIAL):
        roles[c] = 1
        rows[c] = 3 * i
    return me, chip, core, pick(chip, roles), pick(chip, rows)


def slot_place(s, core, special, row):
    k = s % 2
    blk = jnp.where(special == 1, 2 * k + (k + core) % 2, 4 + 2 * s + (s + core) % 2)
    b = jnp.where(special == 1, row + s // 2, row)
    return b, blk


def ring(a, b):
    return min((a - b) % 8, (b - a) % 8)


ARRIVAL = [sorted(range(6), key=lambda s: (ring(2 + s, c), s)) for c in range(8)]
for c in SPECIAL:
    ARRIVAL[c] = [4, 5, 0, 2, 1, 3]


def home_of(b, blk):
    core = ((blk + 1) // 2) % 2
    half = blk // 2
    chip = jnp.where(blk < 4, pick(b // 3, SPECIAL), pick(b, ROW_CHIP))
    slot = jnp.where(blk < 4, (b % 3) * 2 + half, half - 2)
    return chip * 2 + core, slot


def chunk_slot(ch, i, special, row):
    b = jnp.where(special == 1, row + i, row)
    return 2 * i + (b % 2 if ch == 0 else 1 - b % 2)


def kv_index(s, core, special, row):
    _, blk = slot_place(s, core, special, row)
    return jnp.where(special == 1, (s // 2) * 4 + blk, blk)


def served(row, r):
    return jnp.where(row == 0, ROW_CHIP[r], ROW_CHIP[r + 3])


def signal_group(n_dev):
    me = lax.axis_index("cp")
    barrier = pltpu.get_barrier_semaphore()
    for d in range(1, n_dev):
        pl.semaphore_signal(barrier, inc=1, device_id={"cp": lax.rem(me + d, n_dev)}, device_id_type=MESH)


def wait_group(n_dev):
    pl.semaphore_wait(pltpu.get_barrier_semaphore(), n_dev - 1)


def remote(src, dst, send, recv, dev):
    return pltpu.make_async_remote_copy(
        src_ref=src, dst_ref=dst, send_sem=send, recv_sem=recv, device_id={"cp": dev}, device_id_type=MESH
    )


def local(src, dst, sem):
    return pltpu.make_async_copy(src, dst, sem)


def norm_rows(vals, gain):
    inv = lax.rsqrt(jnp.mean(vals * vals, axis=-1, keepdims=True) + NORM_EPS)
    return vals * inv * (1.0 + gain)


def norm_turn(raw, gain, cos, sin):
    half = raw.shape[-1] // 2
    vals = norm_rows(raw.astype(BF16).astype(F32), gain)
    first, second = vals[:, :half], vals[:, half:]
    return jnp.concatenate([first * cos - second * sin, second * cos + first * sin], axis=-1).astype(BF16)


class KeyValues:
    def __init__(self, k_all, v_all, send, recv, fwd):
        self.me, chip, self.core, self.special, self.row = placement()
        self.mate = chip * 2 + 1 - self.core
        self.both = ((0, k_all), (1, v_all))
        self.send, self.recv, self.fwd = send, recv, fwd

    def _copies(self, s, stage):
        idx = kv_index(s, self.core, self.special, self.row)
        _, blk = slot_place(s, self.core, self.special, self.row)
        dev = served(self.row, 0) * 2 + self.core
        for r in (1, 2):
            dev = jnp.where(s // 2 == r, served(self.row, r) * 2 + self.core, dev)
        out = []
        for x, full in self.both:
            out.append((
                local(stage[x], full.at[idx], self.send.at[x, 0, s]),
                remote(stage[x], full.at[idx], self.send.at[x, 1, s], self.recv.at[x, idx], self.mate),
                remote(stage[x], full.at[blk], self.send.at[x, 2, s], self.recv.at[x, blk], dev),
            ))
        return out

    def start(self, s, stage):
        for own, mate, row in self._copies(s, stage):

            @pl.when(self.special == 1)
            def _():
                row.start()

            mate.start()
            own.start()

    def wait_sent(self, s, stage):
        for own, mate, row in self._copies(s, stage):
            own.wait()
            mate.wait_send()

            @pl.when(self.special == 1)
            def _():
                row.wait_send()

    def wait_all(self, slots):
        for x, full in self.both:

            @pl.when(self.special == 0)
            def _():
                for k in range(2):
                    blk = 2 * k + (k + self.core) % 2
                    remote(full.at[blk], full.at[blk], self.fwd.at[x, k], self.recv.at[x, blk], self.mate).wait_recv()
                    remote(full.at[blk], full.at[blk], self.fwd.at[x, k], self.recv.at[x, blk], self.mate).start()

            for s in range(slots):
                idx = kv_index(s, 1 - self.core, self.special, self.row)
                remote(full.at[idx], full.at[idx], self.fwd.at[x, 0], self.recv.at[x, idx], self.mate).wait_recv()

        @pl.when(self.special == 0)
        def _():
            for x, full in self.both:
                for k in range(2):
                    blk = 2 * k + (k + 1 - self.core) % 2
                    remote(full.at[blk], full.at[blk], self.fwd.at[x, k], self.recv.at[x, blk], self.mate).wait()


def first_kernel(n_dev, nq, nk, x_ref, ln_ref, qk_ref, cos_ref, sin_ref, wq_ref, wk_ref, wv_ref,
                 h_ref, q_ref, k_all, v_all, xbuf, abuf, wq, wk, wv, qst, kst, vst,
                 wsem, xsend, xrecv, hsem, qsem, ksend, krecv, fsem):
    me, chip, core, special, row = placement()
    n, rows, dim = x_ref.shape
    hd = qk_ref.shape[-1]
    homes = [home_of(jnp.int32(b), me) for b in range(n)]
    keys = KeyValues(k_all, v_all, ksend, krecv, fsem)

    signal_group(n_dev)
    for b, (dev, slot) in enumerate(homes):

        @pl.when(dev == me)
        def _():
            local(x_ref.at[b], xbuf.at[slot], xrecv.at[slot]).start()

    weights = ((wk_ref, wk), (wv_ref, wv), (wq_ref, wq))
    for j, (src, dst) in enumerate(weights):
        local(src.at[0], dst, wsem.at[j]).start()
    wait_group(n_dev)
    for b in SEND_ORDER:
        dev, slot = homes[b]

        @pl.when(dev != me)
        def _():
            remote(x_ref.at[b], xbuf.at[slot], xsend.at[b], xrecv.at[slot], dev).start()

    gain = ln_ref[0, 0:1, :].astype(F32)

    def take(pair):
        places = [pick(chip, [ARRIVAL[c][2 * pair + j] for c in range(8)]) for j in range(2)]
        for j, s in enumerate(places):
            local(xbuf.at[s], xbuf.at[s], xrecv.at[s]).wait()
            local(xbuf.at[s], h_ref.at[s], hsem.at[s]).start()
            abuf[j * rows : (j + 1) * rows, :] = norm_rows(xbuf[s].astype(F32), gain).astype(BF16)
        return places

    def tables(s):
        r = pl.ds(pl.multiple_of(s * rows, rows), rows)
        return cos_ref[r, :], sin_ref[r, :]

    def product(w, h):
        return jnp.dot(abuf[...], w[:, pl.ds(pl.multiple_of(h * hd, hd), hd)], preferred_element_type=F32)

    for pair in range(n // 2):
        places = take(pair)
        if pair == 0:
            local(wk_ref.at[0], wk, wsem.at[0]).wait()
            local(wv_ref.at[0], wv, wsem.at[1]).wait()
        turn = [tables(s) for s in places]
        k_gain = qk_ref[0, 1:2, :].astype(F32)
        q_gain = qk_ref[0, 0:1, :].astype(F32)

        @pl.loop(0, nk)
        def _(h):
            col = pl.ds(pl.multiple_of(h * hd, hd), hd)
            k_raw, v_raw = product(wk, h), product(wv, h)
            for j, s in enumerate(places):
                part = slice(j * rows, (j + 1) * rows)
                kst[s, :, col] = norm_turn(k_raw[part], k_gain, *turn[j])
                vst[s, :, col] = v_raw[part].astype(BF16)

        if pair == 0:
            local(wq_ref.at[0], wq, wsem.at[2]).wait()

        @pl.loop(0, nq)
        def _(h):
            raw = product(wq, h)
            for j, s in enumerate(places):
                part = slice(j * rows, (j + 1) * rows)
                qst[s, h] = norm_turn(raw[part], q_gain, *turn[j]) * BF16(hd**-0.5)

        for s in places:
            keys.start(s, (kst.at[s], vst.at[s]))
            local(qst.at[s], q_ref.at[s], qsem.at[s]).start()

    for s in range(n):
        keys.wait_sent(s, (kst.at[s], vst.at[s]))
        local(qst.at[s], q_ref.at[s], qsem.at[s]).wait()
        local(xbuf.at[s], h_ref.at[s], hsem.at[s]).wait()
    for b, (dev, slot) in enumerate(homes):

        @pl.when(dev != me)
        def _():
            remote(x_ref.at[b], xbuf.at[slot], xsend.at[b], xrecv.at[slot], dev).wait_send()

    keys.wait_all(n)


SEND_ORDER = (2, 5, 0, 3, 1, 4)


def first(n_dev, x, ln_w, qk_w, cos, sin, w_q, w_k, w_v):
    n, rows, dim = x.shape
    hd = qk_w.shape[-1]
    nq, nk = w_q.shape[-1] // hd, w_k.shape[-1] // hd
    blocks = 16
    q_shape, s_shape, kv_shape = (n, nq, rows, hd), (n, rows, nk * hd), (blocks, rows, nk * hd)
    return pl.pallas_call(
        functools.partial(first_kernel, n_dev, nq, nk),
        out_shape=[jax.ShapeDtypeStruct(a, BF16) for a in (x.shape, q_shape, kv_shape, kv_shape)],
        in_specs=[ANY, WHOLE, WHOLE, WHOLE, WHOLE, ANY, ANY, ANY],
        out_specs=[ANY] * 4,
        scratch_shapes=[
            pltpu.VMEM(x.shape, BF16), pltpu.VMEM((2 * rows, dim), BF16),
            pltpu.VMEM(w_q.shape[1:], BF16), pltpu.VMEM(w_k.shape[1:], BF16), pltpu.VMEM(w_v.shape[1:], BF16),
            pltpu.VMEM(q_shape, BF16), pltpu.VMEM(s_shape, BF16), pltpu.VMEM(s_shape, BF16),
            DMA((3,)), DMA((n,)), DMA((n,)), DMA((n,)), DMA((n,)), DMA((2, 3, n)), DMA((2, blocks)), DMA((2, 2)),
        ],
        compiler_params=pltpu.CompilerParams(collective_id=0, has_side_effects=True, vmem_limit_bytes=VMEM_LIMIT),
    )(x, ln_w, qk_w, cos, sin, w_q, w_k, w_v)


def attn_kernel(window_blocks, q_ref, k_ref, v_ref, o_ref, kbuf, vbuf, qbuf, obuf, sbuf, wacc, wm, wl, bias, qsem, ksem, osem):
    _, _, core, special, row = placement()
    slots, nq, rows, hd = q_ref.shape
    nk = k_ref.shape[-1] // hd
    rep = nq // nk
    per = 4
    tile = per * rows
    tiles = k_ref.shape[0] // per

    def loads(t):
        part = pl.ds(t * per, per)
        return [local(k_ref.at[part], kbuf.at[part], ksem.at[0, t]), local(v_ref.at[part], vbuf.at[part], ksem.at[1, t])]

    for s in range(slots):
        local(q_ref.at[s], qbuf.at[s], qsem.at[s]).start()
    for t in range(tiles):
        for c in loads(t):
            c.start()

    qi = lax.broadcasted_iota(jnp.int32, (rows, tile), 0)
    ki = lax.broadcasted_iota(jnp.int32, (rows, tile), 1)
    bias[0] = jnp.zeros((rows, tile), jnp.float32)
    for j in range(per):
        bias[1 + j] = jnp.where(ki <= qi + j * rows, 0.0, NEG)
        if window_blocks is not None:
            bias[1 + per + j] = jnp.where(ki > qi + j * rows, 0.0, NEG)

    def start_tile(blk):
        if window_blocks is None:
            return jnp.int32(0)
        return jnp.maximum(blk - window_blocks, 0) // per

    def scores(s, t, base, blk):
        edge = jnp.where(t == blk // per, 1 + blk % per, 0)
        if window_blocks is not None:
            old = blk - window_blocks
            edge = jnp.where((old >= 0) & (t == old // per), 1 + per + old % per, edge)
        off = bias[edge][None]
        kt = kbuf.at[pl.ds(base + per * t, per)]
        out = []
        for g in range(nk):
            q2 = qbuf[s, g * rep : (g + 1) * rep].reshape(rep * rows, hd)
            kk = kt[:, :, g * hd : (g + 1) * hd].reshape(tile, hd)
            sc = lax.dot_general(q2, kk, (((1,), (1,)), ((), ())), preferred_element_type=jnp.float32)
            out.append((sc.reshape(rep, rows, tile) + off).reshape(rep * rows, tile))
        return out

    lanes = 128

    def columns(val, op):
        parts = [val[:, j * lanes : (j + 1) * lanes] for j in range(tile // lanes)]
        return functools.reduce(op, parts)

    def spread(val):
        return jnp.concatenate([val] * (tile // lanes), axis=1)

    def row_max(val):
        return jnp.broadcast_to(jnp.max(val, axis=-1, keepdims=True), val.shape)

    def values(t, base, g):
        return vbuf.at[pl.ds(base + per * t, per)][:, :, g * hd : (g + 1) * hd].reshape(tile, hd)

    def finish(s, total, weight):
        for g in range(nk):
            out = (total[g] / jnp.sum(weight[g], axis=-1, keepdims=True)).astype(jnp.bfloat16)
            for h in range(rep):
                lo = (g * rep + h) * hd
                obuf[s, :, lo : lo + hd] = out[h * rows : (h + 1) * rows]
        local(obuf.at[s], o_ref.at[s], osem.at[s]).start()

    for t in range(tiles):
        for c in loads(t):
            c.wait()

    @pl.loop(0, slots)
    def _(s):
        _, blk = slot_place(s, core, special, row)
        base = jnp.where(special == 1, (s // 2) * per, 0)
        first = start_tile(blk)
        last = blk // per + 1
        local(q_ref.at[s], qbuf.at[s], qsem.at[s]).wait()
        for g in range(nk):
            wm[g] = jnp.full(wm.shape[1:], NEG, F32)
            wl[g] = jnp.zeros(wl.shape[1:], F32)
            wacc[g] = jnp.zeros(wacc.shape[1:], F32)

        @pl.loop(first, last)
        def _(t):
            for g, sc in enumerate(scores(s, t, base, blk)):
                sbuf[g, t] = sc
                wm[g] = jnp.maximum(wm[g], columns(sc, jnp.maximum))

        for g in range(nk):
            wm[g] = row_max(wm[g])

        @pl.loop(first, last)
        def _(t):
            for g in range(nk):
                p = jnp.exp(sbuf[g, t] - spread(wm[g]))
                wl[g] += columns(p, jnp.add)
                wacc[g] += jnp.dot(p.astype(BF16), values(t, base, g), preferred_element_type=F32)

        finish(s, [wacc[g] for g in range(nk)], [wl[g] for g in range(nk)])

    for s in range(slots):
        local(obuf.at[s], o_ref.at[s], osem.at[s]).wait()


def attention(window, q, k, v):
    slots, nq, rows, hd = q.shape
    blocks = k.shape[0]
    nk = k.shape[-1] // hd
    wide = nq // nk * rows
    return pl.pallas_call(
        functools.partial(attn_kernel, None if window is None else window // rows),
        out_shape=jax.ShapeDtypeStruct((slots, rows, nq * hd), BF16),
        in_specs=[ANY] * 3,
        out_specs=ANY,
        scratch_shapes=[
            pltpu.VMEM(k.shape, BF16), pltpu.VMEM(v.shape, BF16), pltpu.VMEM(q.shape, BF16),
            pltpu.VMEM((slots, rows, nq * hd), BF16),
            pltpu.VMEM((nk, blocks // 4, wide, 4 * rows), F32),
            pltpu.VMEM((nk, wide, hd), F32), pltpu.VMEM((nk, wide, 128), F32), pltpu.VMEM((nk, wide, 128), F32),
            pltpu.VMEM((9, rows, 4 * rows), F32),
            DMA((slots,)), DMA((2, blocks // 4)), DMA((slots,)),
        ],
        compiler_params=pltpu.CompilerParams(vmem_limit_bytes=VMEM_LIMIT),
    )(q, k, v)


def layer_kernel(layer, last, n_dev, n_o, n_f, n_k, n_q, *refs):
    if last:
        (o_ref, x_ref, ln_ref, wo_ref, wg_ref, wu_ref, wd_ref, out_ref,
         att, y_ref, c_ref, acc, act, ybuf, ysend, yrecv, osend, orecv) = refs
    else:
        (o_ref, x_ref, ln_ref, qk_ref, cos_ref, sin_ref, wo_ref, wg_ref, wu_ref, wd_ref, wk_ref, wv_ref, wq_ref,
         h_ref, q_ref, k_all, v_all,
         att, y_ref, c_ref, acc, act, qst, kst, vst, hsem, qsem, ksend, krecv, fsem) = refs
        keys = KeyValues(k_all, v_all, ksend, krecv, fsem)
        hd = qk_ref.shape[-1]
    me, chip, core, special, row = placement()
    i = pl.program_id(0)
    half = y_ref.shape[1]
    rows = half // 3
    tn = wo_ref.shape[-1]
    span = n_f + 1 + n_k + n_k + n_q

    def slot_rows(s):
        return pl.ds(pl.multiple_of(s * rows, rows), rows)

    def own_rows(m):
        return pl.ds(m * rows, rows)

    def gain(which, l=layer):
        return ln_ref[l, which : which + 1, :].astype(F32)

    def c_of(y):
        return norm_rows(y.astype(F32), gain(2)).astype(BF16)

    @pl.when(i == 0)
    def _():
        signal_group(n_dev)

    @pl.when(i < n_o)
    def _():
        part = jnp.dot(o_ref[...], wo_ref[0], preferred_element_type=F32).astype(BF16)
        att[:, pl.ds(pl.multiple_of(i * tn, tn), tn)] = part

    @pl.when(i == n_o - 1)
    def _():
        for ch in range(2):
            for m in range(3):
                r = slot_rows(chunk_slot(ch, m, special, row))
                y = x_ref[r, :].astype(F32) + norm_rows(att[r, :].astype(F32), gain(1))
                y = y.astype(BF16)
                y_ref[ch, own_rows(m), :] = y
                if ch == 0:
                    c_ref[own_rows(m), :] = c_of(y)

    t = i - n_o

    def up(slot):
        gate = jnp.dot(c_ref[...], wg_ref[0], preferred_element_type=F32)
        val = jnp.dot(c_ref[...], wu_ref[0], preferred_element_type=F32)
        act[slot] = (jax.nn.gelu(gate, approximate=True) * val).astype(BF16)

    def down(slot):
        return jnp.dot(act[slot], wd_ref[0], preferred_element_type=F32)

    j = t % span

    @pl.when((t >= 0) & (j == 0))
    def _():
        up(0)

    @pl.when((t >= 0) & (j == 1))
    def _():
        acc[...] = down(0)
        up(1)

    for parity in range(2):

        @pl.when((t >= 0) & (j > 1) & (j < n_f) & (j % 2 == parity))
        def _():
            acc[...] += down(1 - parity)
            up(parity)

    @pl.when((t >= 0) & (j == n_f))
    def _():
        acc[...] += down((n_f - 1) % 2)

    def result(m, y):
        val = acc[own_rows(m), :].astype(BF16).astype(F32)
        return (y.astype(F32) + norm_rows(val, gain(3))).astype(BF16)

    if last:
        def sent(ch, m):
            b, blk = slot_place(chunk_slot(ch, m, special, row), core, special, row)
            src = y_ref.at[ch, own_rows(m)]
            if ch == 0:
                far = lambda: remote(src, out_ref.at[b], osend.at[m], orecv.at[b], blk)
                return blk, far, lambda: local(src, out_ref.at[b], orecv.at[b])
            return blk, lambda: remote(src, ybuf.at[b // 2], ysend.at[m], yrecv.at[b // 2], blk), None

        def owned(ch, m):
            turn = (me // 2) % 2
            b = 2 * m + (turn if ch == 0 else 1 - turn)
            return b, home_of(b, me)[0]

        @pl.when(t == 1)
        def _():
            wait_group(n_dev)
            for m in range(3):
                dev, far, _ = sent(1, m)

                @pl.when(dev != me)
                def _():
                    far().start()

        @pl.when(t == n_f)
        def _():
            for m in range(3):
                y_ref[0, own_rows(m), :] = result(m, y_ref[0, own_rows(m), :])
            for m in range(3):
                b, dev = owned(1, m)

                @pl.when(dev != me)
                def _():
                    remote(ybuf.at[m], ybuf.at[m], ysend.at[m], yrecv.at[m], me).wait_recv()

            for m in range(3):
                b, blk = slot_place(chunk_slot(1, m, special, row), core, special, row)

                @pl.when(blk == me)
                def _():
                    ybuf[b // 2] = y_ref[1, own_rows(m), :]

            for m in range(3):
                c_ref[own_rows(m), :] = c_of(ybuf[m])

        @pl.when(t == span + 1)
        def _():
            for m in range(3):
                dev, far, near = sent(0, m)

                @pl.when(dev != me)
                def _():
                    far().start()

                @pl.when(dev == me)
                def _():
                    near().start()

        @pl.when(t == span + n_f)
        def _():
            for m in range(3):
                ybuf[m] = result(m, ybuf[m])
            for m in range(3):
                b, _ = owned(1, m)
                local(ybuf.at[m], out_ref.at[b], orecv.at[b]).start()
            for ch in range(2):
                for m in range(3):
                    dev, far, _ = sent(ch, m)

                    @pl.when(dev != me)
                    def _():
                        far().wait_send()

            for b in range(6):
                local(out_ref.at[b], out_ref.at[b], orecv.at[b]).wait()

        return

    for ch in range(2):

        @pl.when(t == ch * span + n_f)
        def _():
            for m in range(3):
                h = result(m, y_ref[ch, own_rows(m), :])
                y_ref[ch, own_rows(m), :] = h
                c_ref[own_rows(m), :] = norm_rows(h.astype(F32), gain(0, layer + 1)).astype(BF16)

        if ch == 1:
            @pl.when(t == span + n_f)
            def _():
                for m in range(3):
                    s = chunk_slot(0, m, special, row)
                    keys.wait_sent(s, (kst.at[m], vst.at[m]))
                    local(qst.at[m], q_ref.at[s], qsem.at[s]).wait()

        if ch == 0:
            @pl.when(t == 1)
            def _():
                wait_group(n_dev)

        def turn(m):
            r = slot_rows(chunk_slot(ch, m, special, row))
            return cos_ref[r, :], sin_ref[r, :]

        def heads(w_ref, put):
            for h in range(w_ref.shape[-1] // hd):
                raw = jnp.dot(c_ref[...], w_ref[0, :, h * hd : (h + 1) * hd], preferred_element_type=F32)
                for m in range(3):
                    put(h, m, raw[m * rows : (m + 1) * rows])

        u = t - (ch * span + n_f + 1)
        per = wk_ref.shape[-1] // hd

        @pl.when((u >= 0) & (u < n_k))
        def _():
            def put(h, m, raw):
                col = pl.ds(pl.multiple_of((u * per + h) * hd, hd), hd)
                kst[m, :, col] = norm_turn(raw, qk_ref[layer + 1, 1:2, :].astype(F32), *turn(m))

            heads(wk_ref, put)

        @pl.when((u >= n_k) & (u < 2 * n_k))
        def _():
            def put(h, m, raw):
                col = pl.ds(pl.multiple_of(((u - n_k) * per + h) * hd, hd), hd)
                vst[m, :, col] = raw.astype(BF16)

            heads(wv_ref, put)

        @pl.when((u >= 2 * n_k) & (u < 2 * n_k + n_q))
        def _():
            def put(h, m, raw):
                out = norm_turn(raw, qk_ref[layer + 1, 0:1, :].astype(F32), *turn(m))
                qst[m, (u - 2 * n_k) * per + h] = out * BF16(hd**-0.5)

            heads(wq_ref, put)

        @pl.when(u == 2 * n_k)
        def _():
            for m in range(3):
                s = chunk_slot(ch, m, special, row)
                keys.start(s, (kst.at[m], vst.at[m]))
                local(y_ref.at[ch, own_rows(m)], h_ref.at[s], hsem.at[s]).start()

        @pl.when(u == 2 * n_k + n_q - 1)
        def _():
            for m in range(3):
                s = chunk_slot(ch, m, special, row)
                local(qst.at[m], q_ref.at[s], qsem.at[s]).start()

    @pl.when(t == span - 1)
    def _():
        for m in range(3):
            c_ref[own_rows(m), :] = c_of(y_ref[1, own_rows(m), :])

    @pl.when(i == pl.num_programs(0) - 1)
    def _():
        for m in range(3):
            s = chunk_slot(1, m, special, row)
            keys.wait_sent(s, (kst.at[m], vst.at[m]))
            local(qst.at[m], q_ref.at[s], qsem.at[s]).wait()
        for s in range(6):
            local(y_ref.at[0, own_rows(0)], h_ref.at[s], hsem.at[s]).wait()
        keys.wait_all(6)


def after_attention(layer, last, n_dev, cid, o, x, ln_w, w_o, w_gate, w_up, w_down, more=()):
    slots, rows, dim = x.shape
    inner, ff = w_o.shape[1], w_gate.shape[-1]
    total = slots * rows
    half = total // 2
    blocks = 16
    tn, tf = min(256, dim), min(512, ff)
    n_o, n_f = dim // tn, ff // tf
    o2, x2 = o.reshape(total, inner), x.reshape(total, dim)
    n_k = n_q = 0
    if not last:
        qk_w, cos, sin, w_q, w_k, w_v = more
        hd = qk_w.shape[-1]
        wide = 2 * hd
        n_k, n_q = w_k.shape[-1] // wide, w_q.shape[-1] // wide
    span = n_f + 1 + 2 * n_k + n_q
    one = lambda a: pl.BlockSpec(a.shape, lambda i: (0,) * a.ndim, pipeline_mode=pl.Buffered(1))

    def at_f(i):
        t = jnp.clip(i - n_o, 0, 2 * span - 1)
        return jnp.minimum(t % span, n_f - 1)

    def next_w(lo, n):
        return lambda i: (layer + 1, 0, jnp.clip(jnp.clip(i - n_o, 0, 2 * span - 1) % span - (n_f + 1 + lo), 0, n - 1))

    mlp_specs = [
        pl.BlockSpec((1, inner, tn), lambda i: (layer, 0, jnp.minimum(i, n_o - 1))),
        pl.BlockSpec((1, dim, tf), lambda i: (layer, 0, at_f(i))),
        pl.BlockSpec((1, dim, tf), lambda i: (layer, 0, at_f(i))),
        pl.BlockSpec((1, tf, dim), lambda i: (layer, at_f(i - 1), 0)),
    ]
    work = [
        pltpu.VMEM((total, dim), BF16), pltpu.VMEM((2, half, dim), BF16), pltpu.VMEM((half, dim), BF16),
        pltpu.VMEM((half, dim), F32), pltpu.VMEM((2, half, tf), BF16),
    ]
    params = pltpu.CompilerParams(
        dimension_semantics=("arbitrary",), collective_id=cid, has_side_effects=True, vmem_limit_bytes=VMEM_LIMIT
    )
    body = functools.partial(layer_kernel, layer, last, n_dev, n_o, n_f, n_k, n_q)
    if last:
        return pl.pallas_call(
            body, grid=(n_o + 2 * span,),
            in_specs=[one(o2), one(x2), one(ln_w)] + mlp_specs,
            out_specs=ANY,
            out_shape=jax.ShapeDtypeStruct(x.shape, BF16),
            scratch_shapes=work + [pltpu.VMEM((3, rows, dim), BF16), DMA((3,)), DMA((3,)), DMA((3,)), DMA((slots,))],
            compiler_params=params,
        )(o2, x2, ln_w, w_o, w_gate, w_up, w_down)
    nq, nk = w_q.shape[-1] // hd, w_k.shape[-1] // hd
    q_shape, kv_shape = (slots, nq, rows, hd), (blocks, rows, nk * hd)
    return pl.pallas_call(
        body, grid=(n_o + 2 * span,),
        in_specs=[one(o2), one(x2), one(ln_w), one(qk_w), one(cos), one(sin)] + mlp_specs + [
            pl.BlockSpec((1, dim, wide), next_w(0, n_k)),
            pl.BlockSpec((1, dim, wide), next_w(n_k, n_k)),
            pl.BlockSpec((1, dim, wide), next_w(2 * n_k, n_q)),
        ],
        out_specs=[ANY] * 4,
        out_shape=[jax.ShapeDtypeStruct(a, BF16) for a in (x.shape, q_shape, kv_shape, kv_shape)],
        scratch_shapes=work + [
            pltpu.VMEM((3, nq, rows, hd), BF16), pltpu.VMEM((3, rows, nk * hd), BF16), pltpu.VMEM((3, rows, nk * hd), BF16),
            DMA((slots,)), DMA((slots,)), DMA((2, 3, slots)), DMA((2, blocks)), DMA((2, 2)),
        ],
        compiler_params=params,
    )(o2, x2, ln_w, qk_w, cos, sin, w_o, w_gate, w_up, w_down, w_k, w_v, w_q)


def rope_tables(pos, hd):
    half = hd // 2
    out = []
    for base, scale in ((LOCAL_BASE, 1.0), (GLOBAL_BASE, GLOBAL_SCALE)):
        freq = base ** (-2.0 * jnp.arange(half, dtype=jnp.float32) / hd)
        ang = (pos.astype(jnp.float32) / scale)[:, None] * freq[None, :]
        out += [jnp.cos(ang), jnp.sin(ang)]
    return out


def solution(mesh):
    n_dev = mesh.shape["cp"]

    def device_fn(x_loc, ln_w, qk_w, w_q, w_k, w_v, w_o, w_gate, w_up, w_down):
        slots, rows, dim = x_loc.shape
        _, _, core, special, row = placement()
        blk = jnp.stack([slot_place(s, core, special, row)[1] for s in range(slots)])
        pos = (blk[:, None] * rows + jnp.arange(rows)[None, :]).reshape(-1)
        cos0, sin0, cos1, sin1 = rope_tables(pos, qk_w.shape[-1])
        x, q, k, v = first(n_dev, x_loc, ln_w, qk_w, cos0, sin0, w_q, w_k, w_v)
        o = attention(WINDOW, q, k, v)
        mlp = (w_o, w_gate, w_up, w_down)
        x, q, k, v = after_attention(0, False, n_dev, 1, o, x, ln_w, *mlp, more=(qk_w, cos1, sin1, w_q, w_k, w_v))
        o = attention(None, q, k, v)
        return after_attention(1, True, n_dev, 2, o, x, ln_w, *mlp)

    act_part = P("dp", "cp", None)
    return jax.shard_map(device_fn, mesh=mesh, in_specs=(act_part,) + (P(),) * 9, out_specs=act_part, check_vma=False)
```

time: 1740 us -> 541 us (0.31)
  the two profiles are of different devices: /device:TPU:21 before, /device:TPU:54 now
where the time goes in v3:
time: 541 us; the launch traced here: 533 us
  Pallas kernels  524 us (97%)
    pallas_call x2, Pallas kernels, after_attention(): pl.pallas_call(body, grid=(n_o + 2 * span,), in_specs=[one(o2), one(x2),...  350 us
    pallas_call x1, Pallas kernels, first(): pl.pallas_call(functools.partial(first_kernel, n_dev, nq, nk), out_shape=...  122 us
    pallas_call x2, Pallas kernels, attention(): pl.pallas_call(functools.partial(attn_kernel, None if window is None else...  51.6 us

profile of v3, /device:TPU:54, one launch (start us, length us, event | category | flops | bytes accessed | tf_op | source)
XLA Modules:
  0.0 533.5 jit_solution(10665829951202453758)
XLA Ops:
  0.0 0.1 stack.27
  0.1 0.1 broadcast_multiply_fusion
  0.2 0.1 convert_bitcast_fusion
  0.3 2.5 multiply_sine_fusion.1
  2.7 2.5 multiply_sine_fusion
  5.2 122.1 %shard_map.100 = (bf16[6,128,2304]{2,1,0:T(8,128)(2,1)}, bf16[6,8,128,256]{3,2,1,0:T(8,128)(2,1)}, bf16[16,128,1024]{2,1,0:T(8,128)(2,1)}, bf16[16,128,1024]{2,1,0:T(8,128)(2,1)}) custom-call(bf16[6,128,2304]{2,1,0:T(8,128)(2,1)} %x_ref.1, bf16[2,4,2304]{2,1,0:T(4,128)(2,1)} %refs_2_.3, bf16[2,2,256]{2,1,0:T(2,128)(2,1)} %refs_3_.2, ...), custom_call_target="tpu_custom_call" | custom-call | tf_op jit(solution)/shard_map/pallas_call | solution.py:279
  127.3 24.8 %shard_map.101 = bf16[6,128,2048]{2,1,0:T(8,128)(2,1)} custom-call(bf16[6,8,128,256]{3,2,1,0:T(8,128)(2,1)} %get-tuple-element.13.q_ref, bf16[16,128,1024]{2,1,0:T(8,128)(2,1)} %get-tuple-element.14.k_ref, bf16[16,128,1024]{2,1,0:T(8,128)(2,1)} %get-tuple-element.15.v_ref), custom_call_target="tpu_custom_call" | custom-call | tf_op jit(solution)/shard_map/pallas_call | solution.py:407
  152.1 203.8 %shard_map.102 = (bf16[6,128,2304]{2,1,0:T(8,128)(2,1)}, bf16[6,8,128,256]{3,2,1,0:T(8,128)(2,1)}, bf16[16,128,1024]{2,1,0:T(8,128)(2,1)}, bf16[16,128,1024]{2,1,0:T(8,128)(2,1)}) custom-call(bf16[768,2048]{1,0:T(8,128)(2,1)} %bitcast.14, bf16[768,2304]{1,0:T(8,128)(2,1)} %bitcast.16, bf16[2,4,2304]{2,1,0:T(4,128)(2,1)} %refs_2_.3, ...), custom_call_target="tpu_custom_call" | custom-call | tf_op jit(solution)/shard_map/pallas_call | solution.py:725
  356.0 26.8 %shard_map.103 = bf16[6,128,2048]{2,1,0:T(8,128)(2,1)} custom-call(bf16[6,8,128,256]{3,2,1,0:T(8,128)(2,1)} %get-tuple-element.17.q_ref, bf16[16,128,1024]{2,1,0:T(8,128)(2,1)} %get-tuple-element.18.k_ref, bf16[16,128,1024]{2,1,0:T(8,128)(2,1)} %get-tuple-element.19.v_ref), custom_call_target="tpu_custom_call" | custom-call | tf_op jit(solution)/shard_map/pallas_call | solution.py:407
  382.7 146.5 %shard_map.104 = bf16[6,128,2304]{2,1,0:T(8,128)(2,1)} custom-call(bf16[768,2048]{1,0:T(8,128)(2,1)} %bitcast.15, bf16[768,2304]{1,0:T(8,128)(2,1)} %bitcast.17, bf16[2,4,2304]{2,1,0:T(4,128)(2,1)} %refs_2_.3, bf16[2,2048,2304]{2,1,0:T(8,128)(2,1)} %refs_3_.3, bf16[2,2304,9216]{2,1,0:T(8,128)(2,1)} %refs_4_.1, bf16[2,2304,9216]{2,1,0:T(8,128)(2,1)} %refs_5_.1, ...), custom_call_target="tpu_custom_call" | custom-call | tf_op jit(solution)/shard_map/pallas_call | solution.py:715
  529.3 4.0 copy.12
  (3 shorter events, 0.0 us)

commit v4 on v3

--- a/solution.py
+++ b/solution.py
@@ -117,10 +117,12 @@
 
 class KeyValues:
     def __init__(self, k_all, v_all, send, recv, fwd):
-        self.me, chip, self.core, self.special, self.row = placement()
-        self.mate = chip * 2 + 1 - self.core
         self.both = ((0, k_all), (1, v_all))
         self.send, self.recv, self.fwd = send, recv, fwd
+
+    def here(self):
+        _, chip, self.core, self.special, self.row = placement()
+        self.mate = chip * 2 + 1 - self.core
 
     def _copies(self, s, stage):
         idx = kv_index(s, self.core, self.special, self.row)
@@ -138,6 +140,7 @@
         return out
 
     def start(self, s, stage):
+        self.here()
         for own, mate, row in self._copies(s, stage):
 
             @pl.when(self.special == 1)
@@ -148,6 +151,7 @@
             own.start()
 
     def wait_sent(self, s, stage):
+        self.here()
         for own, mate, row in self._copies(s, stage):
             own.wait()
             mate.wait_send()
@@ -157,6 +161,7 @@
                 row.wait_send()
 
     def wait_all(self, slots):
+        self.here()
         for x, full in self.both:
 
             @pl.when(self.special == 0)
@@ -243,15 +248,17 @@
         if pair == 0:
             local(wq_ref.at[0], wq, wsem.at[2]).wait()
 
-        @pl.loop(0, nq)
-        def _(h):
+        def query(h):
             raw = product(wq, h)
             for j, s in enumerate(places):
                 part = slice(j * rows, (j + 1) * rows)
                 qst[s, h] = norm_turn(raw[part], q_gain, *turn[j]) * BF16(hd**-0.5)
 
+        query(0)
         for s in places:
             keys.start(s, (kst.at[s], vst.at[s]))
+        pl.loop(1, nq)(query)
+        for s in places:
             local(qst.at[s], q_ref.at[s], qsem.at[s]).start()
 
     for s in range(n):
@@ -431,13 +438,20 @@
          att, y_ref, c_ref, acc, act, qst, kst, vst, hsem, qsem, ksend, krecv, fsem) = refs
         keys = KeyValues(k_all, v_all, ksend, krecv, fsem)
         hd = qk_ref.shape[-1]
-    me, chip, core, special, row = placement()
     i = pl.program_id(0)
     half = y_ref.shape[1]
     rows = half // 3
     tn = wo_ref.shape[-1]
     span = n_f + 1 + n_k + n_k + n_q
 
+    def slot_of(ch, m):
+        _, _, _, special, row = placement()
+        return chunk_slot(ch, m, special, row)
+
+    def place_of(ch, m):
+        _, _, core, special, row = placement()
+        return slot_place(chunk_slot(ch, m, special, row), core, special, row)
+
     def slot_rows(s):
         return pl.ds(pl.multiple_of(s * rows, rows), rows)
 
@@ -463,7 +477,7 @@
     def _():
         for ch in range(2):
             for m in range(3):
-                r = slot_rows(chunk_slot(ch, m, special, row))
+                r = slot_rows(slot_of(ch, m))
                 y = x_ref[r, :].astype(F32) + norm_rows(att[r, :].astype(F32), gain(1))
                 y = y.astype(BF16)
                 y_ref[ch, own_rows(m), :] = y
@@ -480,7 +494,7 @@
     def down(slot):
         return jnp.dot(act[slot], wd_ref[0], preferred_element_type=F32)
 
-    j = t % span
+    j = jnp.where(t >= span, t - span, t)
 
     @pl.when((t >= 0) & (j == 0))
     def _():
@@ -493,7 +507,7 @@
 
     for parity in range(2):
 
-        @pl.when((t >= 0) & (j > 1) & (j < n_f) & (j % 2 == parity))
+        @pl.when((t >= 0) & (j > 1) & (j < n_f) & ((j & 1) == parity))
         def _():
             acc[...] += down(1 - parity)
             up(parity)
@@ -508,7 +522,7 @@
 
     if last:
         def sent(ch, m):
-            b, blk = slot_place(chunk_slot(ch, m, special, row), core, special, row)
+            b, blk = place_of(ch, m)
             src = y_ref.at[ch, own_rows(m)]
             if ch == 0:
                 far = lambda: remote(src, out_ref.at[b], osend.at[m], orecv.at[b], blk)
@@ -516,6 +530,7 @@
             return blk, lambda: remote(src, ybuf.at[b // 2], ysend.at[m], yrecv.at[b // 2], blk), None
 
         def owned(ch, m):
+            me = lax.axis_index("cp")
             turn = (me // 2) % 2
             b = 2 * m + (turn if ch == 0 else 1 - turn)
             return b, home_of(b, me)[0]
@@ -523,6 +538,7 @@
         @pl.when(t == 1)
         def _():
             wait_group(n_dev)
+            me = lax.axis_index("cp")
             for m in range(3):
                 dev, far, _ = sent(1, m)
 
@@ -532,6 +548,7 @@
 
         @pl.when(t == n_f)
         def _():
+            me = lax.axis_index("cp")
             for m in range(3):
                 y_ref[0, own_rows(m), :] = result(m, y_ref[0, own_rows(m), :])
             for m in range(3):
@@ -542,7 +559,7 @@
                     remote(ybuf.at[m], ybuf.at[m], ysend.at[m], yrecv.at[m], me).wait_recv()
 
             for m in range(3):
-                b, blk = slot_place(chunk_slot(1, m, special, row), core, special, row)
+                b, blk = place_of(1, m)
 
                 @pl.when(blk == me)
                 def _():
@@ -553,6 +570,7 @@
 
         @pl.when(t == span + 1)
         def _():
+            me = lax.axis_index("cp")
             for m in range(3):
                 dev, far, near = sent(0, m)
 
@@ -566,6 +584,7 @@
 
         @pl.when(t == span + n_f)
         def _():
+            me = lax.axis_index("cp")
             for m in range(3):
                 ybuf[m] = result(m, ybuf[m])
             for m in range(3):
@@ -597,17 +616,12 @@
             @pl.when(t == span + n_f)
             def _():
                 for m in range(3):
-                    s = chunk_slot(0, m, special, row)
+                    s = slot_of(0, m)
                     keys.wait_sent(s, (kst.at[m], vst.at[m]))
                     local(qst.at[m], q_ref.at[s], qsem.at[s]).wait()
 
-        if ch == 0:
-            @pl.when(t == 1)
-            def _():
-                wait_group(n_dev)
-
         def turn(m):
-            r = slot_rows(chunk_slot(ch, m, special, row))
+            r = slot_rows(slot_of(ch, m))
             return cos_ref[r, :], sin_ref[r, :]
 
         def heads(w_ref, put):
@@ -645,15 +659,17 @@
 
         @pl.when(u == 2 * n_k)
         def _():
-            for m in range(3):
-                s = chunk_slot(ch, m, special, row)
+            if ch == 0:
+                wait_group(n_dev)
+            for m in range(3):
+                s = slot_of(ch, m)
                 keys.start(s, (kst.at[m], vst.at[m]))
                 local(y_ref.at[ch, own_rows(m)], h_ref.at[s], hsem.at[s]).start()
 
         @pl.when(u == 2 * n_k + n_q - 1)
         def _():
             for m in range(3):
-                s = chunk_slot(ch, m, special, row)
+                s = slot_of(ch, m)
                 local(qst.at[m], q_ref.at[s], qsem.at[s]).start()
 
     @pl.when(t == span - 1)
@@ -664,7 +680,7 @@
     @pl.when(i == pl.num_programs(0) - 1)
     def _():
         for m in range(3):
-            s = chunk_slot(1, m, special, row)
+            s = slot_of(1, m)
             keys.wait_sent(s, (kst.at[m], vst.at[m]))
             local(qst.at[m], q_ref.at[s], qsem.at[s]).wait()
         for s in range(6):
@@ -678,7 +694,7 @@
     total = slots * rows
     half = total // 2
     blocks = 16
-    tn, tf = min(256, dim), min(512, ff)
+    tn, tf = min(256, dim), min(768 if last and ff % 768 == 0 else 512, ff)
     n_o, n_f = dim // tn, ff // tf
     o2, x2 = o.reshape(total, inner), x.reshape(total, dim)
     n_k = n_q = 0
@@ -690,12 +706,15 @@
     span = n_f + 1 + 2 * n_k + n_q
     one = lambda a: pl.BlockSpec(a.shape, lambda i: (0,) * a.ndim, pipeline_mode=pl.Buffered(1))
 
+    def at_step(i):
+        t = i - n_o
+        return jnp.where(t >= span, t - span, t)
+
     def at_f(i):
-        t = jnp.clip(i - n_o, 0, 2 * span - 1)
-        return jnp.minimum(t % span, n_f - 1)
+        return jnp.clip(at_step(i), 0, n_f - 1)
 
     def next_w(lo, n):
-        return lambda i: (layer + 1, 0, jnp.clip(jnp.clip(i - n_o, 0, 2 * span - 1) % span - (n_f + 1 + lo), 0, n - 1))
+        return lambda i: (layer + 1, 0, jnp.clip(at_step(i) - (n_f + 1 + lo), 0, n - 1))
 
     mlp_specs = [
         pl.BlockSpec((1, inner, tn), lambda i: (layer, 0, jnp.minimum(i, n_o - 1))),

time: 541 us -> 539 us (level)
  the two profiles are of different devices: /device:TPU:54 before, /device:TPU:61 now
where the time goes in v4:
time: 539 us; the launch traced here: 531 us
  Pallas kernels  521 us (97%)
    pallas_call x2, Pallas kernels, after_attention(): pl.pallas_call(body, grid=(n_o + 2 * span,), in_specs=[one(o2), one(x2),...  351 us
    pallas_call x1, Pallas kernels, first(): pl.pallas_call(functools.partial(first_kernel, n_dev, nq, nk), out_shape=...  118 us
    pallas_call x2, Pallas kernels, attention(): pl.pallas_call(functools.partial(attn_kernel, None if window is None else...  51.6 us

profile of v4, /device:TPU:61, one launch (start us, length us, event | category | flops | bytes accessed | tf_op | source)
XLA Modules:
  0.0 530.5 jit_solution(6214353842337254105)
XLA Ops:
  0.0 0.1 stack.27
  0.1 0.1 broadcast_multiply_fusion
  0.2 0.1 convert_bitcast_fusion
  0.3 2.5 multiply_sine_fusion.1
  2.7 2.5 multiply_sine_fusion
  5.2 118.3 %shard_map.100 = (bf16[6,128,2304]{2,1,0:T(8,128)(2,1)}, bf16[6,8,128,256]{3,2,1,0:T(8,128)(2,1)}, bf16[16,128,1024]{2,1,0:T(8,128)(2,1)}, bf16[16,128,1024]{2,1,0:T(8,128)(2,1)}) custom-call(bf16[6,128,2304]{2,1,0:T(8,128)(2,1)} %x_ref.1, bf16[2,4,2304]{2,1,0:T(4,128)(2,1)} %refs_2_.3, bf16[2,2,256]{2,1,0:T(2,128)(2,1)} %refs_3_.2, ...), custom_call_target="tpu_custom_call" | custom-call | tf_op jit(solution)/shard_map/pallas_call | solution.py:286
  123.5 24.8 %shard_map.101 = bf16[6,128,2048]{2,1,0:T(8,128)(2,1)} custom-call(bf16[6,8,128,256]{3,2,1,0:T(8,128)(2,1)} %get-tuple-element.13.q_ref, bf16[16,128,1024]{2,1,0:T(8,128)(2,1)} %get-tuple-element.14.k_ref, bf16[16,128,1024]{2,1,0:T(8,128)(2,1)} %get-tuple-element.15.v_ref), custom_call_target="tpu_custom_call" | custom-call | tf_op jit(solution)/shard_map/pallas_call | solution.py:414
  148.3 204.7 %shard_map.102 = (bf16[6,128,2304]{2,1,0:T(8,128)(2,1)}, bf16[6,8,128,256]{3,2,1,0:T(8,128)(2,1)}, bf16[16,128,1024]{2,1,0:T(8,128)(2,1)}, bf16[16,128,1024]{2,1,0:T(8,128)(2,1)}) custom-call(bf16[768,2048]{1,0:T(8,128)(2,1)} %bitcast.14, bf16[768,2304]{1,0:T(8,128)(2,1)} %bitcast.16, bf16[2,4,2304]{2,1,0:T(4,128)(2,1)} %refs_2_.3, ...), custom_call_target="tpu_custom_call" | custom-call | tf_op jit(solution)/shard_map/pallas_call | solution.py:744
  353.0 26.8 %shard_map.103 = bf16[6,128,2048]{2,1,0:T(8,128)(2,1)} custom-call(bf16[6,8,128,256]{3,2,1,0:T(8,128)(2,1)} %get-tuple-element.17.q_ref, bf16[16,128,1024]{2,1,0:T(8,128)(2,1)} %get-tuple-element.18.k_ref, bf16[16,128,1024]{2,1,0:T(8,128)(2,1)} %get-tuple-element.19.v_ref), custom_call_target="tpu_custom_call" | custom-call | tf_op jit(solution)/shard_map/pallas_call | solution.py:414
  379.8 146.5 %shard_map.104 = bf16[6,128,2304]{2,1,0:T(8,128)(2,1)} custom-call(bf16[768,2048]{1,0:T(8,128)(2,1)} %bitcast.15, bf16[768,2304]{1,0:T(8,128)(2,1)} %bitcast.17, bf16[2,4,2304]{2,1,0:T(4,128)(2,1)} %refs_2_.3, bf16[2,2048,2304]{2,1,0:T(8,128)(2,1)} %refs_3_.3, bf16[2,2304,9216]{2,1,0:T(8,128)(2,1)} %refs_4_.1, bf16[2,2304,9216]{2,1,0:T(8,128)(2,1)} %refs_5_.1, ...), custom_call_target="tpu_custom_call" | custom-call | tf_op jit(solution)/shard_map/pallas_call | solution.py:734
  526.3 4.0 copy.12
  (3 shorter events, 0.0 us)

commit v5 on v4

--- a/solution.py
+++ b/solution.py
@@ -428,21 +428,72 @@
     )(q, k, v)
 
 
-def layer_kernel(layer, last, n_dev, n_o, n_f, n_k, n_q, *refs):
+class Ring:
+    def __init__(self, buf, sem, count, source):
+        self.buf, self.sem, self.count, self.source = buf, sem, count, source
+        self.depth = buf.shape[0]
+
+    def begin(self):
+        for t in range(min(self.depth, self.count)):
+            self.start(t, t)
+
+    def start(self, t, slot):
+        self.source(t, lambda ref: local(ref, self.buf.at[slot], self.sem.at[slot]).start())
+
+    def get(self, t):
+        slot = lax.rem(t, self.depth) if not isinstance(t, int) else t % self.depth
+        local(self.buf.at[slot], self.buf.at[slot], self.sem.at[slot]).wait()
+        return self.buf.at[slot]
+
+    def free(self, t):
+        new = t + self.depth
+        if isinstance(t, int):
+            if new < self.count:
+                self.start(new, t % self.depth)
+            return
+
+        @pl.when(new < self.count)
+        def _():
+            self.start(new, lax.rem(t, self.depth))
+
+
+def layer_kernel(layer, last, n_dev, *refs):
     if last:
         (o_ref, x_ref, ln_ref, wo_ref, wg_ref, wu_ref, wd_ref, out_ref,
-         att, y_ref, c_ref, acc, act, ybuf, ysend, yrecv, osend, orecv) = refs
+         obuf, y_ref, att, c_ref, acc, act, wo, wg, wu, wd, isem, osem, gsem, usem, dsem,
+         ybuf, ysend, yrecv, osend, orecv) = refs
     else:
         (o_ref, x_ref, ln_ref, qk_ref, cos_ref, sin_ref, wo_ref, wg_ref, wu_ref, wd_ref, wk_ref, wv_ref, wq_ref,
          h_ref, q_ref, k_all, v_all,
-         att, y_ref, c_ref, acc, act, qst, kst, vst, hsem, qsem, ksend, krecv, fsem) = refs
+         obuf, y_ref, att, c_ref, acc, act, wo, wg, wu, wd, isem, osem, gsem, usem, dsem,
+         wn, nsem, qst, kst, vst, hsem, qsem, ksend, krecv, fsem) = refs
         keys = KeyValues(k_all, v_all, ksend, krecv, fsem)
         hd = qk_ref.shape[-1]
-    i = pl.program_id(0)
-    half = y_ref.shape[1]
-    rows = half // 3
-    tn = wo_ref.shape[-1]
-    span = n_f + 1 + n_k + n_k + n_q
+        nk, nq = wk_ref.shape[-1] // hd, wq_ref.shape[-1] // hd
+    rows = acc.shape[0] // 3
+    tn, tf = wo.shape[-1], wg.shape[-1]
+    n_o, n_f = wo_ref.shape[-1] // tn, wg_ref.shape[-1] // tf
+
+    def cols(t, width):
+        start = t * width
+        return pl.ds(start if isinstance(t, int) else pl.multiple_of(start, width), width)
+
+    def tile_f(t):
+        return (t % n_f) if isinstance(t, int) else lax.rem(t, n_f)
+
+    o_ring = Ring(wo, osem, n_o, lambda t, put: put(wo_ref.at[layer, :, cols(t, tn)]))
+    g_ring = Ring(wg, gsem, 2 * n_f, lambda t, put: put(wg_ref.at[layer, :, cols(tile_f(t), tf)]))
+    u_ring = Ring(wu, usem, 2 * n_f, lambda t, put: put(wu_ref.at[layer, :, cols(tile_f(t), tf)]))
+    d_ring = Ring(wd, dsem, 2 * n_f, lambda t, put: put(wd_ref.at[layer, cols(tile_f(t), tf), :]))
+
+    in_o = local(o_ref, obuf, isem.at[0])
+    in_x = local(x_ref, y_ref, isem.at[1])
+    in_o.start()
+    o_ring.begin()
+    in_x.start()
+    for r in (g_ring, u_ring, d_ring):
+        r.begin()
+    signal_group(n_dev)
 
     def slot_of(ch, m):
         _, _, _, special, row = placement()
@@ -458,87 +509,80 @@
     def own_rows(m):
         return pl.ds(m * rows, rows)
 
+    def y_at(ch, m):
+        return y_ref.at[slot_rows(slot_of(ch, m))]
+
     def gain(which, l=layer):
         return ln_ref[l, which : which + 1, :].astype(F32)
 
     def c_of(y):
         return norm_rows(y.astype(F32), gain(2)).astype(BF16)
 
-    @pl.when(i == 0)
-    def _():
-        signal_group(n_dev)
-
-    @pl.when(i < n_o)
-    def _():
-        part = jnp.dot(o_ref[...], wo_ref[0], preferred_element_type=F32).astype(BF16)
-        att[:, pl.ds(pl.multiple_of(i * tn, tn), tn)] = part
-
-    @pl.when(i == n_o - 1)
-    def _():
-        for ch in range(2):
-            for m in range(3):
-                r = slot_rows(slot_of(ch, m))
-                y = x_ref[r, :].astype(F32) + norm_rows(att[r, :].astype(F32), gain(1))
-                y = y.astype(BF16)
-                y_ref[ch, own_rows(m), :] = y
-                if ch == 0:
-                    c_ref[own_rows(m), :] = c_of(y)
-
-    t = i - n_o
-
-    def up(slot):
-        gate = jnp.dot(c_ref[...], wg_ref[0], preferred_element_type=F32)
-        val = jnp.dot(c_ref[...], wu_ref[0], preferred_element_type=F32)
-        act[slot] = (jax.nn.gelu(gate, approximate=True) * val).astype(BF16)
-
-    def down(slot):
-        return jnp.dot(act[slot], wd_ref[0], preferred_element_type=F32)
-
-    j = jnp.where(t >= span, t - span, t)
-
-    @pl.when((t >= 0) & (j == 0))
-    def _():
-        up(0)
-
-    @pl.when((t >= 0) & (j == 1))
-    def _():
-        acc[...] = down(0)
-        up(1)
-
-    for parity in range(2):
-
-        @pl.when((t >= 0) & (j > 1) & (j < n_f) & ((j & 1) == parity))
-        def _():
-            acc[...] += down(1 - parity)
-            up(parity)
-
-    @pl.when((t >= 0) & (j == n_f))
-    def _():
-        acc[...] += down((n_f - 1) % 2)
+    in_o.wait()
+
+    @pl.loop(0, n_o)
+    def _(t):
+        tile = o_ring.get(t)
+        att[:, cols(t, tn)] = jnp.dot(obuf[...], tile[...], preferred_element_type=F32).astype(BF16)
+        o_ring.free(t)
+
+    in_x.wait()
+    for ch in range(2):
+        for m in range(3):
+            r = slot_rows(slot_of(ch, m))
+            y = y_ref[r, :].astype(F32) + norm_rows(att[r, :].astype(F32), gain(1))
+            y = y.astype(BF16)
+            y_ref[r, :] = y
+            if ch == 0 or not last:
+                c_ref[ch, own_rows(m), :] = c_of(y)
+
+    def up(ch, t, to):
+        gate = jnp.dot(c_ref[ch], g_ring.get(t)[...], preferred_element_type=F32)
+        val = jnp.dot(c_ref[ch], u_ring.get(t)[...], preferred_element_type=F32)
+        act[to] = (jax.nn.gelu(gate, approximate=True) * val).astype(BF16)
+        g_ring.free(t)
+        u_ring.free(t)
+
+    def down(t, at):
+        acc[...] += jnp.dot(act[at], d_ring.get(t)[...], preferred_element_type=F32)
+        d_ring.free(t)
+
+    def mlp(ch, after_first):
+        base = ch * n_f
+        acc[...] = jnp.zeros(acc.shape, F32)
+        up(ch, base, 0)
+        after_first()
+
+        @pl.loop(1, n_f)
+        def _(t):
+            even = lax.rem(t, 2)
+            down(base + t - 1, 1 - even)
+            up(ch, base + t, even)
+
+        down(base + n_f - 1, (n_f - 1) % 2)
 
     def result(m, y):
         val = acc[own_rows(m), :].astype(BF16).astype(F32)
         return (y.astype(F32) + norm_rows(val, gain(3))).astype(BF16)
 
     if last:
+        me = lax.axis_index("cp")
+
         def sent(ch, m):
             b, blk = place_of(ch, m)
-            src = y_ref.at[ch, own_rows(m)]
+            src = y_at(ch, m)
             if ch == 0:
                 far = lambda: remote(src, out_ref.at[b], osend.at[m], orecv.at[b], blk)
                 return blk, far, lambda: local(src, out_ref.at[b], orecv.at[b])
             return blk, lambda: remote(src, ybuf.at[b // 2], ysend.at[m], yrecv.at[b // 2], blk), None
 
         def owned(ch, m):
-            me = lax.axis_index("cp")
             turn = (me // 2) % 2
             b = 2 * m + (turn if ch == 0 else 1 - turn)
             return b, home_of(b, me)[0]
 
-        @pl.when(t == 1)
-        def _():
+        def send_streams():
             wait_group(n_dev)
-            me = lax.axis_index("cp")
             for m in range(3):
                 dev, far, _ = sent(1, m)
 
@@ -546,31 +590,7 @@
                 def _():
                     far().start()
 
-        @pl.when(t == n_f)
-        def _():
-            me = lax.axis_index("cp")
-            for m in range(3):
-                y_ref[0, own_rows(m), :] = result(m, y_ref[0, own_rows(m), :])
-            for m in range(3):
-                b, dev = owned(1, m)
-
-                @pl.when(dev != me)
-                def _():
-                    remote(ybuf.at[m], ybuf.at[m], ysend.at[m], yrecv.at[m], me).wait_recv()
-
-            for m in range(3):
-                b, blk = place_of(1, m)
-
-                @pl.when(blk == me)
-                def _():
-                    ybuf[b // 2] = y_ref[1, own_rows(m), :]
-
-            for m in range(3):
-                c_ref[own_rows(m), :] = c_of(ybuf[m])
-
-        @pl.when(t == span + 1)
-        def _():
-            me = lax.axis_index("cp")
+        def send_results():
             for m in range(3):
                 dev, far, near = sent(0, m)
 
@@ -582,110 +602,123 @@
                 def _():
                     near().start()
 
-        @pl.when(t == span + n_f)
-        def _():
-            me = lax.axis_index("cp")
+        mlp(0, send_streams)
+        for m in range(3):
+            y_at(0, m)[...] = result(m, y_at(0, m)[...])
+        for m in range(3):
+            b, dev = owned(1, m)
+
+            @pl.when(dev != me)
+            def _():
+                remote(ybuf.at[m], ybuf.at[m], ysend.at[m], yrecv.at[m], me).wait_recv()
+
+        for m in range(3):
+            b, blk = place_of(1, m)
+
+            @pl.when(blk == me)
+            def _():
+                ybuf[b // 2] = y_at(1, m)[...]
+
+        for m in range(3):
+            c_ref[1, own_rows(m), :] = c_of(ybuf[m])
+        mlp(1, send_results)
+        for m in range(3):
+            ybuf[m] = result(m, ybuf[m])
+        for m in range(3):
+            b, _ = owned(1, m)
+            local(ybuf.at[m], out_ref.at[b], orecv.at[b]).start()
+        for ch in range(2):
             for m in range(3):
-                ybuf[m] = result(m, ybuf[m])
+                dev, far, _ = sent(ch, m)
+
+                @pl.when(dev != me)
+                def _():
+                    far().wait_send()
+
+        for b in range(6):
+            local(out_ref.at[b], out_ref.at[b], orecv.at[b]).wait()
+        return
+
+    def source(t, put):
+        kind = lax.rem(t, 2 * nk) if not isinstance(t, int) else t % (2 * nk)
+        cases = (
+            (jnp.logical_and(t < 4 * nk, kind < nk), lambda: put(wk_ref.at[layer + 1, :, cols(kind, hd)])),
+            (jnp.logical_and(t < 4 * nk, kind >= nk), lambda: put(wv_ref.at[layer + 1, :, cols(kind - nk, hd)])),
+            (t >= 4 * nk, lambda: put(wq_ref.at[layer + 1, :, cols(t - 4 * nk, hd)])),
+        )
+        for cond, do in cases:
+            pl.when(cond)(do)
+
+    n_ring = Ring(wn, nsem, 4 * nk + nq, source)
+    n_ring.begin()
+    k_gain, q_gain = (qk_ref[layer + 1, j : j + 1, :].astype(F32) for j in (1, 0))
+
+    def turn(ch, m):
+        r = slot_rows(slot_of(ch, m))
+        return cos_ref[r, :], sin_ref[r, :]
+
+    def send_keys(ch):
+        for m in range(3):
+            keys.start(slot_of(ch, m), (kst.at[ch, m], vst.at[ch, m]))
+
+    def keys_and_values(ch):
+        for m in range(3):
+            h = result(m, y_at(ch, m)[...])
+            y_at(ch, m)[...] = h
+            c_ref[ch, own_rows(m), :] = norm_rows(h.astype(F32), gain(0, layer + 1)).astype(BF16)
+
+        @pl.loop(0, nk)
+        def _(h):
+            t = ch * 2 * nk + h
+            raw = jnp.dot(c_ref[ch], n_ring.get(t)[...], preferred_element_type=F32)
+            n_ring.free(t)
             for m in range(3):
-                b, _ = owned(1, m)
-                local(ybuf.at[m], out_ref.at[b], orecv.at[b]).start()
-            for ch in range(2):
-                for m in range(3):
-                    dev, far, _ = sent(ch, m)
-
-                    @pl.when(dev != me)
-                    def _():
-                        far().wait_send()
-
-            for b in range(6):
-                local(out_ref.at[b], out_ref.at[b], orecv.at[b]).wait()
-
-        return
-
+                kst[ch, m, :, cols(h, hd)] = norm_turn(raw[m * rows : (m + 1) * rows], k_gain, *turn(ch, m))
+
+        @pl.loop(0, nk)
+        def _(h):
+            t = (ch * 2 + 1) * nk + h
+            raw = jnp.dot(c_ref[ch], n_ring.get(t)[...], preferred_element_type=F32)
+            n_ring.free(t)
+            for m in range(3):
+                vst[ch, m, :, cols(h, hd)] = raw[m * rows : (m + 1) * rows].astype(BF16)
+
+        for m in range(3):
+            s = slot_of(ch, m)
+            local(y_at(ch, m), h_ref.at[s], hsem.at[s]).start()
+
+    def query(h):
+        t = 4 * nk + h
+        tile = n_ring.get(t)
+        for ch in range(2):
+            raw = jnp.dot(c_ref[ch], tile[...], preferred_element_type=F32)
+            for m in range(3):
+                out = norm_turn(raw[m * rows : (m + 1) * rows], q_gain, *turn(ch, m))
+                qst[ch, m, h] = out * BF16(hd**-0.5)
+        n_ring.free(t)
+
+    def first_keys():
+        wait_group(n_dev)
+        send_keys(0)
+
+    mlp(0, lambda: None)
+    keys_and_values(0)
+    mlp(1, first_keys)
+    keys_and_values(1)
+    query(0)
+    send_keys(1)
+    pl.loop(1, nq)(query)
     for ch in range(2):
-
-        @pl.when(t == ch * span + n_f)
-        def _():
-            for m in range(3):
-                h = result(m, y_ref[ch, own_rows(m), :])
-                y_ref[ch, own_rows(m), :] = h
-                c_ref[own_rows(m), :] = norm_rows(h.astype(F32), gain(0, layer + 1)).astype(BF16)
-
-        if ch == 1:
-            @pl.when(t == span + n_f)
-            def _():
-                for m in range(3):
-                    s = slot_of(0, m)
-                    keys.wait_sent(s, (kst.at[m], vst.at[m]))
-                    local(qst.at[m], q_ref.at[s], qsem.at[s]).wait()
-
-        def turn(m):
-            r = slot_rows(slot_of(ch, m))
-            return cos_ref[r, :], sin_ref[r, :]
-
-        def heads(w_ref, put):
-            for h in range(w_ref.shape[-1] // hd):
-                raw = jnp.dot(c_ref[...], w_ref[0, :, h * hd : (h + 1) * hd], preferred_element_type=F32)
-                for m in range(3):
-                    put(h, m, raw[m * rows : (m + 1) * rows])
-
-        u = t - (ch * span + n_f + 1)
-        per = wk_ref.shape[-1] // hd
-
-        @pl.when((u >= 0) & (u < n_k))
-        def _():
-            def put(h, m, raw):
-                col = pl.ds(pl.multiple_of((u * per + h) * hd, hd), hd)
-                kst[m, :, col] = norm_turn(raw, qk_ref[layer + 1, 1:2, :].astype(F32), *turn(m))
-
-            heads(wk_ref, put)
-
-        @pl.when((u >= n_k) & (u < 2 * n_k))
-        def _():
-            def put(h, m, raw):
-                col = pl.ds(pl.multiple_of(((u - n_k) * per + h) * hd, hd), hd)
-                vst[m, :, col] = raw.astype(BF16)
-
-            heads(wv_ref, put)
-
-        @pl.when((u >= 2 * n_k) & (u < 2 * n_k + n_q))
-        def _():
-            def put(h, m, raw):
-                out = norm_turn(raw, qk_ref[layer + 1, 0:1, :].astype(F32), *turn(m))
-                qst[m, (u - 2 * n_k) * per + h] = out * BF16(hd**-0.5)
-
-            heads(wq_ref, put)
-
-        @pl.when(u == 2 * n_k)
-        def _():
-            if ch == 0:
-                wait_group(n_dev)
-            for m in range(3):
-                s = slot_of(ch, m)
-                keys.start(s, (kst.at[m], vst.at[m]))
-                local(y_ref.at[ch, own_rows(m)], h_ref.at[s], hsem.at[s]).start()
-
-        @pl.when(u == 2 * n_k + n_q - 1)
-        def _():
-            for m in range(3):
-                s = slot_of(ch, m)
-                local(qst.at[m], q_ref.at[s], qsem.at[s]).start()
-
-    @pl.when(t == span - 1)
-    def _():
-        for m in range(3):
-            c_ref[own_rows(m), :] = c_of(y_ref[1, own_rows(m), :])
-
-    @pl.when(i == pl.num_programs(0) - 1)
-    def _():
-        for m in range(3):
-            s = slot_of(1, m)
-            keys.wait_sent(s, (kst.at[m], vst.at[m]))
-            local(qst.at[m], q_ref.at[s], qsem.at[s]).wait()
-        for s in range(6):
-            local(y_ref.at[0, own_rows(0)], h_ref.at[s], hsem.at[s]).wait()
-        keys.wait_all(6)
+        for m in range(3):
+            s = slot_of(ch, m)
+            local(qst.at[ch, m], q_ref.at[s], qsem.at[s]).start()
+    for ch in range(2):
+        for m in range(3):
+            s = slot_of(ch, m)
+            keys.wait_sent(s, (kst.at[ch, m], vst.at[ch, m]))
+            local(qst.at[ch, m], q_ref.at[s], qsem.at[s]).wait()
+            local(y_at(ch, m), h_ref.at[s], hsem.at[s]).wait()
+    keys.wait_all(6)
 
 
 def after_attention(layer, last, n_dev, cid, o, x, ln_w, w_o, w_gate, w_up, w_down, more=()):
@@ -694,64 +727,40 @@
     total = slots * rows
     half = total // 2
     blocks = 16
-    tn, tf = min(256, dim), min(768 if last and ff % 768 == 0 else 512, ff)
-    n_o, n_f = dim // tn, ff // tf
+    tn, tf = min(256, dim), min(512, ff)
+    deep = 3
     o2, x2 = o.reshape(total, inner), x.reshape(total, dim)
-    n_k = n_q = 0
-    if not last:
-        qk_w, cos, sin, w_q, w_k, w_v = more
-        hd = qk_w.shape[-1]
-        wide = 2 * hd
-        n_k, n_q = w_k.shape[-1] // wide, w_q.shape[-1] // wide
-    span = n_f + 1 + 2 * n_k + n_q
-    one = lambda a: pl.BlockSpec(a.shape, lambda i: (0,) * a.ndim, pipeline_mode=pl.Buffered(1))
-
-    def at_step(i):
-        t = i - n_o
-        return jnp.where(t >= span, t - span, t)
-
-    def at_f(i):
-        return jnp.clip(at_step(i), 0, n_f - 1)
-
-    def next_w(lo, n):
-        return lambda i: (layer + 1, 0, jnp.clip(at_step(i) - (n_f + 1 + lo), 0, n - 1))
-
-    mlp_specs = [
-        pl.BlockSpec((1, inner, tn), lambda i: (layer, 0, jnp.minimum(i, n_o - 1))),
-        pl.BlockSpec((1, dim, tf), lambda i: (layer, 0, at_f(i))),
-        pl.BlockSpec((1, dim, tf), lambda i: (layer, 0, at_f(i))),
-        pl.BlockSpec((1, tf, dim), lambda i: (layer, at_f(i - 1), 0)),
+    work = [
+        pltpu.VMEM((total, inner), BF16), pltpu.VMEM((total, dim), BF16),
+        pltpu.VMEM((total, dim), BF16), pltpu.VMEM((2, half, dim), BF16),
+        pltpu.VMEM((half, dim), F32), pltpu.VMEM((2, half, tf), BF16),
+        pltpu.VMEM((deep, inner, tn), BF16), pltpu.VMEM((deep, dim, tf), BF16), pltpu.VMEM((deep, dim, tf), BF16),
+        pltpu.VMEM((deep, tf, dim), BF16),
+        DMA((2,)), DMA((deep,)), DMA((deep,)), DMA((deep,)), DMA((deep,)),
     ]
-    work = [
-        pltpu.VMEM((total, dim), BF16), pltpu.VMEM((2, half, dim), BF16), pltpu.VMEM((half, dim), BF16),
-        pltpu.VMEM((half, dim), F32), pltpu.VMEM((2, half, tf), BF16),
-    ]
-    params = pltpu.CompilerParams(
-        dimension_semantics=("arbitrary",), collective_id=cid, has_side_effects=True, vmem_limit_bytes=VMEM_LIMIT
-    )
-    body = functools.partial(layer_kernel, layer, last, n_dev, n_o, n_f, n_k, n_q)
+    params = pltpu.CompilerParams(collective_id=cid, has_side_effects=True, vmem_limit_bytes=VMEM_LIMIT)
+    body = functools.partial(layer_kernel, layer, last, n_dev)
     if last:
         return pl.pallas_call(
-            body, grid=(n_o + 2 * span,),
-            in_specs=[one(o2), one(x2), one(ln_w)] + mlp_specs,
+            body,
+            in_specs=[ANY, ANY, WHOLE] + [ANY] * 4,
             out_specs=ANY,
             out_shape=jax.ShapeDtypeStruct(x.shape, BF16),
             scratch_shapes=work + [pltpu.VMEM((3, rows, dim), BF16), DMA((3,)), DMA((3,)), DMA((3,)), DMA((slots,))],
             compiler_params=params,
         )(o2, x2, ln_w, w_o, w_gate, w_up, w_down)
+    qk_w, cos, sin, w_q, w_k, w_v = more
+    hd = qk_w.shape[-1]
     nq, nk = w_q.shape[-1] // hd, w_k.shape[-1] // hd
     q_shape, kv_shape = (slots, nq, rows, hd), (blocks, rows, nk * hd)
     return pl.pallas_call(
-        body, grid=(n_o + 2 * span,),
-        in_specs=[one(o2), one(x2), one(ln_w), one(qk_w), one(cos), one(sin)] + mlp_specs + [
-            pl.BlockSpec((1, dim, wide), next_w(0, n_k)),
-            pl.BlockSpec((1, dim, wide), next_w(n_k, n_k)),
-            pl.BlockSpec((1, dim, wide), next_w(2 * n_k, n_q)),
-        ],
+        body,
+        in_specs=[ANY, ANY, WHOLE, WHOLE, WHOLE, WHOLE] + [ANY] * 7,
         out_specs=[ANY] * 4,
         out_shape=[jax.ShapeDtypeStruct(a, BF16) for a in (x.shape, q_shape, kv_shape, kv_shape)],
         scratch_shapes=work + [
-            pltpu.VMEM((3, nq, rows, hd), BF16), pltpu.VMEM((3, rows, nk * hd), BF16), pltpu.VMEM((3, rows, nk * hd), BF16),
+            pltpu.VMEM((deep, dim, hd), BF16), DMA((deep,)),
+            pltpu.VMEM((2, 3, nq, rows, hd), BF16), pltpu.VMEM((2, 3, rows, nk * hd), BF16), pltpu.VMEM((2, 3, rows, nk * hd), BF16),
             DMA((slots,)), DMA((slots,)), DMA((2, 3, slots)), DMA((2, blocks)), DMA((2, 2)),
         ],
         compiler_params=params,

time: 539 us -> 548 us (1.017)
  the two profiles are of different devices: /device:TPU:61 before, /device:TPU:181 now
where the time goes in v5:
time: 548 us; the launch traced here: 541 us
  Pallas kernels  532 us (97%)
    pallas_call x1, Pallas kernels, after_attention(): pl.pallas_call(body, in_specs=[ANY, ANY, WHOLE, WHOLE, WHOLE, WHOLE] + [A...  190 us
    pallas_call x1, Pallas kernels, after_attention(): pl.pallas_call(body, in_specs=[ANY, ANY, WHOLE] + [ANY] * 4, out_specs=AN...  162 us
    pallas_call x1, Pallas kernels, first(): pl.pallas_call(functools.partial(first_kernel, n_dev, nq, nk), out_shape=...  128 us
    pallas_call x2, Pallas kernels, attention(): pl.pallas_call(functools.partial(attn_kernel, None if window is None else...  51.7 us

profile of v5, /device:TPU:181, one launch (start us, length us, event | category | flops | bytes accessed | tf_op | source)
XLA Modules:
  0.0 541.1 jit_solution(17324751027835483625)
XLA Ops:
  0.0 0.1 stack.27
  0.1 0.1 broadcast_multiply_fusion
  0.2 0.1 convert_bitcast_fusion
  0.3 2.5 multiply_sine_fusion.1
  2.7 2.5 multiply_sine_fusion
  5.2 127.9 %shard_map.100 = (bf16[6,128,2304]{2,1,0:T(8,128)(2,1)}, bf16[6,8,128,256]{3,2,1,0:T(8,128)(2,1)}, bf16[16,128,1024]{2,1,0:T(8,128)(2,1)}, bf16[16,128,1024]{2,1,0:T(8,128)(2,1)}) custom-call(bf16[6,128,2304]{2,1,0:T(8,128)(2,1)} %x_ref.1, bf16[2,4,2304]{2,1,0:T(4,128)(2,1)} %refs_2_.3, bf16[2,2,256]{2,1,0:T(2,128)(2,1)} %refs_3_.2, ...), custom_call_target="tpu_custom_call" | custom-call | tf_op jit(solution)/shard_map/pallas_call | solution.py:286
  133.1 24.8 %shard_map.101 = bf16[6,128,2048]{2,1,0:T(8,128)(2,1)} custom-call(bf16[6,8,128,256]{3,2,1,0:T(8,128)(2,1)} %get-tuple-element.13.q_ref, bf16[16,128,1024]{2,1,0:T(8,128)(2,1)} %get-tuple-element.14.k_ref, bf16[16,128,1024]{2,1,0:T(8,128)(2,1)} %get-tuple-element.15.v_ref), custom_call_target="tpu_custom_call" | custom-call | tf_op jit(solution)/shard_map/pallas_call | solution.py:414
  157.9 190.1 %shard_map.102 = (bf16[6,128,2304]{2,1,0:T(8,128)(2,1)}, bf16[6,8,128,256]{3,2,1,0:T(8,128)(2,1)}, bf16[16,128,1024]{2,1,0:T(8,128)(2,1)}, bf16[16,128,1024]{2,1,0:T(8,128)(2,1)}) custom-call(bf16[768,2048]{1,0:T(8,128)(2,1)} %bitcast.14, bf16[768,2304]{1,0:T(8,128)(2,1)} %bitcast.16, bf16[2,4,2304]{2,1,0:T(4,128)(2,1)} %refs_2_.3, ...), custom_call_target="tpu_custom_call" | custom-call | tf_op jit(solution)/shard_map/pallas_call | solution.py:756
  348.0 26.9 %shard_map.103 = bf16[6,128,2048]{2,1,0:T(8,128)(2,1)} custom-call(bf16[6,8,128,256]{3,2,1,0:T(8,128)(2,1)} %get-tuple-element.17.q_ref, bf16[16,128,1024]{2,1,0:T(8,128)(2,1)} %get-tuple-element.18.k_ref, bf16[16,128,1024]{2,1,0:T(8,128)(2,1)} %get-tuple-element.19.v_ref), custom_call_target="tpu_custom_call" | custom-call | tf_op jit(solution)/shard_map/pallas_call | solution.py:414
  375.0 161.8 %shard_map.104 = bf16[6,128,2304]{2,1,0:T(8,128)(2,1)} custom-call(bf16[768,2048]{1,0:T(8,128)(2,1)} %bitcast.15, bf16[768,2304]{1,0:T(8,128)(2,1)} %bitcast.17, bf16[2,4,2304]{2,1,0:T(4,128)(2,1)} %refs_2_.3, bf16[2,2048,2304]{2,1,0:T(8,128)(2,1)} %refs_3_.3, bf16[2,2304,9216]{2,1,0:T(8,128)(2,1)} %refs_4_.1, bf16[2,2304,9216]{2,1,0:T(8,128)(2,1)} %refs_5_.1, ...), custom_call_target="tpu_custom_call" | custom-call | tf_op jit(solution)/shard_map/pallas_call | solution.py:744
  536.8 4.0 copy.12
  (3 shorter events, 0.0 us)

commit v6 on v5

--- a/solution.py
+++ b/solution.py
@@ -201,7 +201,7 @@
 
     weights = ((wk_ref, wk), (wv_ref, wv), (wq_ref, wq))
     for j, (src, dst) in enumerate(weights):
-        local(src.at[0], dst, wsem.at[j]).start()
+        start_parts(src.at[0], dst, wsem.at[j])
     wait_group(n_dev)
     for b in SEND_ORDER:
         dev, slot = homes[b]
@@ -428,6 +428,16 @@
     )(q, k, v)
 
 
+def start_parts(src, dst, sem, parts=4):
+    n = src.shape[0]
+    if n % (parts * 16):
+        local(src, dst, sem).start()
+        return
+    for j in range(parts):
+        part = pl.ds(j * (n // parts), n // parts)
+        local(src.at[part], dst.at[part], sem).start()
+
+
 class Ring:
     def __init__(self, buf, sem, count, source):
         self.buf, self.sem, self.count, self.source = buf, sem, count, source
@@ -438,7 +448,10 @@
             self.start(t, t)
 
     def start(self, t, slot):
-        self.source(t, lambda ref: local(ref, self.buf.at[slot], self.sem.at[slot]).start())
+        def put(ref):
+            start_parts(ref, self.buf.at[slot], self.sem.at[slot])
+
+        self.source(t, put)
 
     def get(self, t):
         slot = lax.rem(t, self.depth) if not isinstance(t, int) else t % self.depth
@@ -488,9 +501,9 @@
 
     in_o = local(o_ref, obuf, isem.at[0])
     in_x = local(x_ref, y_ref, isem.at[1])
-    in_o.start()
+    start_parts(o_ref, obuf, isem.at[0], 6)
     o_ring.begin()
-    in_x.start()
+    start_parts(x_ref, y_ref, isem.at[1], 6)
     for r in (g_ring, u_ring, d_ring):
         r.begin()
     signal_group(n_dev)
@@ -536,30 +549,32 @@
             if ch == 0 or not last:
                 c_ref[ch, own_rows(m), :] = c_of(y)
 
-    def up(ch, t, to):
-        gate = jnp.dot(c_ref[ch], g_ring.get(t)[...], preferred_element_type=F32)
-        val = jnp.dot(c_ref[ch], u_ring.get(t)[...], preferred_element_type=F32)
-        act[to] = (jax.nn.gelu(gate, approximate=True) * val).astype(BF16)
-        g_ring.free(t)
-        u_ring.free(t)
-
-    def down(t, at):
-        acc[...] += jnp.dot(act[at], d_ring.get(t)[...], preferred_element_type=F32)
-        d_ring.free(t)
+    def up(ch, g_tile, u_tile):
+        gate = jnp.dot(c_ref[ch], g_tile[...], preferred_element_type=F32)
+        val = jnp.dot(c_ref[ch], u_tile[...], preferred_element_type=F32)
+        return (jax.nn.gelu(gate, approximate=True) * val).astype(BF16)
 
     def mlp(ch, after_first):
         base = ch * n_f
+        act[0] = up(ch, g_ring.get(base), u_ring.get(base))
         acc[...] = jnp.zeros(acc.shape, F32)
-        up(ch, base, 0)
+        g_ring.free(base)
+        u_ring.free(base)
         after_first()
 
         @pl.loop(1, n_f)
         def _(t):
-            even = lax.rem(t, 2)
-            down(base + t - 1, 1 - even)
-            up(ch, base + t, even)
-
-        down(base + n_f - 1, (n_f - 1) % 2)
+            new = lax.rem(t, 2)
+            g_tile, u_tile, d_tile = g_ring.get(base + t), u_ring.get(base + t), d_ring.get(base + t - 1)
+            acc[...] += jnp.dot(act[1 - new], d_tile[...], preferred_element_type=F32)
+            act[new] = up(ch, g_tile, u_tile)
+            g_ring.free(base + t)
+            u_ring.free(base + t)
+            d_ring.free(base + t - 1)
+
+        t = base + n_f - 1
+        acc[...] += jnp.dot(act[(n_f - 1) % 2], d_ring.get(t)[...], preferred_element_type=F32)
+        d_ring.free(t)
 
     def result(m, y):
         val = acc[own_rows(m), :].astype(BF16).astype(F32)

time: 548 us -> 486 us (0.89)
  the two profiles are of different devices: /device:TPU:181 before, /device:TPU:183 now
where the time goes in v6:
time: 486 us; the launch traced here: 479 us
  Pallas kernels  470 us (97%)
  other arithmetic  5.12 us (1%)
    pallas_call x1, Pallas kernels, after_attention(): pl.pallas_call(body, in_specs=[ANY, ANY, WHOLE, WHOLE, WHOLE, WHOLE] + [A...  159 us
    pallas_call x1, Pallas kernels, after_attention(): pl.pallas_call(body, in_specs=[ANY, ANY, WHOLE] + [ANY] * 4, out_specs=AN...  131 us
    pallas_call x1, Pallas kernels, first(): pl.pallas_call(functools.partial(first_kernel, n_dev, nq, nk), out_shape=...  128 us
    pallas_call x2, Pallas kernels, attention(): pl.pallas_call(functools.partial(attn_kernel, None if window is None else...  51.8 us

profile of v6, /device:TPU:183, one launch (start us, length us, event | category | flops | bytes accessed | tf_op | source)
XLA Modules:
  0.0 479.4 jit_solution(1566350399737083807)
XLA Ops:
  0.0 0.1 stack.27
  0.1 0.1 broadcast_multiply_fusion
  0.2 0.1 convert_bitcast_fusion
  0.3 2.5 multiply_sine_fusion.1
  2.7 2.5 multiply_sine_fusion
  5.2 127.9 %shard_map.100 = (bf16[6,128,2304]{2,1,0:T(8,128)(2,1)}, bf16[6,8,128,256]{3,2,1,0:T(8,128)(2,1)}, bf16[16,128,1024]{2,1,0:T(8,128)(2,1)}, bf16[16,128,1024]{2,1,0:T(8,128)(2,1)}) custom-call(bf16[6,128,2304]{2,1,0:T(8,128)(2,1)} %x_ref.1, bf16[2,4,2304]{2,1,0:T(4,128)(2,1)} %refs_2_.3, bf16[2,2,256]{2,1,0:T(2,128)(2,1)} %refs_3_.2, ...), custom_call_target="tpu_custom_call" | custom-call | tf_op jit(solution)/shard_map/pallas_call | solution.py:286
  133.1 24.8 %shard_map.101 = bf16[6,128,2048]{2,1,0:T(8,128)(2,1)} custom-call(bf16[6,8,128,256]{3,2,1,0:T(8,128)(2,1)} %get-tuple-element.13.q_ref, bf16[16,128,1024]{2,1,0:T(8,128)(2,1)} %get-tuple-element.14.k_ref, bf16[16,128,1024]{2,1,0:T(8,128)(2,1)} %get-tuple-element.15.v_ref), custom_call_target="tpu_custom_call" | custom-call | tf_op jit(solution)/shard_map/pallas_call | solution.py:414
  157.9 159.3 %shard_map.102 = (bf16[6,128,2304]{2,1,0:T(8,128)(2,1)}, bf16[6,8,128,256]{3,2,1,0:T(8,128)(2,1)}, bf16[16,128,1024]{2,1,0:T(8,128)(2,1)}, bf16[16,128,1024]{2,1,0:T(8,128)(2,1)}) custom-call(bf16[768,2048]{1,0:T(8,128)(2,1)} %bitcast.14, bf16[768,2304]{1,0:T(8,128)(2,1)} %bitcast.16, bf16[2,4,2304]{2,1,0:T(4,128)(2,1)} %refs_2_.3, ...), custom_call_target="tpu_custom_call" | custom-call | tf_op jit(solution)/shard_map/pallas_call | solution.py:771
  317.2 27.0 %shard_map.103 = bf16[6,128,2048]{2,1,0:T(8,128)(2,1)} custom-call(bf16[6,8,128,256]{3,2,1,0:T(8,128)(2,1)} %get-tuple-element.17.q_ref, bf16[16,128,1024]{2,1,0:T(8,128)(2,1)} %get-tuple-element.18.k_ref, bf16[16,128,1024]{2,1,0:T(8,128)(2,1)} %get-tuple-element.19.v_ref), custom_call_target="tpu_custom_call" | custom-call | tf_op jit(solution)/shard_map/pallas_call | solution.py:414
  344.2 130.7 %shard_map.104 = bf16[6,128,2304]{2,1,0:T(8,128)(2,1)} custom-call(bf16[768,2048]{1,0:T(8,128)(2,1)} %bitcast.15, bf16[768,2304]{1,0:T(8,128)(2,1)} %bitcast.17, bf16[2,4,2304]{2,1,0:T(4,128)(2,1)} %refs_2_.3, bf16[2,2048,2304]{2,1,0:T(8,128)(2,1)} %refs_3_.3, bf16[2,2304,9216]{2,1,0:T(8,128)(2,1)} %refs_4_.1, bf16[2,2304,9216]{2,1,0:T(8,128)(2,1)} %refs_5_.1, ...), custom_call_target="tpu_custom_call" | custom-call | tf_op jit(solution)/shard_map/pallas_call | solution.py:759
  474.9 4.0 copy.12
  (3 shorter events, 0.0 us)

commit v7 on v6

--- a/solution.py
+++ b/solution.py
@@ -70,7 +70,7 @@
 
 def chunk_slot(ch, i, special, row):
     b = jnp.where(special == 1, row + i, row)
-    return 2 * i + (b % 2 if ch == 0 else 1 - b % 2)
+    return 2 * i + (b + ch) % 2
 
 
 def kv_index(s, core, special, row):
@@ -116,7 +116,8 @@
 
 
 class KeyValues:
-    def __init__(self, k_all, v_all, send, recv, fwd):
+    def __init__(self, k_all, v_all, send, recv, fwd, in_place=False):
+        self.in_place = in_place
         self.both = ((0, k_all), (1, v_all))
         self.send, self.recv, self.fwd = send, recv, fwd
 
@@ -132,10 +133,11 @@
             dev = jnp.where(s // 2 == r, served(self.row, r) * 2 + self.core, dev)
         out = []
         for x, full in self.both:
+            src = full.at[idx] if self.in_place else stage[x]
             out.append((
-                local(stage[x], full.at[idx], self.send.at[x, 0, s]),
-                remote(stage[x], full.at[idx], self.send.at[x, 1, s], self.recv.at[x, idx], self.mate),
-                remote(stage[x], full.at[blk], self.send.at[x, 2, s], self.recv.at[x, blk], dev),
+                None if self.in_place else local(src, full.at[idx], self.send.at[x, 0, s]),
+                remote(src, full.at[idx], self.send.at[x, 1, s], self.recv.at[x, idx], self.mate),
+                remote(src, full.at[blk], self.send.at[x, 2, s], self.recv.at[x, blk], dev),
             ))
         return out
 
@@ -148,49 +150,162 @@
                 row.start()
 
             mate.start()
-            own.start()
+            if own is not None:
+                own.start()
 
     def wait_sent(self, s, stage):
         self.here()
         for own, mate, row in self._copies(s, stage):
-            own.wait()
+            if own is not None:
+                own.wait()
             mate.wait_send()
 
             @pl.when(self.special == 1)
             def _():
                 row.wait_send()
 
-    def wait_all(self, slots):
+    def wait_mate(self, slots):
         self.here()
         for x, full in self.both:
-
-            @pl.when(self.special == 0)
-            def _():
-                for k in range(2):
-                    blk = 2 * k + (k + self.core) % 2
-                    remote(full.at[blk], full.at[blk], self.fwd.at[x, k], self.recv.at[x, blk], self.mate).wait_recv()
-                    remote(full.at[blk], full.at[blk], self.fwd.at[x, k], self.recv.at[x, blk], self.mate).start()
-
             for s in range(slots):
                 idx = kv_index(s, 1 - self.core, self.special, self.row)
                 remote(full.at[idx], full.at[idx], self.fwd.at[x, 0], self.recv.at[x, idx], self.mate).wait_recv()
 
+    def wait_special(self):
+        self.here()
+
         @pl.when(self.special == 0)
         def _():
+            for k in range(2):
+                blk = 2 * k + (k + self.core) % 2
+                for x, full in self.both:
+                    remote(full.at[blk], full.at[blk], self.fwd.at[x, k], self.recv.at[x, blk], self.mate).wait_recv()
+                    remote(full.at[blk], full.at[blk], self.fwd.at[x, k], self.recv.at[x, blk], self.mate).start()
             for x, full in self.both:
                 for k in range(2):
                     blk = 2 * k + (k + 1 - self.core) % 2
                     remote(full.at[blk], full.at[blk], self.fwd.at[x, k], self.recv.at[x, blk], self.mate).wait()
 
 
-def first_kernel(n_dev, nq, nk, x_ref, ln_ref, qk_ref, cos_ref, sin_ref, wq_ref, wk_ref, wv_ref,
-                 h_ref, q_ref, k_all, v_all, xbuf, abuf, wq, wk, wv, qst, kst, vst,
-                 wsem, xsend, xrecv, hsem, qsem, ksend, krecv, fsem):
+class Trig:
+    def __init__(self, ref, layer, rows):
+        self.ref, self.layer, self.rows = ref, layer, rows
+
+    def of(self, blk):
+        cu, su = (self.ref[self.layer, j, : self.rows, :] for j in range(2))
+        cb, sb = (self.ref[self.layer, j, pl.ds(self.rows + blk, 1), :] for j in range(2))
+        return cu * cb - su * sb, su * cb + cu * sb
+
+
+class Attention:
+    per, lanes = 4, 128
+
+    def __init__(self, window_blocks, hd, qbuf, kbuf, vbuf, sbuf, wacc, wm, wl, bias, o_ref, osem):
+        self.window_blocks, self.hd = window_blocks, hd
+        self.qbuf, self.kbuf, self.vbuf, self.sbuf, self.bias = qbuf, kbuf, vbuf, sbuf, bias
+        self.wacc, self.wm, self.wl, self.o_ref, self.osem = wacc, wm, wl, o_ref, osem
+        self.slots, self.rows = qbuf.shape[:2]
+        self.nk = kbuf.shape[-1] // hd
+        self.rep = qbuf.shape[-1] // kbuf.shape[-1]
+        self.tile = self.per * self.rows
+
+    def fill_bias(self):
+        rows, tile, bias = self.rows, self.tile, self.bias
+        qi = lax.broadcasted_iota(jnp.int32, (rows, tile), 0)
+        ki = lax.broadcasted_iota(jnp.int32, (rows, tile), 1)
+        bias[0] = jnp.zeros((rows, tile), F32)
+        for j in range(self.per):
+            bias[1 + j] = jnp.where(ki <= qi + j * rows, 0.0, NEG)
+            if self.window_blocks is not None:
+                bias[1 + self.per + j] = jnp.where(ki > qi + j * rows, 0.0, NEG)
+
+    def start_tile(self, blk):
+        if self.window_blocks is None:
+            return jnp.int32(0)
+        return jnp.maximum(blk - self.window_blocks, 0) // self.per
+
+    def part(self, buf, t, base, g):
+        block = buf.at[pl.ds(base + self.per * t, self.per)]
+        return block[:, :, g * self.hd : (g + 1) * self.hd].reshape(self.tile, self.hd)
+
+    def scores(self, s, t, base, blk):
+        rows, rep, hd, per = self.rows, self.rep, self.hd, self.per
+        edge = jnp.where(t == blk // per, 1 + blk % per, 0)
+        if self.window_blocks is not None:
+            old = blk - self.window_blocks
+            edge = jnp.where((old >= 0) & (t == old // per), 1 + per + old % per, edge)
+        off = self.bias[edge][None]
+        out = []
+        for g in range(self.nk):
+            heads = [self.qbuf[s, :, h * hd : (h + 1) * hd] for h in range(g * rep, (g + 1) * rep)]
+            q2 = jnp.concatenate(heads, axis=0)
+            sc = lax.dot_general(q2, self.part(self.kbuf, t, base, g), (((1,), (1,)), ((), ())), preferred_element_type=F32)
+            out.append((sc.reshape(rep, rows, self.tile) + off).reshape(rep * rows, self.tile))
+        return out
+
+    def columns(self, val, op):
+        return functools.reduce(op, [val[:, j * self.lanes : (j + 1) * self.lanes] for j in range(self.tile // self.lanes)])
+
+    def spread(self, val):
+        return jnp.concatenate([val] * (self.tile // self.lanes), axis=1)
+
+    def row_max(self, val):
+        return jnp.broadcast_to(jnp.max(val, axis=-1, keepdims=True), val.shape)
+
+    def passes(self, s, blk, base, first, last):
+        for g in range(self.nk):
+            self.wm[g] = jnp.full(self.wm.shape[1:], NEG, F32)
+            self.wl[g] = jnp.zeros(self.wl.shape[1:], F32)
+            self.wacc[g] = jnp.zeros(self.wacc.shape[1:], F32)
+
+        @pl.loop(first, last)
+        def _(t):
+            for g, sc in enumerate(self.scores(s, t, base, blk)):
+                self.sbuf[g, t - first] = sc
+                self.wm[g] = jnp.maximum(self.wm[g], self.columns(sc, jnp.maximum))
+
+        for g in range(self.nk):
+            self.wm[g] = self.row_max(self.wm[g])
+
+        @pl.loop(first, last)
+        def _(t):
+            for g in range(self.nk):
+                p = jnp.exp(self.sbuf[g, t - first] - self.spread(self.wm[g]))
+                self.wl[g] += self.columns(p, jnp.add)
+                self.wacc[g] += jnp.dot(p.astype(BF16), self.part(self.vbuf, t, base, g), preferred_element_type=F32)
+
+    def merge(self, s, blk, old, old_sum, old_acc):
+        for g, sc in enumerate(self.scores(s, 0, 0, blk)):
+            new = self.row_max(jnp.maximum(old[g], self.columns(sc, jnp.maximum)))
+            p = jnp.exp(sc - self.spread(new))
+            alpha = jnp.exp(old[g] - new)
+            self.wl[g] = alpha * old_sum[g] + self.columns(p, jnp.add)
+            part = jnp.dot(p.astype(BF16), self.part(self.vbuf, 0, 0, g), preferred_element_type=F32)
+            self.wacc[g] = jnp.concatenate([alpha] * (self.hd // self.lanes), axis=1) * old_acc[g] + part
+
+    def finish(self, s):
+        for g in range(self.nk):
+            out = (self.wacc[g] / jnp.sum(self.wl[g], axis=-1, keepdims=True)).astype(BF16)
+            for h in range(self.rep):
+                lo = (g * self.rep + h) * self.hd
+                self.qbuf[s, :, lo : lo + self.hd] = out[h * self.rows : (h + 1) * self.rows]
+        local(self.qbuf.at[s], self.o_ref.at[s], self.osem.at[s]).start()
+
+    def wait_out(self):
+        for s in range(self.slots):
+            local(self.qbuf.at[s], self.o_ref.at[s], self.osem.at[s]).wait()
+
+
+def first_kernel(n_dev, window_blocks, x_ref, ln_ref, qk_ref, trig_ref, wq_ref, wk_ref, wv_ref,
+                 h_ref, o_ref, xbuf, abuf, wq, wk, wv, qbuf, kbuf, vbuf, sbuf, wacc, wm, wl, bias, mx, sm, acc,
+                 wsem, xsend, xrecv, hsem, osem, ksend, krecv, fsem):
     me, chip, core, special, row = placement()
     n, rows, dim = x_ref.shape
     hd = qk_ref.shape[-1]
+    nq, nk = wq.shape[-1] // hd, wk.shape[-1] // hd
     homes = [home_of(jnp.int32(b), me) for b in range(n)]
-    keys = KeyValues(k_all, v_all, ksend, krecv, fsem)
+    keys = KeyValues(kbuf, vbuf, ksend, krecv, fsem, in_place=True)
+    att = Attention(window_blocks, hd, qbuf, kbuf, vbuf, sbuf, wacc, wm, wl, bias, o_ref, osem)
 
     signal_group(n_dev)
     for b, (dev, slot) in enumerate(homes):
@@ -199,8 +314,7 @@
         def _():
             local(x_ref.at[b], xbuf.at[slot], xrecv.at[slot]).start()
 
-    weights = ((wk_ref, wk), (wv_ref, wv), (wq_ref, wq))
-    for j, (src, dst) in enumerate(weights):
+    for j, (src, dst) in enumerate(((wk_ref, wk), (wv_ref, wv), (wq_ref, wq))):
         start_parts(src.at[0], dst, wsem.at[j])
     wait_group(n_dev)
     for b in SEND_ORDER:
@@ -210,60 +324,84 @@
         def _():
             remote(x_ref.at[b], xbuf.at[slot], xsend.at[b], xrecv.at[slot], dev).start()
 
+    att.fill_bias()
+    trig = Trig(trig_ref, 0, rows)
     gain = ln_ref[0, 0:1, :].astype(F32)
-
-    def take(pair):
-        places = [pick(chip, [ARRIVAL[c][2 * pair + j] for c in range(8)]) for j in range(2)]
+    k_gain = qk_ref[0, 1:2, :].astype(F32)
+    q_gain = qk_ref[0, 0:1, :].astype(F32)
+    for j, (src, dst) in enumerate(((wk_ref, wk), (wv_ref, wv), (wq_ref, wq))):
+        local(src.at[0], dst, wsem.at[j]).wait()
+    order = [s for c in range(8) for s in ARRIVAL[c]]
+
+    def col(h):
+        return pl.ds(h * hd if isinstance(h, int) else pl.multiple_of(h * hd, hd), hd)
+
+    def product(w, h):
+        return jnp.dot(abuf[...], w[:, col(h)], preferred_element_type=F32)
+
+    @pl.loop(0, n // 2)
+    def _(pair):
+        places = [pick(chip * n + 2 * pair + j, order) for j in range(2)]
+        turn, idx = [], []
         for j, s in enumerate(places):
             local(xbuf.at[s], xbuf.at[s], xrecv.at[s]).wait()
             local(xbuf.at[s], h_ref.at[s], hsem.at[s]).start()
             abuf[j * rows : (j + 1) * rows, :] = norm_rows(xbuf[s].astype(F32), gain).astype(BF16)
-        return places
-
-    def tables(s):
-        r = pl.ds(pl.multiple_of(s * rows, rows), rows)
-        return cos_ref[r, :], sin_ref[r, :]
-
-    def product(w, h):
-        return jnp.dot(abuf[...], w[:, pl.ds(pl.multiple_of(h * hd, hd), hd)], preferred_element_type=F32)
-
-    for pair in range(n // 2):
-        places = take(pair)
-        if pair == 0:
-            local(wk_ref.at[0], wk, wsem.at[0]).wait()
-            local(wv_ref.at[0], wv, wsem.at[1]).wait()
-        turn = [tables(s) for s in places]
-        k_gain = qk_ref[0, 1:2, :].astype(F32)
-        q_gain = qk_ref[0, 0:1, :].astype(F32)
+            turn.append(trig.of(slot_place(s, core, special, row)[1]))
+            idx.append(kv_index(s, core, special, row))
 
         @pl.loop(0, nk)
         def _(h):
-            col = pl.ds(pl.multiple_of(h * hd, hd), hd)
             k_raw, v_raw = product(wk, h), product(wv, h)
-            for j, s in enumerate(places):
+            for j in range(2):
                 part = slice(j * rows, (j + 1) * rows)
-                kst[s, :, col] = norm_turn(k_raw[part], k_gain, *turn[j])
-                vst[s, :, col] = v_raw[part].astype(BF16)
-
-        if pair == 0:
-            local(wq_ref.at[0], wq, wsem.at[2]).wait()
+                kbuf[idx[j], :, col(h)] = norm_turn(k_raw[part], k_gain, *turn[j])
+                vbuf[idx[j], :, col(h)] = v_raw[part].astype(BF16)
 
         def query(h):
             raw = product(wq, h)
             for j, s in enumerate(places):
                 part = slice(j * rows, (j + 1) * rows)
-                qst[s, h] = norm_turn(raw[part], q_gain, *turn[j]) * BF16(hd**-0.5)
+                qbuf[s, :, col(h)] = norm_turn(raw[part], q_gain, *turn[j]) * BF16(hd**-0.5)
 
         query(0)
         for s in places:
-            keys.start(s, (kst.at[s], vst.at[s]))
+            keys.start(s, None)
         pl.loop(1, nq)(query)
-        for s in places:
-            local(qst.at[s], q_ref.at[s], qsem.at[s]).start()
-
+
+    keys.wait_mate(n)
+
+    @pl.loop(0, n)
+    def _(s):
+        _, blk = slot_place(s, core, special, row)
+        base = jnp.where(special == 1, (s // 2) * att.per, 0)
+        att.passes(s, blk, base, jnp.where(special == 1, 0, jnp.maximum(att.start_tile(blk), 1)), blk // att.per + 1)
+        more = (special == 0) & (s < mx.shape[0])
+
+        @pl.when(more)
+        def _():
+            for g in range(nk):
+                mx[s, g] = wm[g]
+                sm[s, g] = wl[g]
+                acc[s, g] = wacc[g]
+
+        @pl.when(jnp.logical_not(more))
+        def _():
+            att.finish(s)
+
+    keys.wait_special()
+
+    @pl.when(special == 0)
+    def _():
+        @pl.loop(0, mx.shape[0])
+        def _(s):
+            _, blk = slot_place(s, core, special, row)
+            att.merge(s, blk, *[[ref[s, g] for g in range(nk)] for ref in (mx, sm, acc)])
+            att.finish(s)
+
+    att.wait_out()
     for s in range(n):
-        keys.wait_sent(s, (kst.at[s], vst.at[s]))
-        local(qst.at[s], q_ref.at[s], qsem.at[s]).wait()
+        keys.wait_sent(s, None)
         local(xbuf.at[s], h_ref.at[s], hsem.at[s]).wait()
     for b, (dev, slot) in enumerate(homes):
 
@@ -271,157 +409,85 @@
         def _():
             remote(x_ref.at[b], xbuf.at[slot], xsend.at[b], xrecv.at[slot], dev).wait_send()
 
-    keys.wait_all(n)
-
 
 SEND_ORDER = (2, 5, 0, 3, 1, 4)
 
 
-def first(n_dev, x, ln_w, qk_w, cos, sin, w_q, w_k, w_v):
+def attention_scratch(tiles, slots, rows, nq, nk, hd):
+    wide = nq // nk * rows
+    return [
+        pltpu.VMEM((nk, tiles, wide, 4 * rows), F32),
+        pltpu.VMEM((nk, wide, hd), F32), pltpu.VMEM((nk, wide, 128), F32), pltpu.VMEM((nk, wide, 128), F32),
+        pltpu.VMEM((9, rows, 4 * rows), F32),
+    ]
+
+
+def first(n_dev, window, x, ln_w, qk_w, trig, w_q, w_k, w_v):
     n, rows, dim = x.shape
     hd = qk_w.shape[-1]
     nq, nk = w_q.shape[-1] // hd, w_k.shape[-1] // hd
-    blocks = 16
-    q_shape, s_shape, kv_shape = (n, nq, rows, hd), (n, rows, nk * hd), (blocks, rows, nk * hd)
+    blocks, late, wide = 16, 4, nq // nk * rows
+    q_shape, kv_shape = (n, rows, nq * hd), (blocks, rows, nk * hd)
     return pl.pallas_call(
-        functools.partial(first_kernel, n_dev, nq, nk),
-        out_shape=[jax.ShapeDtypeStruct(a, BF16) for a in (x.shape, q_shape, kv_shape, kv_shape)],
-        in_specs=[ANY, WHOLE, WHOLE, WHOLE, WHOLE, ANY, ANY, ANY],
-        out_specs=[ANY] * 4,
+        functools.partial(first_kernel, n_dev, window // rows),
+        out_shape=[jax.ShapeDtypeStruct(a, BF16) for a in (x.shape, q_shape)],
+        in_specs=[ANY, WHOLE, WHOLE, WHOLE, ANY, ANY, ANY],
+        out_specs=[ANY] * 2,
         scratch_shapes=[
             pltpu.VMEM(x.shape, BF16), pltpu.VMEM((2 * rows, dim), BF16),
             pltpu.VMEM(w_q.shape[1:], BF16), pltpu.VMEM(w_k.shape[1:], BF16), pltpu.VMEM(w_v.shape[1:], BF16),
-            pltpu.VMEM(q_shape, BF16), pltpu.VMEM(s_shape, BF16), pltpu.VMEM(s_shape, BF16),
+            pltpu.VMEM(q_shape, BF16), pltpu.VMEM(kv_shape, BF16), pltpu.VMEM(kv_shape, BF16),
+            *attention_scratch(3, n, rows, nq, nk, hd),
+            pltpu.VMEM((late, nk, wide, 128), F32), pltpu.VMEM((late, nk, wide, 128), F32), pltpu.VMEM((late, nk, wide, hd), F32),
             DMA((3,)), DMA((n,)), DMA((n,)), DMA((n,)), DMA((n,)), DMA((2, 3, n)), DMA((2, blocks)), DMA((2, 2)),
         ],
         compiler_params=pltpu.CompilerParams(collective_id=0, has_side_effects=True, vmem_limit_bytes=VMEM_LIMIT),
-    )(x, ln_w, qk_w, cos, sin, w_q, w_k, w_v)
-
-
-def attn_kernel(window_blocks, q_ref, k_ref, v_ref, o_ref, kbuf, vbuf, qbuf, obuf, sbuf, wacc, wm, wl, bias, qsem, ksem, osem):
+    )(x, ln_w, qk_w, trig, w_q, w_k, w_v)
+
+
+def attn_kernel(window_blocks, hd, q_ref, k_ref, v_ref, o_ref, kbuf, vbuf, qbuf, sbuf, wacc, wm, wl, bias, qsem, ksem, osem):
     _, _, core, special, row = placement()
-    slots, nq, rows, hd = q_ref.shape
-    nk = k_ref.shape[-1] // hd
-    rep = nq // nk
-    per = 4
-    tile = per * rows
+    att = Attention(window_blocks, hd, qbuf, kbuf, vbuf, sbuf, wacc, wm, wl, bias, o_ref, osem)
+    per = att.per
     tiles = k_ref.shape[0] // per
 
     def loads(t):
         part = pl.ds(t * per, per)
         return [local(k_ref.at[part], kbuf.at[part], ksem.at[0, t]), local(v_ref.at[part], vbuf.at[part], ksem.at[1, t])]
 
-    for s in range(slots):
+    for s in range(att.slots):
         local(q_ref.at[s], qbuf.at[s], qsem.at[s]).start()
     for t in range(tiles):
         for c in loads(t):
             c.start()
-
-    qi = lax.broadcasted_iota(jnp.int32, (rows, tile), 0)
-    ki = lax.broadcasted_iota(jnp.int32, (rows, tile), 1)
-    bias[0] = jnp.zeros((rows, tile), jnp.float32)
-    for j in range(per):
-        bias[1 + j] = jnp.where(ki <= qi + j * rows, 0.0, NEG)
-        if window_blocks is not None:
-            bias[1 + per + j] = jnp.where(ki > qi + j * rows, 0.0, NEG)
-
-    def start_tile(blk):
-        if window_blocks is None:
-            return jnp.int32(0)
-        return jnp.maximum(blk - window_blocks, 0) // per
-
-    def scores(s, t, base, blk):
-        edge = jnp.where(t == blk // per, 1 + blk % per, 0)
-        if window_blocks is not None:
-            old = blk - window_blocks
-            edge = jnp.where((old >= 0) & (t == old // per), 1 + per + old % per, edge)
-        off = bias[edge][None]
-        kt = kbuf.at[pl.ds(base + per * t, per)]
-        out = []
-        for g in range(nk):
-            q2 = qbuf[s, g * rep : (g + 1) * rep].reshape(rep * rows, hd)
-            kk = kt[:, :, g * hd : (g + 1) * hd].reshape(tile, hd)
-            sc = lax.dot_general(q2, kk, (((1,), (1,)), ((), ())), preferred_element_type=jnp.float32)
-            out.append((sc.reshape(rep, rows, tile) + off).reshape(rep * rows, tile))
-        return out
-
-    lanes = 128
-
-    def columns(val, op):
-        parts = [val[:, j * lanes : (j + 1) * lanes] for j in range(tile // lanes)]
-        return functools.reduce(op, parts)
-
-    def spread(val):
-        return jnp.concatenate([val] * (tile // lanes), axis=1)
-
-    def row_max(val):
-        return jnp.broadcast_to(jnp.max(val, axis=-1, keepdims=True), val.shape)
-
-    def values(t, base, g):
-        return vbuf.at[pl.ds(base + per * t, per)][:, :, g * hd : (g + 1) * hd].reshape(tile, hd)
-
-    def finish(s, total, weight):
-        for g in range(nk):
-            out = (total[g] / jnp.sum(weight[g], axis=-1, keepdims=True)).astype(jnp.bfloat16)
-            for h in range(rep):
-                lo = (g * rep + h) * hd
-                obuf[s, :, lo : lo + hd] = out[h * rows : (h + 1) * rows]
-        local(obuf.at[s], o_ref.at[s], osem.at[s]).start()
-
+    att.fill_bias()
     for t in range(tiles):
         for c in loads(t):
             c.wait()
 
-    @pl.loop(0, slots)
+    @pl.loop(0, att.slots)
     def _(s):
         _, blk = slot_place(s, core, special, row)
+        local(q_ref.at[s], qbuf.at[s], qsem.at[s]).wait()
         base = jnp.where(special == 1, (s // 2) * per, 0)
-        first = start_tile(blk)
-        last = blk // per + 1
-        local(q_ref.at[s], qbuf.at[s], qsem.at[s]).wait()
-        for g in range(nk):
-            wm[g] = jnp.full(wm.shape[1:], NEG, F32)
-            wl[g] = jnp.zeros(wl.shape[1:], F32)
-            wacc[g] = jnp.zeros(wacc.shape[1:], F32)
-
-        @pl.loop(first, last)
-        def _(t):
-            for g, sc in enumerate(scores(s, t, base, blk)):
-                sbuf[g, t] = sc
-                wm[g] = jnp.maximum(wm[g], columns(sc, jnp.maximum))
-
-        for g in range(nk):
-            wm[g] = row_max(wm[g])
-
-        @pl.loop(first, last)
-        def _(t):
-            for g in range(nk):
-                p = jnp.exp(sbuf[g, t] - spread(wm[g]))
-                wl[g] += columns(p, jnp.add)
-                wacc[g] += jnp.dot(p.astype(BF16), values(t, base, g), preferred_element_type=F32)
-
-        finish(s, [wacc[g] for g in range(nk)], [wl[g] for g in range(nk)])
-
-    for s in range(slots):
-        local(obuf.at[s], o_ref.at[s], osem.at[s]).wait()
-
-
-def attention(window, q, k, v):
-    slots, nq, rows, hd = q.shape
+        att.passes(s, blk, base, att.start_tile(blk), blk // per + 1)
+        att.finish(s)
+
+    att.wait_out()
+
+
+def attention(window, hd, q, k, v):
+    slots, rows = q.shape[:2]
     blocks = k.shape[0]
-    nk = k.shape[-1] // hd
-    wide = nq // nk * rows
+    nq, nk = q.shape[-1] // hd, k.shape[-1] // hd
     return pl.pallas_call(
-        functools.partial(attn_kernel, None if window is None else window // rows),
-        out_shape=jax.ShapeDtypeStruct((slots, rows, nq * hd), BF16),
+        functools.partial(attn_kernel, None if window is None else window // rows, hd),
+        out_shape=jax.ShapeDtypeStruct(q.shape, BF16),
         in_specs=[ANY] * 3,
         out_specs=ANY,
         scratch_shapes=[
             pltpu.VMEM(k.shape, BF16), pltpu.VMEM(v.shape, BF16), pltpu.VMEM(q.shape, BF16),
-            pltpu.VMEM((slots, rows, nq * hd), BF16),
-            pltpu.VMEM((nk, blocks // 4, wide, 4 * rows), F32),
-            pltpu.VMEM((nk, wide, hd), F32), pltpu.VMEM((nk, wide, 128), F32), pltpu.VMEM((nk, wide, 128), F32),
-            pltpu.VMEM((9, rows, 4 * rows), F32),
+            *attention_scratch(blocks // 4, slots, rows, nq, nk, hd),
             DMA((slots,)), DMA((2, blocks // 4)), DMA((slots,)),
         ],
         compiler_params=pltpu.CompilerParams(vmem_limit_bytes=VMEM_LIMIT),
@@ -476,10 +542,10 @@
          obuf, y_ref, att, c_ref, acc, act, wo, wg, wu, wd, isem, osem, gsem, usem, dsem,
          ybuf, ysend, yrecv, osend, orecv) = refs
     else:
-        (o_ref, x_ref, ln_ref, qk_ref, cos_ref, sin_ref, wo_ref, wg_ref, wu_ref, wd_ref, wk_ref, wv_ref, wq_ref,
+        (o_ref, x_ref, ln_ref, qk_ref, trig_ref, wo_ref, wg_ref, wu_ref, wd_ref, wk_ref, wv_ref, wq_ref,
          h_ref, q_ref, k_all, v_all,
          obuf, y_ref, att, c_ref, acc, act, wo, wg, wu, wd, isem, osem, gsem, usem, dsem,
-         wn, nsem, qst, kst, vst, hsem, qsem, ksend, krecv, fsem) = refs
+         wn, nsem, qst, kst, vst, tbuf, hsem, qsem, ksend, krecv, fsem) = refs
         keys = KeyValues(k_all, v_all, ksend, krecv, fsem)
         hd = qk_ref.shape[-1]
         nk, nq = wk_ref.shape[-1] // hd, wq_ref.shape[-1] // hd
@@ -520,7 +586,7 @@
         return pl.ds(pl.multiple_of(s * rows, rows), rows)
 
     def own_rows(m):
-        return pl.ds(m * rows, rows)
+        return pl.ds(m * rows if isinstance(m, int) else pl.multiple_of(m * rows, rows), rows)
 
     def y_at(ch, m):
         return y_ref.at[slot_rows(slot_of(ch, m))]
@@ -540,14 +606,15 @@
         o_ring.free(t)
 
     in_x.wait()
-    for ch in range(2):
-        for m in range(3):
-            r = slot_rows(slot_of(ch, m))
-            y = y_ref[r, :].astype(F32) + norm_rows(att[r, :].astype(F32), gain(1))
-            y = y.astype(BF16)
-            y_ref[r, :] = y
-            if ch == 0 or not last:
-                c_ref[ch, own_rows(m), :] = c_of(y)
+
+    @pl.loop(0, 6)
+    def _(j):
+        ch, m = j // 3, lax.rem(j, 3)
+        r = slot_rows(slot_of(ch, m))
+        y = y_ref[r, :].astype(F32) + norm_rows(att[r, :].astype(F32), gain(1))
+        y = y.astype(BF16)
+        y_ref[r, :] = y
+        c_ref[ch, own_rows(m), :] = c_of(y)
 
     def up(ch, g_tile, u_tile):
         gate = jnp.dot(c_ref[ch], g_tile[...], preferred_element_type=F32)
@@ -560,7 +627,7 @@
         acc[...] = jnp.zeros(acc.shape, F32)
         g_ring.free(base)
         u_ring.free(base)
-        after_first()
+        after_first(ch)
 
         @pl.loop(1, n_f)
         def _(t):
@@ -617,28 +684,42 @@
                 def _():
                     near().start()
 
-        mlp(0, send_streams)
-        for m in range(3):
-            y_at(0, m)[...] = result(m, y_at(0, m)[...])
-        for m in range(3):
-            b, dev = owned(1, m)
-
-            @pl.when(dev != me)
+        def after_first(ch):
+            pl.when(ch == 0)(send_streams)
+            pl.when(ch == 1)(send_results)
+
+        @pl.loop(0, 2)
+        def _(ch):
+            mlp(ch, after_first)
+
+            @pl.when(ch == 0)
             def _():
-                remote(ybuf.at[m], ybuf.at[m], ysend.at[m], yrecv.at[m], me).wait_recv()
-
-        for m in range(3):
-            b, blk = place_of(1, m)
-
-            @pl.when(blk == me)
-            def _():
-                ybuf[b // 2] = y_at(1, m)[...]
-
-        for m in range(3):
-            c_ref[1, own_rows(m), :] = c_of(ybuf[m])
-        mlp(1, send_results)
-        for m in range(3):
+                @pl.loop(0, 3)
+                def _(m):
+                    y_at(0, m)[...] = result(m, y_at(0, m)[...])
+
+                for m in range(3):
+                    _, dev = owned(1, m)
+
+                    @pl.when(dev != me)
+                    def _():
+                        remote(ybuf.at[m], ybuf.at[m], ysend.at[m], yrecv.at[m], me).wait_recv()
+
+                for m in range(3):
+                    b, blk = place_of(1, m)
+
+                    @pl.when(blk == me)
+                    def _():
+                        ybuf[b // 2] = y_at(1, m)[...]
+
+                @pl.loop(0, 3)
+                def _(m):
+                    c_ref[1, own_rows(m), :] = c_of(ybuf[m])
+
+        @pl.loop(0, 3)
+        def _(m):
             ybuf[m] = result(m, ybuf[m])
+
         for m in range(3):
             b, _ = owned(1, m)
             local(ybuf.at[m], out_ref.at[b], orecv.at[b]).start()
@@ -668,16 +749,23 @@
     n_ring.begin()
     k_gain, q_gain = (qk_ref[layer + 1, j : j + 1, :].astype(F32) for j in (1, 0))
 
+    trig = Trig(trig_ref, layer + 1, rows)
+
+    @pl.loop(0, 6)
+    def _(j):
+        ch, m = j // 3, lax.rem(j, 3)
+        tbuf[ch, m, 0], tbuf[ch, m, 1] = trig.of(place_of(ch, m)[1])
+
     def turn(ch, m):
-        r = slot_rows(slot_of(ch, m))
-        return cos_ref[r, :], sin_ref[r, :]
+        return tbuf[ch, m, 0], tbuf[ch, m, 1]
 
     def send_keys(ch):
         for m in range(3):
             keys.start(slot_of(ch, m), (kst.at[ch, m], vst.at[ch, m]))
 
     def keys_and_values(ch):
-        for m in range(3):
+        @pl.loop(0, 3)
+        def _(m):
             h = result(m, y_at(ch, m)[...])
             y_at(ch, m)[...] = h
             c_ref[ch, own_rows(m), :] = norm_rows(h.astype(F32), gain(0, layer + 1)).astype(BF16)
@@ -709,17 +797,18 @@
             raw = jnp.dot(c_ref[ch], tile[...], preferred_element_type=F32)
             for m in range(3):
                 out = norm_turn(raw[m * rows : (m + 1) * rows], q_gain, *turn(ch, m))
-                qst[ch, m, h] = out * BF16(hd**-0.5)
+                qst[ch, m, :, cols(h, hd)] = out * BF16(hd**-0.5)
         n_ring.free(t)
 
     def first_keys():
         wait_group(n_dev)
         send_keys(0)
 
-    mlp(0, lambda: None)
-    keys_and_values(0)
-    mlp(1, first_keys)
-    keys_and_values(1)
+    @pl.loop(0, 2)
+    def _(ch):
+        mlp(ch, lambda ch: pl.when(ch == 1)(first_keys))
+        keys_and_values(ch)
+
     query(0)
     send_keys(1)
     pl.loop(1, nq)(query)
@@ -733,7 +822,8 @@
             keys.wait_sent(s, (kst.at[ch, m], vst.at[ch, m]))
             local(qst.at[ch, m], q_ref.at[s], qsem.at[s]).wait()
             local(y_at(ch, m), h_ref.at[s], hsem.at[s]).wait()
-    keys.wait_all(6)
+    keys.wait_mate(6)
+    keys.wait_special()
 
 
 def after_attention(layer, last, n_dev, cid, o, x, ln_w, w_o, w_gate, w_up, w_down, more=()):
@@ -764,48 +854,46 @@
             scratch_shapes=work + [pltpu.VMEM((3, rows, dim), BF16), DMA((3,)), DMA((3,)), DMA((3,)), DMA((slots,))],
             compiler_params=params,
         )(o2, x2, ln_w, w_o, w_gate, w_up, w_down)
-    qk_w, cos, sin, w_q, w_k, w_v = more
+    qk_w, trig, w_q, w_k, w_v = more
     hd = qk_w.shape[-1]
     nq, nk = w_q.shape[-1] // hd, w_k.shape[-1] // hd
-    q_shape, kv_shape = (slots, nq, rows, hd), (blocks, rows, nk * hd)
+    q_shape, kv_shape = (slots, rows, nq * hd), (blocks, rows, nk * hd)
     return pl.pallas_call(
         body,
-        in_specs=[ANY, ANY, WHOLE, WHOLE, WHOLE, WHOLE] + [ANY] * 7,
+        in_specs=[ANY, ANY, WHOLE, WHOLE, WHOLE] + [ANY] * 7,
         out_specs=[ANY] * 4,
         out_shape=[jax.ShapeDtypeStruct(a, BF16) for a in (x.shape, q_shape, kv_shape, kv_shape)],
         scratch_shapes=work + [
             pltpu.VMEM((deep, dim, hd), BF16), DMA((deep,)),
-            pltpu.VMEM((2, 3, nq, rows, hd), BF16), pltpu.VMEM((2, 3, rows, nk * hd), BF16), pltpu.VMEM((2, 3, rows, nk * hd), BF16),
+            pltpu.VMEM((2, 3, rows, nq * hd), BF16), pltpu.VMEM((2, 3, rows, nk * hd), BF16), pltpu.VMEM((2, 3, rows, nk * hd), BF16),
+            pltpu.VMEM((2, 3, 2, rows, hd // 2), F32),
             DMA((slots,)), DMA((slots,)), DMA((2, 3, slots)), DMA((2, blocks)), DMA((2, 2)),
         ],
         compiler_params=params,
-    )(o2, x2, ln_w, qk_w, cos, sin, w_o, w_gate, w_up, w_down, w_k, w_v, w_q)
-
-
-def rope_tables(pos, hd):
+    )(o2, x2, ln_w, qk_w, trig, w_o, w_gate, w_up, w_down, w_k, w_v, w_q)
+
+
+def rope_table(rows, blocks, hd):
     half = hd // 2
+    pos = jnp.concatenate([jnp.arange(rows), rows * jnp.arange(blocks)]).astype(F32)
     out = []
     for base, scale in ((LOCAL_BASE, 1.0), (GLOBAL_BASE, GLOBAL_SCALE)):
-        freq = base ** (-2.0 * jnp.arange(half, dtype=jnp.float32) / hd)
-        ang = (pos.astype(jnp.float32) / scale)[:, None] * freq[None, :]
-        out += [jnp.cos(ang), jnp.sin(ang)]
-    return out
+        freq = base ** (-2.0 * jnp.arange(half, dtype=F32) / hd)
+        ang = (pos / scale)[:, None] * freq[None, :]
+        out.append(jnp.stack([jnp.cos(ang), jnp.sin(ang)]))
+    return jnp.stack(out)
 
 
 def solution(mesh):
     n_dev = mesh.shape["cp"]
 
     def device_fn(x_loc, ln_w, qk_w, w_q, w_k, w_v, w_o, w_gate, w_up, w_down):
-        slots, rows, dim = x_loc.shape
-        _, _, core, special, row = placement()
-        blk = jnp.stack([slot_place(s, core, special, row)[1] for s in range(slots)])
-        pos = (blk[:, None] * rows + jnp.arange(rows)[None, :]).reshape(-1)
-        cos0, sin0, cos1, sin1 = rope_tables(pos, qk_w.shape[-1])
-        x, q, k, v = first(n_dev, x_loc, ln_w, qk_w, cos0, sin0, w_q, w_k, w_v)
-        o = attention(WINDOW, q, k, v)
+        rows, hd = x_loc.shape[1], qk_w.shape[-1]
+        trig = rope_table(rows, n_dev, hd)
+        x, o = first(n_dev, WINDOW, x_loc, ln_w, qk_w, trig, w_q, w_k, w_v)
         mlp = (w_o, w_gate, w_up, w_down)
-        x, q, k, v = after_attention(0, False, n_dev, 1, o, x, ln_w, *mlp, more=(qk_w, cos1, sin1, w_q, w_k, w_v))
-        o = attention(None, q, k, v)
+        x, q, k, v = after_attention(0, False, n_dev, 1, o, x, ln_w, *mlp, more=(qk_w, trig, w_q, w_k, w_v))
+        o = attention(None, hd, q, k, v)
         return after_attention(1, True, n_dev, 2, o, x, ln_w, *mlp)
 
     act_part = P("dp", "cp", None)

time: 486 us -> 471 us (0.969); the launches traced: 479 us -> 471 us
  Pallas kernels: 470 us -> 465 us
    pallas_call x2 -> x1, Pallas kernels: 51.8 us -> 26.8 us  [attention(): pl.pallas_call(functools.partial(attn_kernel, None if window is None else...]
    pallas_call x2, Pallas kernels: 287 us -> 307 us  [the longest x1 159 us: after_attention(): pl.pallas_call(body, in_specs=[ANY, ANY, WHOLE, WHOLE, WHOLE] + [ANY] * 7...]
    sin x2 -> x0, other arithmetic: 4.94 us -> none  [rope_tables(): out += [jnp.cos(ang), jnp.sin(ang)]]
where the time goes in v7:
time: 471 us
  Pallas kernels  465 us (99%)
    pallas_call x1, Pallas kernels, after_attention(): pl.pallas_call(body, in_specs=[ANY, ANY, WHOLE, WHOLE, WHOLE] + [ANY] * 7...  159 us
    pallas_call x1, Pallas kernels, first(): pl.pallas_call(functools.partial(first_kernel, n_dev, window // rows), ou...  147 us
    pallas_call x1, Pallas kernels, after_attention(): pl.pallas_call(body, in_specs=[ANY, ANY, WHOLE] + [ANY] * 4, out_specs=AN...  132 us
    pallas_call x1, Pallas kernels, attention(): pl.pallas_call(functools.partial(attn_kernel, None if window is None else...  26.8 us

profile of v7, /device:TPU:183, one launch (start us, length us, event | category | flops | bytes accessed | tf_op | source)
XLA Modules:
  0.0 470.8 jit_solution(80403729187627520)
XLA Ops:
  0.1 0.3 multiply_cosine_fusion.1
  0.4 0.3 multiply_cosine_fusion
  0.8 0.7 pad_maximum_fusion.trig_ref.refs_4_
  1.5 147.4 %shard_map.100 = (bf16[6,128,2304]{2,1,0:T(8,128)(2,1)}, bf16[6,128,2048]{2,1,0:T(8,128)(2,1)}) custom-call(bf16[6,128,2304]{2,1,0:T(8,128)(2,1)} %x_ref.1, bf16[2,4,2304]{2,1,0:T(4,128)(2,1)} %refs_2_.3, bf16[2,2,256]{2,1,0:T(2,128)(2,1)} %refs_3_.2, f32[2,2,144,128]{3,2,1,0:T(8,128)} %pad_maximum_fusion.trig_ref.refs_4_, bf16[2,2304,2048]{2,1,0:T(8,128)(2,1)} %refs_11_.1, ...), custom_call_target="tpu_custom_call" | custom-call | tf_op jit(solution)/shard_map/pallas_call | solution.py:431
  148.9 159.4 %shard_map.101 = (bf16[6,128,2304]{2,1,0:T(8,128)(2,1)}, bf16[6,128,2048]{2,1,0:T(8,128)(2,1)}, bf16[16,128,1024]{2,1,0:T(8,128)(2,1)}, bf16[16,128,1024]{2,1,0:T(8,128)(2,1)}) custom-call(bf16[768,2048]{1,0:T(8,128)(2,1)} %bitcast.11, bf16[768,2304]{1,0:T(8,128)(2,1)} %bitcast.10, bf16[2,4,2304]{2,1,0:T(4,128)(2,1)} %refs_2_.3, bf16[2,2,256]{2,1,0:T(2,128)(2,1)} %refs_3_.2, ...), custom_call_target="tpu_custom_call" | custom-call | tf_op jit(solution)/shard_map/pallas_call | solution.py:861
  308.3 26.8 %shard_map.102 = bf16[6,128,2048]{2,1,0:T(8,128)(2,1)} custom-call(bf16[6,128,2048]{2,1,0:T(8,128)(2,1)} %get-tuple-element.13.q_ref, bf16[16,128,1024]{2,1,0:T(8,128)(2,1)} %get-tuple-element.14.k_ref, bf16[16,128,1024]{2,1,0:T(8,128)(2,1)} %get-tuple-element.15.v_ref), custom_call_target="tpu_custom_call" | custom-call | tf_op jit(solution)/shard_map/pallas_call | solution.py:483
  335.1 131.7 %shard_map.103 = bf16[6,128,2304]{2,1,0:T(8,128)(2,1)} custom-call(bf16[768,2048]{1,0:T(8,128)(2,1)} %bitcast.8, bf16[768,2304]{1,0:T(8,128)(2,1)} %bitcast.9, bf16[2,4,2304]{2,1,0:T(4,128)(2,1)} %refs_2_.3, bf16[2,2048,2304]{2,1,0:T(8,128)(2,1)} %refs_3_.3, bf16[2,2304,9216]{2,1,0:T(8,128)(2,1)} %refs_4_.1, bf16[2,2304,9216]{2,1,0:T(8,128)(2,1)} %refs_5_.3, ...), custom_call_target="tpu_custom_call" | custom-call | tf_op jit(solution)/shard_map/pallas_call | solution.py:849
  466.8 4.0 copy.12
  (7 shorter events, 0.1 us)

commit v8 on v7

--- a/solution.py
+++ b/solution.py
@@ -51,13 +51,20 @@
     return b, blk
 
 
-def ring(a, b):
-    return min((a - b) % 8, (b - a) % 8)
-
-
-ARRIVAL = [sorted(range(6), key=lambda s: (ring(2 + s, c), s)) for c in range(8)]
-for c in SPECIAL:
-    ARRIVAL[c] = [4, 5, 0, 2, 1, 3]
+EARLY_ORDER = (2, 5, 1, 4, 0, 3)
+
+
+def arrival():
+    out = []
+    for dev in range(16):
+        chip, core = dev // 2, dev % 2
+        if chip in SPECIAL:
+            out += [4, 5, 2, 3, 0, 1]
+            continue
+        b = ROW_CHIP.index(chip)
+        for step in range(6):
+            out += [(j - 4) // 2 for j in range(4, 16) if (j + step) % 6 == b and (j + 1) // 2 % 2 == core]
+    return out
 
 
 def home_of(b, blk):
@@ -208,6 +215,7 @@
         self.nk = kbuf.shape[-1] // hd
         self.rep = qbuf.shape[-1] // kbuf.shape[-1]
         self.tile = self.per * self.rows
+        self.group = wacc.shape[1] // (self.rep * self.rows)
 
     def fill_bias(self):
         rows, tile, bias = self.rows, self.tile, self.bias
@@ -228,19 +236,25 @@
         block = buf.at[pl.ds(base + self.per * t, self.per)]
         return block[:, :, g * self.hd : (g + 1) * self.hd].reshape(self.tile, self.hd)
 
-    def scores(self, s, t, base, blk):
-        rows, rep, hd, per = self.rows, self.rep, self.hd, self.per
-        edge = jnp.where(t == blk // per, 1 + blk % per, 0)
+    def edge(self, t, blk):
+        per = self.per
+        out = jnp.where(t == blk // per, 1 + blk % per, 0)
         if self.window_blocks is not None:
             old = blk - self.window_blocks
-            edge = jnp.where((old >= 0) & (t == old // per), 1 + per + old % per, edge)
-        off = self.bias[edge][None]
+            out = jnp.where((old >= 0) & (t == old // per), 1 + per + old % per, out)
+        return out
+
+    def scores(self, s, t, base, blks):
+        rows, rep, hd, group = self.rows, self.rep, self.hd, self.group
+        offs = [self.bias[self.edge(t, blk)][None] for blk in blks]
         out = []
         for g in range(self.nk):
-            heads = [self.qbuf[s, :, h * hd : (h + 1) * hd] for h in range(g * rep, (g + 1) * rep)]
-            q2 = jnp.concatenate(heads, axis=0)
-            sc = lax.dot_general(q2, self.part(self.kbuf, t, base, g), (((1,), (1,)), ((), ())), preferred_element_type=F32)
-            out.append((sc.reshape(rep, rows, self.tile) + off).reshape(rep * rows, self.tile))
+            heads = [self.qbuf[s + j, :, h * hd : (h + 1) * hd] for j in range(group) for h in range(g * rep, (g + 1) * rep)]
+            q = jnp.concatenate(heads, axis=0)
+            sc = lax.dot_general(q, self.part(self.kbuf, t, base, g), (((1,), (1,)), ((), ())), preferred_element_type=F32)
+            sc = sc.reshape(group, rep, rows, self.tile)
+            sc = jnp.concatenate([sc[j] + offs[j] for j in range(group)], axis=0)
+            out.append(sc.reshape(group * rep * rows, self.tile))
         return out
 
     def columns(self, val, op):
@@ -252,7 +266,7 @@
     def row_max(self, val):
         return jnp.broadcast_to(jnp.max(val, axis=-1, keepdims=True), val.shape)
 
-    def passes(self, s, blk, base, first, last):
+    def passes(self, s, blks, base, first, last):
         for g in range(self.nk):
             self.wm[g] = jnp.full(self.wm.shape[1:], NEG, F32)
             self.wl[g] = jnp.zeros(self.wl.shape[1:], F32)
@@ -260,7 +274,7 @@
 
         @pl.loop(first, last)
         def _(t):
-            for g, sc in enumerate(self.scores(s, t, base, blk)):
+            for g, sc in enumerate(self.scores(s, t, base, blks)):
                 self.sbuf[g, t - first] = sc
                 self.wm[g] = jnp.maximum(self.wm[g], self.columns(sc, jnp.maximum))
 
@@ -275,7 +289,7 @@
                 self.wacc[g] += jnp.dot(p.astype(BF16), self.part(self.vbuf, t, base, g), preferred_element_type=F32)
 
     def merge(self, s, blk, old, old_sum, old_acc):
-        for g, sc in enumerate(self.scores(s, 0, 0, blk)):
+        for g, sc in enumerate(self.scores(s, 0, 0, [blk])):
             new = self.row_max(jnp.maximum(old[g], self.columns(sc, jnp.maximum)))
             p = jnp.exp(sc - self.spread(new))
             alpha = jnp.exp(old[g] - new)
@@ -286,10 +300,12 @@
     def finish(self, s):
         for g in range(self.nk):
             out = (self.wacc[g] / jnp.sum(self.wl[g], axis=-1, keepdims=True)).astype(BF16)
-            for h in range(self.rep):
-                lo = (g * self.rep + h) * self.hd
-                self.qbuf[s, :, lo : lo + self.hd] = out[h * self.rows : (h + 1) * self.rows]
-        local(self.qbuf.at[s], self.o_ref.at[s], self.osem.at[s]).start()
+            for j in range(self.group):
+                for h in range(self.rep):
+                    lo, r = (g * self.rep + h) * self.hd, (j * self.rep + h) * self.rows
+                    self.qbuf[s + j, :, lo : lo + self.hd] = out[r : r + self.rows]
+        for j in range(self.group):
+            local(self.qbuf.at[s + j], self.o_ref.at[s + j], self.osem.at[s + j]).start()
 
     def wait_out(self):
         for s in range(self.slots):
@@ -317,8 +333,9 @@
     for j, (src, dst) in enumerate(((wk_ref, wk), (wv_ref, wv), (wq_ref, wq))):
         start_parts(src.at[0], dst, wsem.at[j])
     wait_group(n_dev)
-    for b in SEND_ORDER:
-        dev, slot = homes[b]
+    for step in range(n):
+        b = jnp.where(me < 4, EARLY_ORDER[step], lax.rem(me + step, n))
+        dev, slot = home_of(b, me)
 
         @pl.when(dev != me)
         def _():
@@ -331,7 +348,7 @@
     q_gain = qk_ref[0, 0:1, :].astype(F32)
     for j, (src, dst) in enumerate(((wk_ref, wk), (wv_ref, wv), (wq_ref, wq))):
         local(src.at[0], dst, wsem.at[j]).wait()
-    order = [s for c in range(8) for s in ARRIVAL[c]]
+    order = arrival()
 
     def col(h):
         return pl.ds(h * hd if isinstance(h, int) else pl.multiple_of(h * hd, hd), hd)
@@ -341,7 +358,7 @@
 
     @pl.loop(0, n // 2)
     def _(pair):
-        places = [pick(chip * n + 2 * pair + j, order) for j in range(2)]
+        places = [pick(me * n + 2 * pair + j, order) for j in range(2)]
         turn, idx = [], []
         for j, s in enumerate(places):
             local(xbuf.at[s], xbuf.at[s], xrecv.at[s]).wait()
@@ -375,7 +392,7 @@
     def _(s):
         _, blk = slot_place(s, core, special, row)
         base = jnp.where(special == 1, (s // 2) * att.per, 0)
-        att.passes(s, blk, base, jnp.where(special == 1, 0, jnp.maximum(att.start_tile(blk), 1)), blk // att.per + 1)
+        att.passes(s, [blk], base, jnp.where(special == 1, 0, jnp.maximum(att.start_tile(blk), 1)), blk // att.per + 1)
         more = (special == 0) & (s < mx.shape[0])
 
         @pl.when(more)
@@ -410,11 +427,8 @@
             remote(x_ref.at[b], xbuf.at[slot], xsend.at[b], xrecv.at[slot], dev).wait_send()
 
 
-SEND_ORDER = (2, 5, 0, 3, 1, 4)
-
-
-def attention_scratch(tiles, slots, rows, nq, nk, hd):
-    wide = nq // nk * rows
+def attention_scratch(tiles, group, rows, nq, nk, hd):
+    wide = group * nq // nk * rows
     return [
         pltpu.VMEM((nk, tiles, wide, 4 * rows), F32),
         pltpu.VMEM((nk, wide, hd), F32), pltpu.VMEM((nk, wide, 128), F32), pltpu.VMEM((nk, wide, 128), F32),
@@ -437,7 +451,7 @@
             pltpu.VMEM(x.shape, BF16), pltpu.VMEM((2 * rows, dim), BF16),
             pltpu.VMEM(w_q.shape[1:], BF16), pltpu.VMEM(w_k.shape[1:], BF16), pltpu.VMEM(w_v.shape[1:], BF16),
             pltpu.VMEM(q_shape, BF16), pltpu.VMEM(kv_shape, BF16), pltpu.VMEM(kv_shape, BF16),
-            *attention_scratch(3, n, rows, nq, nk, hd),
+            *attention_scratch(3, 1, rows, nq, nk, hd),
             pltpu.VMEM((late, nk, wide, 128), F32), pltpu.VMEM((late, nk, wide, 128), F32), pltpu.VMEM((late, nk, wide, hd), F32),
             DMA((3,)), DMA((n,)), DMA((n,)), DMA((n,)), DMA((n,)), DMA((2, 3, n)), DMA((2, blocks)), DMA((2, 2)),
         ],
@@ -461,16 +475,23 @@
         for c in loads(t):
             c.start()
     att.fill_bias()
-    for t in range(tiles):
-        for c in loads(t):
-            c.wait()
-
-    @pl.loop(0, att.slots)
-    def _(s):
-        _, blk = slot_place(s, core, special, row)
-        local(q_ref.at[s], qbuf.at[s], qsem.at[s]).wait()
-        base = jnp.where(special == 1, (s // 2) * per, 0)
-        att.passes(s, blk, base, att.start_tile(blk), blk // per + 1)
+    group = att.group
+
+    @pl.loop(0, att.slots // group)
+    def _(i):
+        for t in range(tiles):
+
+            @pl.when(i == max(t - 1, 0))
+            def _():
+                for c in loads(t):
+                    c.wait()
+
+        s = i * group
+        blks = [slot_place(s + j, core, special, row)[1] for j in range(group)]
+        for j in range(group):
+            local(q_ref.at[s + j], qbuf.at[s + j], qsem.at[s + j]).wait()
+        base = jnp.where(special == 1, i * per, 0)
+        att.passes(s, blks, base, att.start_tile(blks[0]), blks[0] // per + 1)
         att.finish(s)
 
     att.wait_out()
@@ -487,7 +508,7 @@
         out_specs=ANY,
         scratch_shapes=[
             pltpu.VMEM(k.shape, BF16), pltpu.VMEM(v.shape, BF16), pltpu.VMEM(q.shape, BF16),
-            *attention_scratch(blocks // 4, slots, rows, nq, nk, hd),
+            *attention_scratch(blocks // 4, 2, rows, nq, nk, hd),
             DMA((slots,)), DMA((2, blocks // 4)), DMA((slots,)),
         ],
         compiler_params=pltpu.CompilerParams(vmem_limit_bytes=VMEM_LIMIT),

time: 471 us -> 463 us (0.983)
  the two profiles are of different devices: /device:TPU:183 before, /device:TPU:181 now
where the time goes in v8:
time: 463 us
  Pallas kernels  457 us (99%)
    pallas_call x1, Pallas kernels, after_attention(): pl.pallas_call(body, in_specs=[ANY, ANY, WHOLE, WHOLE, WHOLE] + [ANY] * 7...  159 us
    pallas_call x1, Pallas kernels, first(): pl.pallas_call(functools.partial(first_kernel, n_dev, window // rows), ou...  145 us
    pallas_call x1, Pallas kernels, after_attention(): pl.pallas_call(body, in_specs=[ANY, ANY, WHOLE] + [ANY] * 4, out_specs=AN...  132 us
    pallas_call x1, Pallas kernels, attention(): pl.pallas_call(functools.partial(attn_kernel, None if window is None else...  21.3 us

profile of v8, /device:TPU:181, one launch (start us, length us, event | category | flops | bytes accessed | tf_op | source)
XLA Modules:
  0.0 462.5 jit_solution(12243254329748780102)
XLA Ops:
  0.1 0.3 multiply_cosine_fusion.1
  0.4 0.3 multiply_cosine_fusion
  0.8 0.7 pad_maximum_fusion.trig_ref.refs_4_
  1.5 144.6 %shard_map.100 = (bf16[6,128,2304]{2,1,0:T(8,128)(2,1)}, bf16[6,128,2048]{2,1,0:T(8,128)(2,1)}) custom-call(bf16[6,128,2304]{2,1,0:T(8,128)(2,1)} %x_ref.1, bf16[2,4,2304]{2,1,0:T(4,128)(2,1)} %refs_2_.3, bf16[2,2,256]{2,1,0:T(2,128)(2,1)} %refs_3_.2, f32[2,2,144,128]{3,2,1,0:T(8,128)} %pad_maximum_fusion.trig_ref.refs_4_, bf16[2,2304,2048]{2,1,0:T(8,128)(2,1)} %refs_11_.1, ...), custom_call_target="tpu_custom_call" | custom-call | tf_op jit(solution)/shard_map/pallas_call | solution.py:445
  146.1 159.4 %shard_map.101 = (bf16[6,128,2304]{2,1,0:T(8,128)(2,1)}, bf16[6,128,2048]{2,1,0:T(8,128)(2,1)}, bf16[16,128,1024]{2,1,0:T(8,128)(2,1)}, bf16[16,128,1024]{2,1,0:T(8,128)(2,1)}) custom-call(bf16[768,2048]{1,0:T(8,128)(2,1)} %bitcast.11, bf16[768,2304]{1,0:T(8,128)(2,1)} %bitcast.10, bf16[2,4,2304]{2,1,0:T(4,128)(2,1)} %refs_2_.3, bf16[2,2,256]{2,1,0:T(2,128)(2,1)} %refs_3_.2, ...), custom_call_target="tpu_custom_call" | custom-call | tf_op jit(solution)/shard_map/pallas_call | solution.py:882
  305.5 21.3 %shard_map.102 = bf16[6,128,2048]{2,1,0:T(8,128)(2,1)} custom-call(bf16[6,128,2048]{2,1,0:T(8,128)(2,1)} %get-tuple-element.13.q_ref, bf16[16,128,1024]{2,1,0:T(8,128)(2,1)} %get-tuple-element.14.k_ref, bf16[16,128,1024]{2,1,0:T(8,128)(2,1)} %get-tuple-element.15.v_ref), custom_call_target="tpu_custom_call" | custom-call | tf_op jit(solution)/shard_map/pallas_call | solution.py:504
  326.8 131.7 %shard_map.103 = bf16[6,128,2304]{2,1,0:T(8,128)(2,1)} custom-call(bf16[768,2048]{1,0:T(8,128)(2,1)} %bitcast.8, bf16[768,2304]{1,0:T(8,128)(2,1)} %bitcast.9, bf16[2,4,2304]{2,1,0:T(4,128)(2,1)} %refs_2_.3, bf16[2,2048,2304]{2,1,0:T(8,128)(2,1)} %refs_3_.3, bf16[2,2304,9216]{2,1,0:T(8,128)(2,1)} %refs_4_.1, bf16[2,2304,9216]{2,1,0:T(8,128)(2,1)} %refs_5_.3, ...), custom_call_target="tpu_custom_call" | custom-call | tf_op jit(solution)/shard_map/pallas_call | solution.py:870
  458.5 4.0 copy.12
  (7 shorter events, 0.1 us)

commit v9 on v8

--- a/solution.py
+++ b/solution.py
@@ -148,17 +148,25 @@
             ))
         return out
 
-    def start(self, s, stage):
+    def start(self, s, stage, rows_too=True):
         self.here()
         for own, mate, row in self._copies(s, stage):
 
-            @pl.when(self.special == 1)
+            @pl.when((self.special == 1) & rows_too)
             def _():
                 row.start()
 
             mate.start()
             if own is not None:
                 own.start()
+
+    def start_rows(self, s):
+        self.here()
+
+        @pl.when(self.special == 1)
+        def _():
+            for _, _, row in self._copies(s, None):
+                row.start()
 
     def wait_sent(self, s, stage):
         self.here()
@@ -383,9 +391,11 @@
 
         query(0)
         for s in places:
-            keys.start(s, None)
+            keys.start(s, None, pair == 0)
         pl.loop(1, nq)(query)
 
+    for s in (2, 0, 3, 1):
+        keys.start_rows(s)
     keys.wait_mate(n)
 
     @pl.loop(0, n)
@@ -757,10 +767,10 @@
         return
 
     def source(t, put):
-        kind = lax.rem(t, 2 * nk) if not isinstance(t, int) else t % (2 * nk)
+        head = lax.rem(t // 2, nk)
         cases = (
-            (jnp.logical_and(t < 4 * nk, kind < nk), lambda: put(wk_ref.at[layer + 1, :, cols(kind, hd)])),
-            (jnp.logical_and(t < 4 * nk, kind >= nk), lambda: put(wv_ref.at[layer + 1, :, cols(kind - nk, hd)])),
+            ((t < 4 * nk) & (t % 2 == 0), lambda: put(wk_ref.at[layer + 1, :, cols(head, hd)])),
+            ((t < 4 * nk) & (t % 2 == 1), lambda: put(wv_ref.at[layer + 1, :, cols(head, hd)])),
             (t >= 4 * nk, lambda: put(wq_ref.at[layer + 1, :, cols(t - 4 * nk, hd)])),
         )
         for cond, do in cases:
@@ -793,19 +803,16 @@
 
         @pl.loop(0, nk)
         def _(h):
-            t = ch * 2 * nk + h
-            raw = jnp.dot(c_ref[ch], n_ring.get(t)[...], preferred_element_type=F32)
+            t = 2 * (ch * nk + h)
+            k_tile, v_tile = n_ring.get(t), n_ring.get(t + 1)
+            k_raw = jnp.dot(c_ref[ch], k_tile[...], preferred_element_type=F32)
+            v_raw = jnp.dot(c_ref[ch], v_tile[...], preferred_element_type=F32)
+            for m in range(3):
+                part = slice(m * rows, (m + 1) * rows)
+                kst[ch, m, :, cols(h, hd)] = norm_turn(k_raw[part], k_gain, *turn(ch, m))
+                vst[ch, m, :, cols(h, hd)] = v_raw[part].astype(BF16)
             n_ring.free(t)
-            for m in range(3):
-                kst[ch, m, :, cols(h, hd)] = norm_turn(raw[m * rows : (m + 1) * rows], k_gain, *turn(ch, m))
-
-        @pl.loop(0, nk)
-        def _(h):
-            t = (ch * 2 + 1) * nk + h
-            raw = jnp.dot(c_ref[ch], n_ring.get(t)[...], preferred_element_type=F32)
-            n_ring.free(t)
-            for m in range(3):
-                vst[ch, m, :, cols(h, hd)] = raw[m * rows : (m + 1) * rows].astype(BF16)
+            n_ring.free(t + 1)
 
         for m in range(3):
             s = slot_of(ch, m)
@@ -853,7 +860,7 @@
     total = slots * rows
     half = total // 2
     blocks = 16
-    tn, tf = min(256, dim), min(512, ff)
+    tn, tf = min(256, dim), min(768 if last and ff % 768 == 0 else 512, ff)
     deep = 3
     o2, x2 = o.reshape(total, inner), x.reshape(total, dim)
     work = [
@@ -885,7 +892,7 @@
         out_specs=[ANY] * 4,
         out_shape=[jax.ShapeDtypeStruct(a, BF16) for a in (x.shape, q_shape, kv_shape, kv_shape)],
         scratch_shapes=work + [
-            pltpu.VMEM((deep, dim, hd), BF16), DMA((deep,)),
+            pltpu.VMEM((4, dim, hd), BF16), DMA((4,)),
             pltpu.VMEM((2, 3, rows, nq * hd), BF16), pltpu.VMEM((2, 3, rows, nk * hd), BF16), pltpu.VMEM((2, 3, rows, nk * hd), BF16),
             pltpu.VMEM((2, 3, 2, rows, hd // 2), F32),
             DMA((slots,)), DMA((slots,)), DMA((2, 3, slots)), DMA((2, blocks)), DMA((2, 2)),

time: 463 us -> 457 us (0.987)
  the two profiles are of different devices: /device:TPU:181 before, /device:TPU:55 now
where the time goes in v9:
time: 457 us
  Pallas kernels  451 us (99%)
    pallas_call x1, Pallas kernels, after_attention(): pl.pallas_call(body, in_specs=[ANY, ANY, WHOLE, WHOLE, WHOLE] + [ANY] * 7...  157 us
    pallas_call x1, Pallas kernels, after_attention(): pl.pallas_call(body, in_specs=[ANY, ANY, WHOLE] + [ANY] * 4, out_specs=AN...  141 us
    pallas_call x1, Pallas kernels, first(): pl.pallas_call(functools.partial(first_kernel, n_dev, window // rows), ou...  132 us
    pallas_call x1, Pallas kernels, attention(): pl.pallas_call(functools.partial(attn_kernel, None if window is None else...  21.3 us

profile of v9, /device:TPU:55, one launch (start us, length us, event | category | flops | bytes accessed | tf_op | source)
XLA Modules:
  0.0 456.5 jit_solution(8803073143752354593)
XLA Ops:
  0.1 0.3 multiply_cosine_fusion.1
  0.4 0.3 multiply_cosine_fusion
  0.8 0.7 pad_maximum_fusion.trig_ref.refs_4_
  1.5 132.0 %shard_map.100 = (bf16[6,128,2304]{2,1,0:T(8,128)(2,1)}, bf16[6,128,2048]{2,1,0:T(8,128)(2,1)}) custom-call(bf16[6,128,2304]{2,1,0:T(8,128)(2,1)} %x_ref.1, bf16[2,4,2304]{2,1,0:T(4,128)(2,1)} %refs_2_.3, bf16[2,2,256]{2,1,0:T(2,128)(2,1)} %refs_3_.2, f32[2,2,144,128]{3,2,1,0:T(8,128)} %pad_maximum_fusion.trig_ref.refs_4_, bf16[2,2304,2048]{2,1,0:T(8,128)(2,1)} %refs_11_.1, ...), custom_call_target="tpu_custom_call" | custom-call | tf_op jit(solution)/shard_map/pallas_call | solution.py:455
  133.5 156.9 %shard_map.101 = (bf16[6,128,2304]{2,1,0:T(8,128)(2,1)}, bf16[6,128,2048]{2,1,0:T(8,128)(2,1)}, bf16[16,128,1024]{2,1,0:T(8,128)(2,1)}, bf16[16,128,1024]{2,1,0:T(8,128)(2,1)}) custom-call(bf16[768,2048]{1,0:T(8,128)(2,1)} %bitcast.11, bf16[768,2304]{1,0:T(8,128)(2,1)} %bitcast.10, bf16[2,4,2304]{2,1,0:T(4,128)(2,1)} %refs_2_.3, bf16[2,2,256]{2,1,0:T(2,128)(2,1)} %refs_3_.2, ...), custom_call_target="tpu_custom_call" | custom-call | tf_op jit(solution)/shard_map/pallas_call | solution.py:889
  290.5 21.3 %shard_map.102 = bf16[6,128,2048]{2,1,0:T(8,128)(2,1)} custom-call(bf16[6,128,2048]{2,1,0:T(8,128)(2,1)} %get-tuple-element.13.q_ref, bf16[16,128,1024]{2,1,0:T(8,128)(2,1)} %get-tuple-element.14.k_ref, bf16[16,128,1024]{2,1,0:T(8,128)(2,1)} %get-tuple-element.15.v_ref), custom_call_target="tpu_custom_call" | custom-call | tf_op jit(solution)/shard_map/pallas_call | solution.py:514
  311.7 140.7 %shard_map.103 = bf16[6,128,2304]{2,1,0:T(8,128)(2,1)} custom-call(bf16[768,2048]{1,0:T(8,128)(2,1)} %bitcast.8, bf16[768,2304]{1,0:T(8,128)(2,1)} %bitcast.9, bf16[2,4,2304]{2,1,0:T(4,128)(2,1)} %refs_2_.3, bf16[2,2048,2304]{2,1,0:T(8,128)(2,1)} %refs_3_.3, bf16[2,2304,9216]{2,1,0:T(8,128)(2,1)} %refs_4_.1, bf16[2,2304,9216]{2,1,0:T(8,128)(2,1)} %refs_5_.3, ...), custom_call_target="tpu_custom_call" | custom-call | tf_op jit(solution)/shard_map/pallas_call | solution.py:877
  452.5 4.0 copy.12
  (7 shorter events, 0.1 us)
